TPU v7x, 256 devices: a whole 4x4x8 slice. The times are simulated.
256 devices in a mesh: cond: 2 (over z_hi), gx: 8 (over y, core), yz: 16 (over x, z_lo).
Axes of the slice: x: 4, y: 4, z: 8 (z_hi: 2, z_lo: 4; z = z_hi * 4 + z_lo), core: 2. Of those that a mesh axis runs over, the one named last changes fastest.
Arguments:
- adjoint: float32 [2, 5, 64, 256, 256], P('cond', None, 'gx', 'yz'), may hold values from -6 to 6
- objective_gradient: float32 [2, 5, 64, 256, 256], P('cond', None, 'gx', 'yz'), may hold values from -6 to 6
- diagonal: float32 [64, 256, 256], P('gx', 'yz'), may hold values from 4 to 12
- flux_blocks: float32 [2, 6, 5, 5], P('cond'), may hold values from -1 to 1
- flux_sensitivity: bfloat16 [2, 5, 64, 256, 256], P('cond', None, 'gx', 'yz'), may hold values from -6 to 6
- surface_mask: int32 [64, 256, 256], P('gx', 'yz'), may hold values 0 or 1
- patch_band_slot: int32 [64, 256], P('gx', 'yz'), may hold values from 0 to 62
- design_basis: float32 [256, 128], replicated, may hold values from -0.015625 to 0.015625
- condition_weights: int32 [2], replicated, may hold values from 1 to 999, as said below
Outputs:
- smoothed: float32 [2, 5, 64, 256, 256], P('cond', None, 'gx', 'yz')
- residual: float32 [2, 5, 64, 256, 256], P('cond', None, 'gx', 'yz')
- design_gradient: float32 [4096], P(('gx', 'yz'))
Inputs may be any that keep to these rules, and one draw needn't show every extreme that they name: `condition_weights`: positive integer weights; one condition has weight 999.
All inputs are finite; a program needn't handle non-finite values. No bound on the sum of `surface_mask` on one device may be relied on, other than what follows from the above.
Results may differ from a plain program's by a relative error of at most 0.0003.
Values sent between devices are 32-bit elements; how exact they have to be, the bound alone decides.
No kernel may reach another device: no remote copies, remote signals or barrier semaphores. Data moves between devices by JAX's collectives and lax.ppermute only.
A program may use at most 64 MiB of HBM per device.

v0:
```python
import functools

import jax
import jax.numpy as jnp
from jax import lax
from jax.sharding import Mesh
from jax.sharding import PartitionSpec as P

NDES = 4096
GX_YZ = ("gx_0", "gx_1", "yz_0", "yz_1")
GX = ("gx_0", "gx_1")
YZ = ("yz_0", "yz_1")
COND_GX_YZ = ("cond", "gx_0", "gx_1", "yz_0", "yz_1")


relaxation = 0.8
neighbour_starts = ((2, 1, 1), (0, 1, 1), (1, 2, 1), (1, 0, 1), (1, 1, 2), (1, 1, 0))


def padded(x, sides, width):
    edges = {}
    for axis, dim in sides:
        size, length = (lax.axis_size(axis), x.shape[dim])
        up = [(i, (i + 1) % size) for i in range(size - 1)]
        last = lax.slice_in_dim(x, length - width, length, axis=dim)
        initial = lax.slice_in_dim(x, 0, width, axis=dim)
        edges[dim] = (
            lax.ppermute(last, axis, up),
            lax.ppermute(initial, axis, [(b, a) for a, b in up]),
        )
    done = []
    for _, dim in sides:
        low, high = edges[dim]
        around = [(width, width) if d in done else (0, 0) for d in range(x.ndim)]
        x = jnp.concatenate([jnp.pad(low, around), x, jnp.pad(high, around)], axis=dim)
        done.append(dim)
    return x


def one_axis_at_a_time(x, axes):
    return functools.reduce(lax.psum, axes, x)


def apply_operator(padded_field, diagonal, blocks):
    size_x = padded_field.shape[1] - 2
    size_y = padded_field.shape[2] - 2
    size_z = padded_field.shape[3] - 2
    result = diagonal * padded_field[:, 1:-1, 1:-1, 1:-1]
    for direction in range(6):
        start_x, start_y, start_z = neighbour_starts[direction]
        shifted = padded_field[
            :, start_x : start_x + size_x, start_y : start_y + size_y, start_z : start_z + size_z
        ]
        result = result - jnp.einsum(
            "ec,exyz->cxyz", blocks[direction], shifted, precision=lax.Precision.HIGHEST
        )
    return result


def spread_bands(slot_lookup):
    halfway = slot_lookup.shape[1] // 2
    first_half = jnp.pad(slot_lookup[:, :halfway], ((0, 1), (0, 0)))
    second_half = jnp.pad(slot_lookup[:, halfway:], ((1, 0), (0, 0)))
    return (first_half + second_half).reshape(-1)


def pad_third(values):
    return jnp.pad(values, ((0, 0), (0, 0), (0, 0), (1, 1)))


def local(
    adjoint,
    objective_gradient,
    diagonal,
    flux_blocks,
    flux_sensitivity,
    surface_mask,
    patch_band_slot,
    design_basis,
    condition_weights,
):
    blocks = flux_blocks[0]
    source = objective_gradient[0]
    start_field = adjoint[0]

    def operate(values):
        haloed = padded(values, ((GX, 1), (YZ, 2)), 1)
        return apply_operator(pad_third(haloed), diagonal, blocks)

    relaxed = start_field + relaxation * (source - operate(start_field)) / diagonal
    smoothed = relaxed + relaxation * (source - operate(relaxed)) / diagonal
    residual = source - operate(smoothed)
    surface = surface_mask.astype(jnp.float32) * jnp.sum(
        smoothed * flux_sensitivity[0].astype(jnp.float32), axis=0
    )
    projected_gradient = jnp.dot(
        surface.reshape(-1, surface.shape[-1]),
        design_basis,
        precision=lax.Precision.HIGHEST,
        preferred_element_type=jnp.float32,
    )
    slot_count = 2 * NDES // design_basis.shape[1] - 1
    onehot = (jnp.arange(slot_count)[:, None] == patch_band_slot.reshape(1, -1)).astype(jnp.float32)
    slot_lookup = jnp.dot(
        onehot,
        projected_gradient,
        precision=lax.Precision.HIGHEST,
        preferred_element_type=jnp.float32,
    )
    gradient = spread_bands(slot_lookup)
    weights_float = condition_weights.astype(jnp.float32)
    picked = jnp.arange(weights_float.shape[0]) == lax.axis_index("cond")
    local_portion = jnp.sum(jnp.where(picked, weights_float, 0.0)) / jnp.sum(weights_float)
    summed = one_axis_at_a_time(local_portion * gradient, COND_GX_YZ)
    pieces = NDES // lax.axis_size(GX_YZ)
    design_gradient = lax.dynamic_slice_in_dim(summed, lax.axis_index(GX_YZ) * pieces, pieces, 0)
    return (smoothed[None], residual[None], design_gradient)


def solution(mesh):
    torus = Mesh(
        mesh.devices.reshape(mesh.shape["cond"], 4, 2, 4, 4),
        ("cond", "gx_0", "gx_1", "yz_0", "yz_1"),
    )
    in_specs = (
        P("cond", None, GX, YZ, None),
        P("cond", None, GX, YZ, None),
        P(GX, YZ, None),
        P("cond", None, None, None),
        P("cond", None, GX, YZ, None),
        P(GX, YZ, None),
        P(GX, YZ),
        P(),
        P(),
    )
    out_specs = (P("cond", None, GX, YZ, None), P("cond", None, GX, YZ, None), P(GX_YZ))
    return jax.shard_map(local, mesh=torus, in_specs=in_specs, out_specs=out_specs, check_vma=False)
```

profile of v0, /device:TPU:0, one launch (start us, length us, event | category | flops | bytes accessed | tf_op | source)
XLA Modules:
  0.0 146.4 jit_solution(6187131229460594439)
XLA Ops:
  0.7 1.5 %copy.88 = f32[1,5,8,16,256]{4,1,3,2,0:T(8,128)S(1)} copy(f32[1,5,8,16,256]{4,3,2,1,0:T(8,128)} %param.9) | data formatting | bytes 1310720 | tf_op args[0]
  2.2 1.3 collective-permute-start.2
  3.5 4.5 %collective-permute-start.3 = (f32[5,8,1,256]{3,0,2,1:T(8,128)S(1)}, f32[5,8,1,256]{3,0,2,1:T(8,128)S(1)}, u32[]{:S(2)}, u32[]{:S(2)}) collective-permute-start(f32[5,8,1,256]{3,0,2,1:T(8,128)S(1)} %get-tuple-element.18), channel_id=1, source_target_pairs={{0,1},{1,2},{2,3},{3,4},{4,5},{5,6},{6,7},{7,8},{8,9},{9,10},{10,1... | collective-permute-start | bytes 122888 | tf_op jit(solution)/shard_map/ppermute | solution.py:28
  8.1 1.3 collective-permute-start
  9.4 3.0 %collective-permute-start.1 = (f32[5,1,16,256]{3,0,2,1:T(8,128)S(1)}, f32[5,1,16,256]{3,0,2,1:T(8,128)S(1)}, u32[]{:S(2)}, u32[]{:S(2)}) collective-permute-start(f32[5,1,16,256]{3,0,2,1:T(8,128)S(1)} %get-tuple-element.16), channel_id=1, source_target_pairs={{0,16},{16,32},{32,48},{48,64},{64,80},{80,96},{96,112},{1,17},{17... | collective-permute-start | bytes 245768 | tf_op jit(solution)/shard_map/ppermute | solution.py:28
  15.2 1.2 convolution_bitcast_fusion.11
  19.8 2.0 %fusion.94 = f32[5,8,16,256]{3,0,2,1:T(8,128)S(1)} fusion(f32[5,8,16,256]{3,0,2,1:T(8,128)S(1)} %bitcast.184, f32[5,8,16,256]{3,0,2,1:T(8,128)S(1)} %convolution_bitcast_fusion.10, f32[5,8,16,256]{3,0,2,1:T(8,128)S(1)} %convolution_bitcast_fusion.11, f32[5,8,16,256]{3,0,2,1:T(8,128)S(1)} %fusion.61, f32[5,8,16,256]{3,0,2,1:T(8,128)S(1)} %fusion.64, ...), kind=kOutput, calls=%fused_computation.108 | convolution fusion | flops 11816960 | bytes 5455972 | tf_op jit(solution)/shard_map/ec,exyz->cxyz/dot_general | solution.py:54
  21.8 1.3 collective-permute-start.6
  23.1 4.5 %collective-permute-start.7 = (f32[5,8,1,256]{3,0,2,1:T(8,128)S(1)}, f32[5,8,1,256]{3,0,2,1:T(8,128)S(1)}, u32[]{:S(2)}, u32[]{:S(2)}) collective-permute-start(f32[5,8,1,256]{3,0,2,1:T(8,128)S(1)} %get-tuple-element.14), channel_id=1, source_target_pairs={{0,1},{1,2},{2,3},{3,4},{4,5},{5,6},{6,7},{7,8},{8,9},{9,10},{10,1... | collective-permute-start | bytes 122888 | tf_op jit(solution)/shard_map/ppermute | solution.py:28
  27.7 1.3 collective-permute-start.4
  29.0 3.2 %collective-permute-start.5 = (f32[5,1,16,256]{3,0,2,1:T(8,128)S(1)}, f32[5,1,16,256]{3,0,2,1:T(8,128)S(1)}, u32[]{:S(2)}, u32[]{:S(2)}) collective-permute-start(f32[5,1,16,256]{3,0,2,1:T(8,128)S(1)} %get-tuple-element.12), channel_id=1, source_target_pairs={{0,16},{16,32},{32,48},{48,64},{64,80},{80,96},{96,112},{1,17},{17... | collective-permute-start | bytes 245768 | tf_op jit(solution)/shard_map/ppermute | solution.py:28
  36.0 1.2 convolution_bitcast_fusion.9
  40.5 2.2 %fusion.119 = (f32[8,16,256]{2,1,0:T(8,128)S(1)}, f32[5,8,16,256]{3,0,2,1:T(8,128)S(1)}) fusion(bf16[1,5,8,16,256]{4,3,2,1,0:T(8,128)(2,1)S(1)} %copy-done.3, f32[5,8,16,256]{3,0,2,1:T(8,128)S(1)} %fusion.94, f32[5,8,16,256]{3,0,2,1:T(8,128)S(1)} %convolution_bitcast_fusion.8, f32[5,8,16,256]{3,0,2,1:T(8,128)S(1)} %convolution_bitcast_fusion.9, ...), kind=kOutput, calls=%fused_computation.134 | convolution fusion | flops 12275712 | bytes 5914724 | tf_op jit(solution)/shard_map/ec,exyz->cxyz/dot_general | solution.py:54
  42.7 1.3 collective-permute-start.10
  44.0 4.5 %collective-permute-start.11 = (f32[5,8,1,256]{3,0,2,1:T(8,128)S(1)}, f32[5,8,1,256]{3,0,2,1:T(8,128)S(1)}, u32[]{:S(2)}, u32[]{:S(2)}) collective-permute-start(f32[5,8,1,256]{3,0,2,1:T(8,128)S(1)} %get-tuple-element.10), channel_id=1, source_target_pairs={{0,1},{1,2},{2,3},{3,4},{4,5},{5,6},{6,7},{7,8},{8,9},{9,10},{10,1... | collective-permute-start | bytes 122888 | tf_op jit(solution)/shard_map/ppermute | solution.py:28
  48.6 1.3 collective-permute-start.8
  49.9 4.8 %collective-permute-start.9 = (f32[5,1,16,256]{3,0,2,1:T(8,128)S(1)}, f32[5,1,16,256]{3,0,2,1:T(8,128)S(1)}, u32[]{:S(2)}, u32[]{:S(2)}) collective-permute-start(f32[5,1,16,256]{3,0,2,1:T(8,128)S(1)} %get-tuple-element.8), channel_id=1, source_target_pairs={{0,16},{16,32},{32,48},{48,64},{64,80},{80,96},{96,112},{1,17},{17... | collective-permute-start | bytes 245768 | tf_op jit(solution)/shard_map/ppermute | solution.py:28
  55.3 17.2 %psum.35 = f32[4096]{0:T(1024)S(1)} all-reduce(f32[4096]{0:T(1024)S(1)} %mul.63), channel_id=1, replica_groups=mesh['cond'=2,'gx_0'=4,'gx_1'=2,'yz_0'=4,'yz_1'=4] {'cond'}, use_global_device_ids=true, to_apply=%region_3.4 | all-reduce | flops 4096 | bytes 32768 | tf_op jit(solution)/shard_map/psum | solution.py:41
  72.5 18.6 %psum.36 = f32[4096]{0:T(1024)S(1)} all-reduce(f32[4096]{0:T(1024)S(1)} %psum.35), channel_id=1, replica_groups=mesh['cond'=2,'gx_0'=4,'gx_1'=2,'yz_0'=4,'yz_1'=4] {'gx_0'}, use_global_device_ids=true, to_apply=%region_4.5 | all-reduce | flops 4096 | bytes 32768 | tf_op jit(solution)/shard_map/psum | solution.py:41
  91.1 3.3 %psum.37 = f32[4096]{0:T(1024)S(1)} all-reduce(f32[4096]{0:T(1024)S(1)} %psum.36), channel_id=1, replica_groups=mesh['cond'=2,'gx_0'=4,'gx_1'=2,'yz_0'=4,'yz_1'=4] {'gx_1'}, use_global_device_ids=true, to_apply=%region_5.6 | all-reduce | flops 4096 | bytes 32768 | tf_op jit(solution)/shard_map/psum | solution.py:41
  95.5 22.5 %psum.38 = f32[4096]{0:T(1024)S(1)} all-reduce(f32[4096]{0:T(1024)S(1)} %psum.37), channel_id=1, replica_groups=mesh['cond'=2,'gx_0'=4,'gx_1'=2,'yz_0'=4,'yz_1'=4] {'yz_0'}, use_global_device_ids=true, to_apply=%region_6.7 | all-reduce | flops 4096 | bytes 32768 | tf_op jit(solution)/shard_map/psum | solution.py:41
  118.0 18.6 %psum.39 = f32[4096]{0:T(1024)S(1)} all-reduce(f32[4096]{0:T(1024)S(1)} %psum.38), channel_id=1, replica_groups=mesh['cond'=2,'gx_0'=4,'gx_1'=2,'yz_0'=4,'yz_1'=4] {'yz_1'}, use_global_device_ids=true, to_apply=%region_7.8 | all-reduce | flops 4096 | bytes 32768 | tf_op jit(solution)/shard_map/psum | solution.py:41
  138.9 1.2 convolution_bitcast_fusion.7
  143.3 2.0 %fusion.86 = f32[1,5,8,16,256]{4,1,3,2,0:T(8,128)S(1)} fusion(f32[5,8,16,256]{3,0,2,1:T(8,128)S(1)} %convolution_bitcast_fusion.6, f32[5,8,16,256]{3,0,2,1:T(8,128)S(1)} %convolution_bitcast_fusion.7, f32[5,8,16,256]{3,0,2,1:T(8,128)S(1)} %fusion.49, f32[5,8,16,256]{3,0,2,1:T(8,128)S(1)} %fusion.52, f32[5,8,16,256]{3,0,2,1:T(8,128)S(1)} %convolution_bitcast_fusion, ...), kind=kOutput, calls=%fused_computation.100 | convolution fusion | flops 11325440 | bytes 5455972 | tf_op jit(solution)/shard_map/ec,exyz->cxyz/dot_general | solution.py:54
  (73 shorter events, 19.9 us)
Async XLA Ops:
  0.6 54.1 %copy-start = (f32[256,128]{1,0:T(8,128)S(1)}, f32[256,128]{1,0:T(8,128)}, u32[]{:S(2)}) copy-start(f32[256,128]{1,0:T(8,128)} %param.16) | copy-start | bytes 393220
  0.6 11.8 %copy-start.4 = (f32[1,6,5,5]{1,0,3,2:T(1,128)S(1)}, f32[1,6,5,5]{1,0,3,2:T(1,128)}, u32[]{:S(2)}) copy-start(f32[1,6,5,5]{1,0,3,2:T(1,128)} %param.12) | copy-start | bytes 1804
  2.2 11.2 %collective-permute-start.2 = (f32[5,8,1,256]{3,0,2,1:T(8,128)S(1)}, f32[5,8,1,256]{3,0,2,1:T(8,128)S(1)}, u32[]{:S(2)}, u32[]{:S(2)}) collective-permute-start(f32[5,8,1,256]{3,0,2,1:T(8,128)S(1)} %get-tuple-element.19), channel_id=1, source_target_pairs={{1,0},{2,1},{3,2},{4,3},{5,4},{6,5},{7,6},{8,7},{9,8},{10,9},{11,1... | collective-permute-start | bytes 122888 | tf_op jit(solution)/shard_map/ppermute | solution.py:29
  3.5 10.0 %collective-permute-start.3 = (f32[5,8,1,256]{3,0,2,1:T(8,128)S(1)}, f32[5,8,1,256]{3,0,2,1:T(8,128)S(1)}, u32[]{:S(2)}, u32[]{:S(2)}) collective-permute-start(f32[5,8,1,256]{3,0,2,1:T(8,128)S(1)} %get-tuple-element.18), channel_id=1, source_target_pairs={{0,1},{1,2},{2,3},{3,4},{4,5},{5,6},{6,7},{7,8},{8,9},{9,10},{10,1... | collective-permute-start | bytes 122888 | tf_op jit(solution)/shard_map/ppermute | solution.py:28
  8.1 5.4 %collective-permute-start = (f32[5,1,16,256]{3,0,2,1:T(8,128)S(1)}, f32[5,1,16,256]{3,0,2,1:T(8,128)S(1)}, u32[]{:S(2)}, u32[]{:S(2)}) collective-permute-start(f32[5,1,16,256]{3,0,2,1:T(8,128)S(1)} %get-tuple-element.17), channel_id=1, source_target_pairs={{16,0},{32,16},{48,32},{64,48},{80,64},{96,80},{112,96},{17,1},{33... | collective-permute-start | bytes 245768 | tf_op jit(solution)/shard_map/ppermute | solution.py:29
  9.4 4.1 %collective-permute-start.1 = (f32[5,1,16,256]{3,0,2,1:T(8,128)S(1)}, f32[5,1,16,256]{3,0,2,1:T(8,128)S(1)}, u32[]{:S(2)}, u32[]{:S(2)}) collective-permute-start(f32[5,1,16,256]{3,0,2,1:T(8,128)S(1)} %get-tuple-element.16), channel_id=1, source_target_pairs={{0,16},{16,32},{32,48},{48,64},{64,80},{80,96},{96,112},{1,17},{17... | collective-permute-start | bytes 245768 | tf_op jit(solution)/shard_map/ppermute | solution.py:28
  17.5 2.2 %copy-start.1 = (f32[1,5,8,16,256]{4,3,2,1,0:T(8,128)S(1)}, f32[1,5,8,16,256]{4,3,2,1,0:T(8,128)}, u32[]{:S(2)}) copy-start(f32[1,5,8,16,256]{4,3,2,1,0:T(8,128)} %param.10) | copy-start | bytes 1966084
  17.5 2.2 %copy-start.2 = (f32[8,16,256]{2,1,0:T(8,128)S(1)}, f32[8,16,256]{2,1,0:T(8,128)}, u32[]{:S(2)}) copy-start(f32[8,16,256]{2,1,0:T(8,128)} %param.11) | copy-start | bytes 393220
  19.7 12.5 %copy-start.7 = (s32[2]{0:T(128)S(1)}, s32[2]{0:T(128)}, u32[]{:S(2)}) copy-start(s32[2]{0:T(128)} %param.17) | copy-start | bytes 28
  19.7 13.1 %copy-start.6 = (s32[8,16]{1,0:T(8,128)S(1)}, s32[8,16]{1,0:T(8,128)}, u32[]{:S(2)}) copy-start(s32[8,16]{1,0:T(8,128)} %param.15) | copy-start | bytes 1540
  21.8 12.4 %collective-permute-start.6 = (f32[5,8,1,256]{3,0,2,1:T(8,128)S(1)}, f32[5,8,1,256]{3,0,2,1:T(8,128)S(1)}, u32[]{:S(2)}, u32[]{:S(2)}) collective-permute-start(f32[5,8,1,256]{3,0,2,1:T(8,128)S(1)} %get-tuple-element.15), channel_id=1, source_target_pairs={{1,0},{2,1},{3,2},{4,3},{5,4},{6,5},{7,6},{8,7},{9,8},{10,9},{11,1... | collective-permute-start | bytes 122888 | tf_op jit(solution)/shard_map/ppermute | solution.py:29
  23.1 11.2 %collective-permute-start.7 = (f32[5,8,1,256]{3,0,2,1:T(8,128)S(1)}, f32[5,8,1,256]{3,0,2,1:T(8,128)S(1)}, u32[]{:S(2)}, u32[]{:S(2)}) collective-permute-start(f32[5,8,1,256]{3,0,2,1:T(8,128)S(1)} %get-tuple-element.14), channel_id=1, source_target_pairs={{0,1},{1,2},{2,3},{3,4},{4,5},{5,6},{6,7},{7,8},{8,9},{9,10},{10,1... | collective-permute-start | bytes 122888 | tf_op jit(solution)/shard_map/ppermute | solution.py:28
  27.7 6.6 %collective-permute-start.4 = (f32[5,1,16,256]{3,0,2,1:T(8,128)S(1)}, f32[5,1,16,256]{3,0,2,1:T(8,128)S(1)}, u32[]{:S(2)}, u32[]{:S(2)}) collective-permute-start(f32[5,1,16,256]{3,0,2,1:T(8,128)S(1)} %get-tuple-element.13), channel_id=1, source_target_pairs={{16,0},{32,16},{48,32},{64,48},{80,64},{96,80},{112,96},{17,1},{33... | collective-permute-start | bytes 245768 | tf_op jit(solution)/shard_map/ppermute | solution.py:29
  29.0 5.3 %collective-permute-start.5 = (f32[5,1,16,256]{3,0,2,1:T(8,128)S(1)}, f32[5,1,16,256]{3,0,2,1:T(8,128)S(1)}, u32[]{:S(2)}, u32[]{:S(2)}) collective-permute-start(f32[5,1,16,256]{3,0,2,1:T(8,128)S(1)} %get-tuple-element.12), channel_id=1, source_target_pairs={{0,16},{16,32},{32,48},{48,64},{64,80},{80,96},{96,112},{1,17},{17... | collective-permute-start | bytes 245768 | tf_op jit(solution)/shard_map/ppermute | solution.py:28
  38.3 2.2 %copy-start.3 = (bf16[1,5,8,16,256]{4,3,2,1,0:T(8,128)(2,1)S(1)}, bf16[1,5,8,16,256]{4,3,2,1,0:T(8,128)(2,1)}, u32[]{:S(2)}) copy-start(bf16[1,5,8,16,256]{4,3,2,1,0:T(8,128)(2,1)} %param.13) | copy-start | bytes 983044
  40.5 14.2 %copy-start.5 = (s32[8,16,256]{2,1,0:T(8,128)S(1)}, s32[8,16,256]{2,1,0:T(8,128)}, u32[]{:S(2)}) copy-start(s32[8,16,256]{2,1,0:T(8,128)} %param.14) | copy-start | bytes 393220
  42.7 94.4 %collective-permute-start.10 = (f32[5,8,1,256]{3,0,2,1:T(8,128)S(1)}, f32[5,8,1,256]{3,0,2,1:T(8,128)S(1)}, u32[]{:S(2)}, u32[]{:S(2)}) collective-permute-start(f32[5,8,1,256]{3,0,2,1:T(8,128)S(1)} %get-tuple-element.11), channel_id=1, source_target_pairs={{1,0},{2,1},{3,2},{4,3},{5,4},{6,5},{7,6},{8,7},{9,8},{10,9},{11,1... | collective-permute-start | bytes 122888 | tf_op jit(solution)/shard_map/ppermute | solution.py:29
  44.0 93.1 %collective-permute-start.11 = (f32[5,8,1,256]{3,0,2,1:T(8,128)S(1)}, f32[5,8,1,256]{3,0,2,1:T(8,128)S(1)}, u32[]{:S(2)}, u32[]{:S(2)}) collective-permute-start(f32[5,8,1,256]{3,0,2,1:T(8,128)S(1)} %get-tuple-element.10), channel_id=1, source_target_pairs={{0,1},{1,2},{2,3},{3,4},{4,5},{5,6},{6,7},{7,8},{8,9},{9,10},{10,1... | collective-permute-start | bytes 122888 | tf_op jit(solution)/shard_map/ppermute | solution.py:28
  48.6 88.6 %collective-permute-start.8 = (f32[5,1,16,256]{3,0,2,1:T(8,128)S(1)}, f32[5,1,16,256]{3,0,2,1:T(8,128)S(1)}, u32[]{:S(2)}, u32[]{:S(2)}) collective-permute-start(f32[5,1,16,256]{3,0,2,1:T(8,128)S(1)} %get-tuple-element.9), channel_id=1, source_target_pairs={{16,0},{32,16},{48,32},{64,48},{80,64},{96,80},{112,96},{17,1},{33... | collective-permute-start | bytes 245768 | tf_op jit(solution)/shard_map/ppermute | solution.py:29
  49.9 87.3 %collective-permute-start.9 = (f32[5,1,16,256]{3,0,2,1:T(8,128)S(1)}, f32[5,1,16,256]{3,0,2,1:T(8,128)S(1)}, u32[]{:S(2)}, u32[]{:S(2)}) collective-permute-start(f32[5,1,16,256]{3,0,2,1:T(8,128)S(1)} %get-tuple-element.8), channel_id=1, source_target_pairs={{0,16},{16,32},{32,48},{48,64},{64,80},{80,96},{96,112},{1,17},{17... | collective-permute-start | bytes 245768 | tf_op jit(solution)/shard_map/ppermute | solution.py:28
where the time goes:
time: 147 us; the launch traced here: 146 us
  blocking collectives  80.2 us (55%)
  starting transfers between devices  32.4 us (22%)
  matrix products  23 us (16%)
  local copies, waits for them, and re-layouts  5.6 us (4%)
  other arithmetic  2.59 us (2%)
  between operations  2.56 us (2%)
    psum x5, blocking collectives, one_axis_at_a_time(): return functools.reduce(lax.psum, axes, x)  80.2 us
    ppermute x6, starting transfers between devices, padded(): lax.ppermute(last, axis, up)  24.7 us
    dot_general x18, matrix products, apply_operator(): jnp.einsum('ec,exyz->cxyz', blocks[direction], shifted, precision=lax.Pre...  22.6 us
    ppermute x6, starting transfers between devices, padded(): lax.ppermute(initial, axis, [(b, a) for a, b in up])  7.75 us
    unnamed x25, local copies, waits for them, and re-layouts  4.44 us
  transfers between devices with their start and end apart: 12, of which 0 were waited for; matrix products, arithmetic and copies ran while one was open for 3% of the time, Pallas kernels for 0%

commit v1 on v0

v1 whole, which is shorter than its diff:
```python
import functools

import jax
import jax.numpy as jnp
from jax import lax
from jax.experimental import pallas as pl
from jax.experimental.pallas import tpu as pltpu
from jax.sharding import Mesh
from jax.sharding import PartitionSpec as P

NDES = 4096
GX = ("gx_0", "gx_1")
YZ = ("yz_0", "yz_1")
RING = ("cond", "yz_1")
SPREAD = ("gx_0", "gx_1", "yz_0")
RELAXATION = 0.8
HIGHEST = lax.Precision.HIGHEST

VMEM = pl.BlockSpec(memory_space=pltpu.VMEM)
SMEM = pl.BlockSpec(memory_space=pltpu.SMEM)


def f32(*shape):
    return jax.ShapeDtypeStruct(shape, jnp.float32)


def position():
    gx = lax.axis_index("gx_0") * 2 + lax.axis_index("gx_1")
    yz = lax.axis_index("yz_0") * 4 + lax.axis_index("yz_1")
    return gx, yz


def write_sides(read, nvar, nx, ny, xa_ref, xb_ref, ya_ref, yb_ref):
    gx, yz = position()
    gx_even, yz_even = lax.rem(gx, 2) == 0, lax.rem(yz, 2) == 0
    for k in range(nvar):
        low, high = read(k, 0), read(k, nx - 1)
        xa_ref[k] = jnp.where(gx_even, high, low)
        xb_ref[k] = jnp.where(gx_even, low, high)
        for x in range(nx):
            slab = read(k, x)
            first, last = slab[0:1], slab[ny - 1 : ny]
            ya_ref[k, x : x + 1, :] = jnp.where(yz_even, last, first)
            yb_ref[k, x : x + 1, :] = jnp.where(yz_even, first, last)


def sides_kernel(v_ref, xa_ref, xb_ref, ya_ref, yb_ref):
    nvar, nx, ny, _ = v_ref.shape
    write_sides(lambda k, x: v_ref[k, x], nvar, nx, ny, xa_ref, xb_ref, ya_ref, yb_ref)


def neighbour_sums(v_ref, blocks_ref, x):
    nvar, nx, ny, nz = v_ref.shape
    row = lax.broadcasted_iota(jnp.int32, (ny, nz), 0)
    lane = lax.broadcasted_iota(jnp.int32, (ny, nz), 1)
    sums = [None] * nvar
    for e in range(nvar):
        centre = v_ref[e, x]
        shifted = {}
        if x + 1 < nx:
            shifted[0] = v_ref[e, x + 1]
        if x > 0:
            shifted[1] = v_ref[e, x - 1]
        shifted[2] = jnp.where(row == ny - 1, 0.0, pltpu.roll(centre, ny - 1, 0))
        shifted[3] = jnp.where(row == 0, 0.0, pltpu.roll(centre, 1, 0))
        shifted[4] = jnp.where(lane == nz - 1, 0.0, pltpu.roll(centre, nz - 1, 1))
        shifted[5] = jnp.where(lane == 0, 0.0, pltpu.roll(centre, 1, 1))
        for d, values in shifted.items():
            for k in range(nvar):
                term = blocks_ref[0, d, e, k] * values
                sums[k] = term if sums[k] is None else sums[k] + term
    return sums


def inner_sweep_kernel(blocks_ref, v_ref, source_ref, diagonal_ref, out_ref):
    nvar, nx, _, _ = v_ref.shape
    for x in range(nx):
        sums = neighbour_sums(v_ref, blocks_ref, x)
        diagonal = diagonal_ref[x]
        scale = RELAXATION / diagonal
        for k in range(nvar):
            value = v_ref[k, x]
            out_ref[k, x] = value + scale * (source_ref[k, x] - diagonal * value + sums[k])


def inner_residual_kernel(blocks_ref, v_ref, source_ref, diagonal_ref, out_ref):
    nvar, nx, _, _ = v_ref.shape
    for x in range(nx):
        sums = neighbour_sums(v_ref, blocks_ref, x)
        diagonal = diagonal_ref[x]
        for k in range(nvar):
            out_ref[k, x] = source_ref[k, x] - diagonal * v_ref[k, x] + sums[k]


def add_halo(blocks_ref, inner_ref, diagonal_ref, xa_ref, xb_ref, ya_ref, yb_ref, out_ref):
    nvar, nx, ny, nz = inner_ref.shape
    gx, yz = position()
    gx_even, yz_even = lax.rem(gx, 2) == 0, lax.rem(yz, 2) == 0
    has_low_x, has_high_x = gx > 0, gx < 7
    has_low_y, has_high_y = yz > 0, yz < 15

    def halo_sums(direction, pick):
        sums = [None] * nvar
        for e in range(nvar):
            values = pick(e)
            for k in range(nvar):
                term = blocks_ref[0, direction, e, k] * values
                sums[k] = term if sums[k] is None else sums[k] + term
        return sums

    def picker(even, a_ref, b_ref, exists):
        return lambda e: jnp.where(exists, jnp.where(even, a_ref[e], b_ref[e]), 0.0)

    high_y = halo_sums(2, picker(yz_even, ya_ref, yb_ref, has_high_y))
    low_y = halo_sums(3, picker(yz_even, yb_ref, ya_ref, has_low_y))
    row = lax.broadcasted_iota(jnp.int32, (8, nz), 0)
    for x in range(nx):
        if x == 0:
            at_x = halo_sums(1, picker(gx_even, xb_ref, xa_ref, has_low_x))
        elif x == nx - 1:
            at_x = halo_sums(0, picker(gx_even, xa_ref, xb_ref, has_high_x))
        else:
            at_x = None
        for start in range(0, ny, 8):
            rows = slice(start, start + 8)
            scale = None if diagonal_ref is None else RELAXATION / diagonal_ref[x, rows]
            for k in range(nvar):
                more = None
                if start == 0:
                    more = jnp.where(row == 0, low_y[k][x : x + 1], 0.0)
                if start == ny - 8:
                    last = jnp.where(row == 7, high_y[k][x : x + 1], 0.0)
                    more = last if more is None else more + last
                if at_x is not None:
                    more = at_x[k][rows] if more is None else more + at_x[k][rows]
                value = inner_ref[k, x, rows]
                if more is not None:
                    value = value + (more if scale is None else scale * more)
                out_ref[k, x, rows] = value


def outer_sweep_kernel(
    blocks_ref, inner_ref, diagonal_ref, xa_ref, xb_ref, ya_ref, yb_ref,
    out_ref, next_xa_ref, next_xb_ref, next_ya_ref, next_yb_ref,
):
    nvar, nx, ny, _ = inner_ref.shape
    add_halo(blocks_ref, inner_ref, diagonal_ref, xa_ref, xb_ref, ya_ref, yb_ref, out_ref)
    write_sides(
        lambda k, x: out_ref[k, x], nvar, nx, ny, next_xa_ref, next_xb_ref, next_ya_ref, next_yb_ref
    )


def last_sweep_kernel(
    blocks_ref, weights_ref, inner_ref, diagonal_ref, xa_ref, xb_ref, ya_ref, yb_ref,
    sensitivity_ref, mask_ref, slot_ref, basis_ref,
    out_ref, next_xa_ref, next_xb_ref, next_ya_ref, next_yb_ref, gradient_ref, surface_ref,
):
    outer_sweep_kernel(
        blocks_ref, inner_ref, diagonal_ref, xa_ref, xb_ref, ya_ref, yb_ref,
        out_ref, next_xa_ref, next_xb_ref, next_ya_ref, next_yb_ref,
    )
    nvar, nx, ny, _ = inner_ref.shape
    for x in range(nx):
        total = out_ref[0, x] * sensitivity_ref[0, x].astype(jnp.float32)
        for k in range(1, nvar):
            total = total + out_ref[k, x] * sensitivity_ref[k, x].astype(jnp.float32)
        surface_ref[x * ny : (x + 1) * ny, :] = mask_ref[x].astype(jnp.float32) * total
    projected = jnp.dot(
        surface_ref[...], basis_ref[...], precision=HIGHEST, preferred_element_type=jnp.float32
    )
    patches, band = projected.shape
    half = band // 2
    pairs = NDES // band
    wanted = lax.broadcasted_iota(jnp.int32, (2 * pairs, patches), 0)
    wanted = jnp.where(wanted < pairs, 2 * wanted, 2 * (wanted - pairs) + 1)
    onehot = (wanted == slot_ref[...]).astype(jnp.float32)
    by_slot = jnp.dot(onehot, projected, precision=HIGHEST, preferred_element_type=jnp.float32)
    even, odd = by_slot[:pairs], pltpu.roll(by_slot[pairs:], half, 1)
    row = lax.broadcasted_iota(jnp.int32, (pairs, band), 0)
    lane = lax.broadcasted_iota(jnp.int32, (pairs, band), 1)
    before = jnp.where(row == 0, 0.0, pltpu.roll(odd, 1, 0))
    gradient = even + jnp.where(lane < half, before, odd)
    mine = jnp.where(lax.axis_index("cond") == 0, weights_ref[0], weights_ref[1])
    total = weights_ref[0].astype(jnp.float32) + weights_ref[1].astype(jnp.float32)
    one = jnp.ones((pairs, band), jnp.float32)
    gradient_ref[...] = gradient * ((one * mine.astype(jnp.float32)) / (one * total))


def outer_residual_kernel(
    blocks_ref, inner_ref, xa_ref, xb_ref, ya_ref, yb_ref, out_ref,
):
    add_halo(blocks_ref, inner_ref, None, xa_ref, xb_ref, ya_ref, yb_ref, out_ref)


def swap_a(n):
    return [(i, i ^ 1) for i in range(n)]


def swap_b(n):
    return [(i, (((i + 1) ^ 1) - 1) % n) for i in range(n)]


def exchange(xa, xb, ya, yb):
    far = lax.ppermute(yb, YZ, swap_b(16))
    near = lax.ppermute(ya, YZ, swap_a(16))
    chip = lax.ppermute(xb, GX, swap_b(8))
    core = lax.ppermute(xa, GX, swap_a(8))
    return core, chip, near, far


def local(
    adjoint,
    objective_gradient,
    diagonal,
    flux_blocks,
    flux_sensitivity,
    surface_mask,
    patch_band_slot,
    design_basis,
    condition_weights,
):
    v, source, sensitivity = adjoint[0], objective_gradient[0], flux_sensitivity[0]
    nvar, nx, ny, nz = v.shape
    field = f32(nvar, nx, ny, nz)
    sides = (f32(nvar, ny, nz), f32(nvar, ny, nz), f32(nvar, nx, nz), f32(nvar, nx, nz))
    slot = patch_band_slot.reshape(1, -1)

    first = pl.pallas_call(
        sides_kernel, out_shape=sides, in_specs=[VMEM], out_specs=[VMEM] * 4, name="sides"
    )(v)
    halo = exchange(*first)
    inner_sweep = pl.pallas_call(
        inner_sweep_kernel, out_shape=field, in_specs=[SMEM] + [VMEM] * 3, out_specs=VMEM, name="inner_sweep"
    )
    inner = inner_sweep(flux_blocks, v, source, diagonal)
    relaxed, *second = pl.pallas_call(
        outer_sweep_kernel,
        out_shape=(field, *sides),
        in_specs=[SMEM] + [VMEM] * 6,
        out_specs=[VMEM] * 5,
        name="outer_sweep",
    )(flux_blocks, inner, diagonal, *halo)

    halo = exchange(*second)
    inner = inner_sweep(flux_blocks, relaxed, source, diagonal)
    smoothed, xa, xb, ya, yb, gradient = pl.pallas_call(
        last_sweep_kernel,
        out_shape=(field, *sides, f32(NDES // 128, 128)),
        in_specs=[SMEM, SMEM] + [VMEM] * 10,
        out_specs=[VMEM] * 6,
        scratch_shapes=[pltpu.VMEM((nx * ny, nz), jnp.float32)],
        name="last_sweep",
    )(flux_blocks, condition_weights, inner, diagonal, *halo, sensitivity, surface_mask, slot, design_basis)

    halo = exchange(xa, xb, ya, yb)
    parts = lax.all_to_all(gradient, SPREAD, 0, 0, tiled=True)
    total = jnp.sum(parts, axis=0, keepdims=True)
    total = total + lax.ppermute(total, RING, [(i, i ^ 1) for i in range(8)])
    total = total + lax.ppermute(total, RING, [(i, (((i + 1) ^ 1) - 1) % 8) for i in range(8)])
    total = total + lax.ppermute(total, RING, [(0, 3), (3, 0), (1, 6), (6, 1), (2, 5), (5, 2), (4, 7), (7, 4)])
    design_gradient = lax.dynamic_slice(total, (0, lax.axis_index("yz_1") * 32), (1, 32))[0]

    inner = pl.pallas_call(
        inner_residual_kernel, out_shape=field, in_specs=[SMEM] + [VMEM] * 3, out_specs=VMEM, name="inner_residual"
    )(flux_blocks, smoothed, source, diagonal)
    residual = pl.pallas_call(
        outer_residual_kernel, out_shape=field, in_specs=[SMEM] + [VMEM] * 5, out_specs=VMEM, name="outer_residual"
    )(flux_blocks, inner, *halo)
    return smoothed[None], residual[None], design_gradient


def solution(mesh):
    torus = Mesh(
        mesh.devices.reshape(mesh.shape["cond"], 4, 2, 4, 4),
        ("cond", "gx_0", "gx_1", "yz_0", "yz_1"),
    )
    in_specs = (
        P("cond", None, GX, YZ, None),
        P("cond", None, GX, YZ, None),
        P(GX, YZ, None),
        P("cond", None, None, None),
        P("cond", None, GX, YZ, None),
        P(GX, YZ, None),
        P(GX, YZ),
        P(),
        P(),
    )
    out_specs = (P("cond", None, GX, YZ, None), P("cond", None, GX, YZ, None), P(GX + YZ))
    return jax.shard_map(local, mesh=torus, in_specs=in_specs, out_specs=out_specs, check_vma=False)
```

time: 147 us -> 69.9 us (0.48)
  the two profiles are of different devices: /device:TPU:0 before, /device:TPU:1 now
where the time goes in v1:
time: 69.9 us; the launch traced here: 69.6 us
  starting transfers between devices  27.8 us (40%)
  Pallas kernels  20.7 us (30%)
  blocking collectives  11.9 us (17%)
  local copies, waits for them, and re-layouts  5.08 us (7%)
  waiting for transfers between devices  3.2 us (5%)
  between operations  0.78 us (1%)
    all_to_all x1, blocking collectives, local(): parts = lax.all_to_all(gradient, SPREAD, 0, 0, tiled=True)  11.9 us
    ppermute x3, starting transfers between devices, exchange(): far = lax.ppermute(yb, YZ, swap_b(16))  9.77 us
    ppermute x3, starting transfers between devices, exchange(): core = lax.ppermute(xa, GX, swap_a(8))  9.46 us
    ppermute x1, starting transfers between devices, local(): lax.ppermute(total, RING, [(i, ((i + 1 ^ 1) - 1) % 8) for i in range(8)])  4.57 us
    unnamed x31, local copies, waits for them, and re-layouts  3.91 us
    pallas_call x1, Pallas kernels, local(): inner = inner_sweep(flux_blocks, relaxed, source, diagonal)  3.8 us
    pallas_call x1, Pallas kernels, local(): inner = inner_sweep(flux_blocks, v, source, diagonal)  3.8 us
    pallas_call x1, Pallas kernels, local(): pl.pallas_call(inner_residual_kernel, out_shape=field, in_specs=[SMEM] +...  3.76 us
  transfers between devices with their start and end apart: 15, of which 2 were waited for; matrix products, arithmetic and copies ran while one was open for 3% of the time, Pallas kernels for 16%

profile of v1, /device:TPU:1, one launch (start us, length us, event | category | flops | bytes accessed | tf_op | source)
XLA Modules:
  0.0 69.6 jit_solution(6645368172338554952)
XLA Ops:
  0.6 1.8 %sides.1 = (f32[5,16,256]{2,1,0:T(8,128)}, f32[5,16,256]{2,1,0:T(8,128)}, f32[5,8,256]{2,1,0:T(8,128)}, f32[5,8,256]{2,1,0:T(8,128)}) custom-call(f32[5,8,16,256]{3,2,1,0:T(8,128)} %bitcast.15), custom_call_target="tpu_custom_call" | custom-call | tf_op jit(solution)/shard_map/sides/pallas_call | solution.py:228
  2.5 3.2 %collective-permute-start = (f32[5,16,256]{2,1,0:T(8,128)}, f32[5,16,256]{2,1,0:T(8,128)S(1)}, u32[]{:S(2)}, u32[]{:S(2)}) collective-permute-start(f32[5,16,256]{2,1,0:T(8,128)} %get-tuple-element.18), channel_id=1, source_target_pairs={{0,16},{16,0},{32,48},{48,32},{64,80},{80,64},{96,112},{112,96},{1... | collective-permute-start | bytes 245768 | tf_op jit(solution)/shard_map/ppermute | solution.py:207
  5.7 1.1 %collective-permute-start.2 = (f32[5,8,256]{2,1,0:T(8,128)}, f32[5,8,256]{2,1,0:T(8,128)S(1)}, u32[]{:S(2)}, u32[]{:S(2)}) collective-permute-start(f32[5,8,256]{2,1,0:T(8,128)} %get-tuple-element.20), channel_id=1, source_target_pairs={{0,1},{1,0},{2,3},{3,2},{4,5},{5,4},{6,7},{7,6},{8,9},{9,8},{10,11... | collective-permute-start | bytes 122888 | tf_op jit(solution)/shard_map/ppermute | solution.py:205
  6.8 4.9 %collective-permute-start.3 = (f32[5,8,256]{2,1,0:T(8,128)}, f32[5,8,256]{2,1,0:T(8,128)S(1)}, u32[]{:S(2)}, u32[]{:S(2)}) collective-permute-start(f32[5,8,256]{2,1,0:T(8,128)} %get-tuple-element.21), channel_id=1, source_target_pairs={{0,15},{1,2},{2,1},{3,4},{4,3},{5,6},{6,5},{7,8},{8,7},{9,10},{10,... | collective-permute-start | bytes 122888 | tf_op jit(solution)/shard_map/ppermute | solution.py:204
  11.7 0.7 %copy.21.blocks_ref = f32[1,6,5,5]{3,2,1,0:T(8,128)} copy(f32[1,6,5,5]{1,0,3,2:T(1,128)S(1)} %copy-done.12) | data formatting | bytes 1200 | tf_op args[3]
  12.4 3.8 %inner_sweep.2.inner_ref = f32[5,8,16,256]{3,2,1,0:T(8,128)} custom-call(f32[1,6,5,5]{3,2,1,0:T(8,128)} %copy.21.blocks_ref, f32[5,8,16,256]{3,2,1,0:T(8,128)} %bitcast.16, f32[5,8,16,256]{3,2,1,0:T(8,128)} %bitcast.12, f32[8,16,256]{2,1,0:T(8,128)} %diagonal_ref.9), custom_call_target="tpu_custom_call" | custom-call | tf_op jit(solution)/shard_map/inner_sweep/pallas_call | solution.py:235
  16.9 0.6 copy-done.4
  17.5 2.3 %outer_sweep.1 = (f32[5,8,16,256]{3,2,1,0:T(8,128)}, f32[5,16,256]{2,1,0:T(8,128)}, f32[5,16,256]{2,1,0:T(8,128)}, f32[5,8,256]{2,1,0:T(8,128)}, f32[5,8,256]{2,1,0:T(8,128)}) custom-call(f32[1,6,5,5]{3,2,1,0:T(8,128)} %copy.21.blocks_ref, f32[5,8,16,256]{3,2,1,0:T(8,128)} %inner_sweep.2.inner_ref, f32[8,16,256]{2,1,0:T(8,128)} %diagonal_ref.9, ...), custom_call_target="tpu_custom_call" | custom-call | tf_op jit(solution)/shard_map/outer_sweep/pallas_call | solution.py:236
  19.9 2.4 %collective-permute-start.4 = (f32[5,16,256]{2,1,0:T(8,128)}, f32[5,16,256]{2,1,0:T(8,128)S(1)}, u32[]{:S(2)}, u32[]{:S(2)}) collective-permute-start(f32[5,16,256]{2,1,0:T(8,128)} %get-tuple-element.23), channel_id=1, source_target_pairs={{0,16},{16,0},{32,48},{48,32},{64,80},{80,64},{96,112},{112,96},{1... | collective-permute-start | bytes 245768 | tf_op jit(solution)/shard_map/ppermute | solution.py:207
  22.3 3.3 %collective-permute-start.7 = (f32[5,8,256]{2,1,0:T(8,128)}, f32[5,8,256]{2,1,0:T(8,128)S(1)}, u32[]{:S(2)}, u32[]{:S(2)}) collective-permute-start(f32[5,8,256]{2,1,0:T(8,128)} %get-tuple-element.26), channel_id=1, source_target_pairs={{0,15},{1,2},{2,1},{3,4},{4,3},{5,6},{6,5},{7,8},{8,7},{9,10},{10,... | collective-permute-start | bytes 122888 | tf_op jit(solution)/shard_map/ppermute | solution.py:204
  25.5 0.6 reshape.11.slot_ref
  26.1 3.8 %inner_sweep.3.inner_ref = f32[5,8,16,256]{3,2,1,0:T(8,128)} custom-call(f32[1,6,5,5]{3,2,1,0:T(8,128)} %copy.21.blocks_ref, f32[5,8,16,256]{3,2,1,0:T(8,128)} %get-tuple-element.22.v_ref, f32[5,8,16,256]{3,2,1,0:T(8,128)} %bitcast.13, f32[8,16,256]{2,1,0:T(8,128)} %diagonal_ref.9), custom_call_target="tpu_custom_call" | custom-call | tf_op jit(solution)/shard_map/inner_sweep/pallas_call | solution.py:245
  30.6 3.0 %last_sweep.1 = (f32[5,8,16,256]{3,2,1,0:T(8,128)}, f32[5,16,256]{2,1,0:T(8,128)}, f32[5,16,256]{2,1,0:T(8,128)}, f32[5,8,256]{2,1,0:T(8,128)}, f32[5,8,256]{2,1,0:T(8,128)}, /*index=5*/f32[32,128]{1,0:T(8,128)}) custom-call(f32[1,6,5,5]{3,2,1,0:T(8,128)} %copy.21.blocks_ref, s32[2]{0:T(128)} %weights_ref.1, f32[5,8,16,256]{3,2,1,0:T(8,128)} %inner_sweep.3.inner_ref, ...), custom_call_target="tpu_custom_call" | custom-call | tf_op jit(solution)/shard_map/last_sweep/pallas_call | solution.py:246
  33.6 11.9 %all_to_all.9 = f32[32,1,128]{2,1,0:T(1,128)S(1)} all-to-all(f32[32,1,128]{2,1,0:T(1,128)} %bitcast.20), channel_id=1, replica_groups=mesh['cond'=2,'gx_0'=4,'gx_1'=2,'yz_0'=4,'yz_1'=4] {'gx_0','gx_1','yz_0'}, dimensions={0} | all-to-all | bytes 32768 | tf_op jit(solution)/shard_map/all_to_all | solution.py:256
  45.9 2.2 %collective-permute-done.12 = f32[1,128]{1,0:T(1,128)S(1)} collective-permute-done((f32[1,128]{1,0:T(1,128)S(1)}, f32[1,128]{1,0:T(1,128)S(1)}, u32[]{:S(2)}, u32[]{:S(2)}) %collective-permute-start.12) | collective-permute-done | bytes 544 | tf_op jit(solution)/shard_map/ppermute | solution.py:258
  48.1 4.6 %collective-permute-start.13 = (f32[1,128]{1,0:T(1,128)S(1)}, f32[1,128]{1,0:T(1,128)S(1)}, u32[]{:S(2)}, u32[]{:S(2)}) collective-permute-start(f32[1,128]{1,0:T(1,128)S(1)} %bitcast_add_fusion), channel_id=1, source_target_pairs={{0,131},{1,2},{2,1},{3,128},{128,3},{129,130},{130,129},{131,0},{4... | collective-permute-start | bytes 1544 | tf_op jit(solution)/shard_map/ppermute | solution.py:259
  52.7 1.0 %collective-permute-done.13 = f32[1,128]{1,0:T(1,128)S(1)} collective-permute-done((f32[1,128]{1,0:T(1,128)S(1)}, f32[1,128]{1,0:T(1,128)S(1)}, u32[]{:S(2)}, u32[]{:S(2)}) %collective-permute-start.13) | collective-permute-done | bytes 544 | tf_op jit(solution)/shard_map/ppermute | solution.py:259
  53.7 0.8 %collective-permute-start.14 = (f32[1,128]{1,0:T(1,128)S(1)}, f32[1,128]{1,0:T(1,128)S(1)}, u32[]{:S(2)}, u32[]{:S(2)}) collective-permute-start(f32[1,128]{1,0:T(1,128)S(1)} %add.13), channel_id=1, source_target_pairs={{0,3},{3,0},{1,130},{130,1},{2,129},{129,2},{128,131},{131,128},{4... | collective-permute-start | bytes 1544 | tf_op jit(solution)/shard_map/ppermute | solution.py:260
  54.5 1.5 %collective-permute-start.10 = (f32[5,8,256]{2,1,0:T(8,128)}, f32[5,8,256]{2,1,0:T(8,128)S(1)}, u32[]{:S(2)}, u32[]{:S(2)}) collective-permute-start(f32[5,8,256]{2,1,0:T(8,128)} %get-tuple-element.30), channel_id=1, source_target_pairs={{0,1},{1,0},{2,3},{3,2},{4,5},{5,4},{6,7},{7,6},{8,9},{9,8},{10,11... | collective-permute-start | bytes 122888 | tf_op jit(solution)/shard_map/ppermute | solution.py:205
  56.0 1.6 %collective-permute-start.11 = (f32[5,8,256]{2,1,0:T(8,128)S(1)}, f32[5,8,256]{2,1,0:T(8,128)S(1)}, u32[]{:S(2)}, u32[]{:S(2)}) collective-permute-start(f32[5,8,256]{2,1,0:T(8,128)S(1)} %copy-done.14), channel_id=1, source_target_pairs={{0,15},{1,2},{2,1},{3,4},{4,3},{5,6},{6,5},{7,8},{8,7},{9,10},{10,... | collective-permute-start | bytes 122888 | tf_op jit(solution)/shard_map/ppermute | solution.py:204
  57.6 3.9 %collective-permute-start.8 = (f32[5,16,256]{2,1,0:T(8,128)}, f32[5,16,256]{2,1,0:T(8,128)S(1)}, u32[]{:S(2)}, u32[]{:S(2)}) collective-permute-start(f32[5,16,256]{2,1,0:T(8,128)} %get-tuple-element.28), channel_id=1, source_target_pairs={{0,16},{16,0},{32,48},{48,32},{64,80},{80,64},{96,112},{112,96},{1... | collective-permute-start | bytes 245768 | tf_op jit(solution)/shard_map/ppermute | solution.py:207
  61.7 3.8 %inner_residual.1.inner_ref = f32[5,8,16,256]{3,2,1,0:T(8,128)} custom-call(f32[1,6,5,5]{3,2,1,0:T(8,128)} %copy.21.blocks_ref, f32[5,8,16,256]{3,2,1,0:T(8,128)} %get-tuple-element.27.v_ref, f32[5,8,16,256]{3,2,1,0:T(8,128)} %bitcast.14, f32[8,16,256]{2,1,0:T(8,128)} %diagonal_ref.9), custom_call_target="tpu_custom_call" | custom-call | tf_op jit(solution)/shard_map/inner_residual/pallas_call | solution.py:263
  66.7 0.6 copy-done.5
  67.3 2.2 %outer_residual.1 = f32[5,8,16,256]{3,2,1,0:T(8,128)} custom-call(f32[1,6,5,5]{3,2,1,0:T(8,128)} %copy.21.blocks_ref, f32[5,8,16,256]{3,2,1,0:T(8,128)} %inner_residual.1.inner_ref, f32[5,16,256]{2,1,0:T(8,128)} %copy-done.3, f32[5,16,256]{2,1,0:T(8,128)} %copy-done.5, f32[5,8,256]{2,1,0:T(8,128)} %copy-done.6, f32[5,8,256]{2,1,0:T(8,128)} %copy-done.7), custom_call_target="tpu_custom_call" | custom-call | tf_op jit(solution)/shard_map/outer_residual/pallas_call | solution.py:266
  (51 shorter events, 3.1 us)
Async XLA Ops:
  0.6 11.1 %copy-start.12 = (f32[1,6,5,5]{1,0,3,2:T(1,128)S(1)}, f32[1,6,5,5]{1,0,3,2:T(1,128)}, u32[]{:S(2)}) copy-start(f32[1,6,5,5]{1,0,3,2:T(1,128)} %param.12) | copy-start | bytes 1804
  2.5 13.8 %collective-permute-start = (f32[5,16,256]{2,1,0:T(8,128)}, f32[5,16,256]{2,1,0:T(8,128)S(1)}, u32[]{:S(2)}, u32[]{:S(2)}) collective-permute-start(f32[5,16,256]{2,1,0:T(8,128)} %get-tuple-element.18), channel_id=1, source_target_pairs={{0,16},{16,0},{32,48},{48,32},{64,80},{80,64},{96,112},{112,96},{1... | collective-permute-start | bytes 245768 | tf_op jit(solution)/shard_map/ppermute | solution.py:207
  5.7 10.6 %collective-permute-start.1 = (f32[5,16,256]{2,1,0:T(8,128)}, f32[5,16,256]{2,1,0:T(8,128)S(1)}, u32[]{:S(2)}, u32[]{:S(2)}) collective-permute-start(f32[5,16,256]{2,1,0:T(8,128)} %get-tuple-element.19), channel_id=1, source_target_pairs={{0,112},{16,32},{32,16},{48,64},{64,48},{80,96},{96,80},{112,0},{1... | collective-permute-start | bytes 245768 | tf_op jit(solution)/shard_map/ppermute | solution.py:206
  5.7 10.6 %collective-permute-start.2 = (f32[5,8,256]{2,1,0:T(8,128)}, f32[5,8,256]{2,1,0:T(8,128)S(1)}, u32[]{:S(2)}, u32[]{:S(2)}) collective-permute-start(f32[5,8,256]{2,1,0:T(8,128)} %get-tuple-element.20), channel_id=1, source_target_pairs={{0,1},{1,0},{2,3},{3,2},{4,5},{5,4},{6,7},{7,6},{8,9},{9,8},{10,11... | collective-permute-start | bytes 122888 | tf_op jit(solution)/shard_map/ppermute | solution.py:205
  6.8 9.4 %collective-permute-start.3 = (f32[5,8,256]{2,1,0:T(8,128)}, f32[5,8,256]{2,1,0:T(8,128)S(1)}, u32[]{:S(2)}, u32[]{:S(2)}) collective-permute-start(f32[5,8,256]{2,1,0:T(8,128)} %get-tuple-element.21), channel_id=1, source_target_pairs={{0,15},{1,2},{2,1},{3,4},{4,3},{5,6},{6,5},{7,8},{8,7},{9,10},{10,... | collective-permute-start | bytes 122888 | tf_op jit(solution)/shard_map/ppermute | solution.py:204
  16.2 0.6 copy-start.11
  16.3 0.7 copy-start.1
  19.9 5.7 %copy-start.13 = (s32[8,16]{1,0:T(8,128)S(1)}, s32[8,16]{1,0:T(8,128)}, u32[]{:S(2)}) copy-start(s32[8,16]{1,0:T(8,128)} %param.15) | copy-start | bytes 1540
  19.9 10.1 %collective-permute-start.4 = (f32[5,16,256]{2,1,0:T(8,128)}, f32[5,16,256]{2,1,0:T(8,128)S(1)}, u32[]{:S(2)}, u32[]{:S(2)}) collective-permute-start(f32[5,16,256]{2,1,0:T(8,128)} %get-tuple-element.23), channel_id=1, source_target_pairs={{0,16},{16,0},{32,48},{48,32},{64,80},{80,64},{96,112},{112,96},{1... | collective-permute-start | bytes 245768 | tf_op jit(solution)/shard_map/ppermute | solution.py:207
  22.2 7.7 %collective-permute-start.5 = (f32[5,16,256]{2,1,0:T(8,128)}, f32[5,16,256]{2,1,0:T(8,128)S(1)}, u32[]{:S(2)}, u32[]{:S(2)}) collective-permute-start(f32[5,16,256]{2,1,0:T(8,128)} %get-tuple-element.24), channel_id=1, source_target_pairs={{0,112},{16,32},{32,16},{48,64},{64,48},{80,96},{96,80},{112,0},{1... | collective-permute-start | bytes 245768 | tf_op jit(solution)/shard_map/ppermute | solution.py:206
  22.2 7.7 %collective-permute-start.6 = (f32[5,8,256]{2,1,0:T(8,128)}, f32[5,8,256]{2,1,0:T(8,128)S(1)}, u32[]{:S(2)}, u32[]{:S(2)}) collective-permute-start(f32[5,8,256]{2,1,0:T(8,128)} %get-tuple-element.25), channel_id=1, source_target_pairs={{0,1},{1,0},{2,3},{3,2},{4,5},{5,4},{6,7},{7,6},{8,9},{9,8},{10,11... | collective-permute-start | bytes 122888 | tf_op jit(solution)/shard_map/ppermute | solution.py:205
  22.3 7.7 %collective-permute-start.7 = (f32[5,8,256]{2,1,0:T(8,128)}, f32[5,8,256]{2,1,0:T(8,128)S(1)}, u32[]{:S(2)}, u32[]{:S(2)}) collective-permute-start(f32[5,8,256]{2,1,0:T(8,128)} %get-tuple-element.26), channel_id=1, source_target_pairs={{0,15},{1,2},{2,1},{3,4},{4,3},{5,6},{6,5},{7,8},{8,7},{9,10},{10,... | collective-permute-start | bytes 122888 | tf_op jit(solution)/shard_map/ppermute | solution.py:204
  30.0 0.6 copy-start.2
  33.6 22.4 %copy-start.14 = (f32[5,8,256]{2,1,0:T(8,128)S(1)}, f32[5,8,256]{2,1,0:T(8,128)}, u32[]{:S(2)}) copy-start(f32[5,8,256]{2,1,0:T(8,128)} %get-tuple-element.31) | copy-start | bytes 122884
  45.6 2.5 %collective-permute-start.12 = (f32[1,128]{1,0:T(1,128)S(1)}, f32[1,128]{1,0:T(1,128)S(1)}, u32[]{:S(2)}, u32[]{:S(2)}) collective-permute-start(f32[1,128]{1,0:T(1,128)S(1)} %bitcast.21), channel_id=1, source_target_pairs={{0,1},{1,0},{2,3},{3,2},{128,129},{129,128},{130,131},{131,130},{4... | collective-permute-start | bytes 1544 | tf_op jit(solution)/shard_map/ppermute | solution.py:258
  48.1 5.5 %collective-permute-start.13 = (f32[1,128]{1,0:T(1,128)S(1)}, f32[1,128]{1,0:T(1,128)S(1)}, u32[]{:S(2)}, u32[]{:S(2)}) collective-permute-start(f32[1,128]{1,0:T(1,128)S(1)} %bitcast_add_fusion), channel_id=1, source_target_pairs={{0,131},{1,2},{2,1},{3,128},{128,3},{129,130},{130,129},{131,0},{4... | collective-permute-start | bytes 1544 | tf_op jit(solution)/shard_map/ppermute | solution.py:259
  53.7 11.8 %collective-permute-start.14 = (f32[1,128]{1,0:T(1,128)S(1)}, f32[1,128]{1,0:T(1,128)S(1)}, u32[]{:S(2)}, u32[]{:S(2)}) collective-permute-start(f32[1,128]{1,0:T(1,128)S(1)} %add.13), channel_id=1, source_target_pairs={{0,3},{3,0},{1,130},{130,1},{2,129},{129,2},{128,131},{131,128},{4... | collective-permute-start | bytes 1544 | tf_op jit(solution)/shard_map/ppermute | solution.py:260
  54.5 11.6 %collective-permute-start.10 = (f32[5,8,256]{2,1,0:T(8,128)}, f32[5,8,256]{2,1,0:T(8,128)S(1)}, u32[]{:S(2)}, u32[]{:S(2)}) collective-permute-start(f32[5,8,256]{2,1,0:T(8,128)} %get-tuple-element.30), channel_id=1, source_target_pairs={{0,1},{1,0},{2,3},{3,2},{4,5},{5,4},{6,7},{7,6},{8,9},{9,8},{10,11... | collective-permute-start | bytes 122888 | tf_op jit(solution)/shard_map/ppermute | solution.py:205
  56.0 10.0 %collective-permute-start.11 = (f32[5,8,256]{2,1,0:T(8,128)S(1)}, f32[5,8,256]{2,1,0:T(8,128)S(1)}, u32[]{:S(2)}, u32[]{:S(2)}) collective-permute-start(f32[5,8,256]{2,1,0:T(8,128)S(1)} %copy-done.14), channel_id=1, source_target_pairs={{0,15},{1,2},{2,1},{3,4},{4,3},{5,6},{6,5},{7,8},{8,7},{9,10},{10,... | collective-permute-start | bytes 122888 | tf_op jit(solution)/shard_map/ppermute | solution.py:204
  57.6 8.5 %collective-permute-start.8 = (f32[5,16,256]{2,1,0:T(8,128)}, f32[5,16,256]{2,1,0:T(8,128)S(1)}, u32[]{:S(2)}, u32[]{:S(2)}) collective-permute-start(f32[5,16,256]{2,1,0:T(8,128)} %get-tuple-element.28), channel_id=1, source_target_pairs={{0,16},{16,0},{32,48},{48,32},{64,80},{80,64},{96,112},{112,96},{1... | collective-permute-start | bytes 245768 | tf_op jit(solution)/shard_map/ppermute | solution.py:207
  61.5 4.6 %collective-permute-start.9 = (f32[5,16,256]{2,1,0:T(8,128)}, f32[5,16,256]{2,1,0:T(8,128)S(1)}, u32[]{:S(2)}, u32[]{:S(2)}) collective-permute-start(f32[5,16,256]{2,1,0:T(8,128)} %get-tuple-element.29), channel_id=1, source_target_pairs={{0,112},{16,32},{32,16},{48,64},{64,48},{80,96},{96,80},{112,0},{1... | collective-permute-start | bytes 245768 | tf_op jit(solution)/shard_map/ppermute | solution.py:206
  66.1 0.6 copy-start.7
  66.1 0.6 copy-start.3
  66.7 0.6 copy-start.5
  (6 other events, 3.7 us)

commit v2 on v1

--- a/solution.py
+++ b/solution.py
@@ -1,5 +1,3 @@
-import functools
-
 import jax
 import jax.numpy as jnp
 from jax import lax
@@ -8,6 +6,7 @@
 from jax.sharding import Mesh
 from jax.sharding import PartitionSpec as P
 
+
 NDES = 4096
 GX = ("gx_0", "gx_1")
 YZ = ("yz_0", "yz_1")
@@ -22,6 +21,19 @@
 
 def f32(*shape):
     return jax.ShapeDtypeStruct(shape, jnp.float32)
+
+
+def kept(*shape):
+    return pltpu.VMEM(shape, jnp.float32)
+
+
+def near_core(x):
+    return pltpu.with_memory_space_constraint(x, pltpu.VMEM)
+
+
+def call(kernel, **options):
+    params = pltpu.CompilerParams(vmem_limit_bytes=8 * 2**20)
+    return pl.pallas_call(kernel, compiler_params=params, **options)
 
 
 def position():
@@ -67,7 +79,7 @@
         shifted[5] = jnp.where(lane == 0, 0.0, pltpu.roll(centre, 1, 1))
         for d, values in shifted.items():
             for k in range(nvar):
-                term = blocks_ref[0, d, e, k] * values
+                term = blocks_ref[e, k, 0, d] * values
                 sums[k] = term if sums[k] is None else sums[k] + term
     return sums
 
@@ -104,7 +116,7 @@
         for e in range(nvar):
             values = pick(e)
             for k in range(nvar):
-                term = blocks_ref[0, direction, e, k] * values
+                term = blocks_ref[e, k, 0, direction] * values
                 sums[k] = term if sums[k] is None else sums[k] + term
         return sums
 
@@ -173,7 +185,15 @@
     pairs = NDES // band
     wanted = lax.broadcasted_iota(jnp.int32, (2 * pairs, patches), 0)
     wanted = jnp.where(wanted < pairs, 2 * wanted, 2 * (wanted - pairs) + 1)
-    onehot = (wanted == slot_ref[...]).astype(jnp.float32)
+    lane = lax.broadcasted_iota(jnp.int32, (ny, patches), 1)
+    repeat = lax.rem(lane, ny) == lax.broadcasted_iota(jnp.int32, (ny, patches), 0)
+    slots = jnp.dot(
+        slot_ref[...].astype(jnp.float32), repeat.astype(jnp.float32), preferred_element_type=jnp.float32
+    )
+    lane = lax.broadcasted_iota(jnp.int32, (nx, patches), 1)
+    own = lax.div(lane, ny) == lax.broadcasted_iota(jnp.int32, (nx, patches), 0)
+    slots = jnp.sum(jnp.where(own, slots, 0.0), axis=0, keepdims=True)
+    onehot = (wanted.astype(jnp.float32) == slots).astype(jnp.float32)
     by_slot = jnp.dot(onehot, projected, precision=HIGHEST, preferred_element_type=jnp.float32)
     even, odd = by_slot[:pairs], pltpu.roll(by_slot[pairs:], half, 1)
     row = lax.broadcasted_iota(jnp.int32, (pairs, band), 0)
@@ -205,10 +225,10 @@
     near = lax.ppermute(ya, YZ, swap_a(16))
     chip = lax.ppermute(xb, GX, swap_b(8))
     core = lax.ppermute(xa, GX, swap_a(8))
-    return core, chip, near, far
-
-
-def local(
+    return tuple(near_core(x) for x in (core, chip, near, far))
+
+
+def step(
     adjoint,
     objective_gradient,
     diagonal,
@@ -219,53 +239,64 @@
     design_basis,
     condition_weights,
 ):
-    v, source, sensitivity = adjoint[0], objective_gradient[0], flux_sensitivity[0]
+    v, source = near_core(adjoint[0]), near_core(objective_gradient[0])
+    sensitivity, mask = near_core(flux_sensitivity[0]), near_core(surface_mask)
+    diagonal, basis = near_core(diagonal), near_core(design_basis)
+    blocks = flux_blocks.transpose(2, 3, 0, 1)
     nvar, nx, ny, nz = v.shape
-    field = f32(nvar, nx, ny, nz)
-    sides = (f32(nvar, ny, nz), f32(nvar, ny, nz), f32(nvar, nx, nz), f32(nvar, nx, nz))
-    slot = patch_band_slot.reshape(1, -1)
-
-    first = pl.pallas_call(
+    field = kept(nvar, nx, ny, nz)
+    sides = (kept(nvar, ny, nz), kept(nvar, ny, nz), kept(nvar, nx, nz), kept(nvar, nx, nz))
+
+    first = call(
         sides_kernel, out_shape=sides, in_specs=[VMEM], out_specs=[VMEM] * 4, name="sides"
     )(v)
     halo = exchange(*first)
-    inner_sweep = pl.pallas_call(
+    inner_sweep = call(
         inner_sweep_kernel, out_shape=field, in_specs=[SMEM] + [VMEM] * 3, out_specs=VMEM, name="inner_sweep"
     )
-    inner = inner_sweep(flux_blocks, v, source, diagonal)
-    relaxed, *second = pl.pallas_call(
+    inner = inner_sweep(blocks, v, source, diagonal)
+    relaxed, *second = call(
         outer_sweep_kernel,
         out_shape=(field, *sides),
         in_specs=[SMEM] + [VMEM] * 6,
         out_specs=[VMEM] * 5,
         name="outer_sweep",
-    )(flux_blocks, inner, diagonal, *halo)
+    )(blocks, near_core(inner), diagonal, *halo)
 
     halo = exchange(*second)
-    inner = inner_sweep(flux_blocks, relaxed, source, diagonal)
-    smoothed, xa, xb, ya, yb, gradient = pl.pallas_call(
+    inner = inner_sweep(blocks, near_core(relaxed), source, diagonal)
+    smoothed, xa, xb, ya, yb, gradient = call(
         last_sweep_kernel,
-        out_shape=(field, *sides, f32(NDES // 128, 128)),
+        out_shape=(field, *sides, kept(NDES // 128, 128)),
         in_specs=[SMEM, SMEM] + [VMEM] * 10,
         out_specs=[VMEM] * 6,
         scratch_shapes=[pltpu.VMEM((nx * ny, nz), jnp.float32)],
         name="last_sweep",
-    )(flux_blocks, condition_weights, inner, diagonal, *halo, sensitivity, surface_mask, slot, design_basis)
-
-    halo = exchange(xa, xb, ya, yb)
+    )(blocks, condition_weights, near_core(inner), diagonal, *halo, sensitivity, mask, near_core(patch_band_slot), basis)
+
     parts = lax.all_to_all(gradient, SPREAD, 0, 0, tiled=True)
     total = jnp.sum(parts, axis=0, keepdims=True)
     total = total + lax.ppermute(total, RING, [(i, i ^ 1) for i in range(8)])
+    halo = exchange(xa, xb, ya, yb)
     total = total + lax.ppermute(total, RING, [(i, (((i + 1) ^ 1) - 1) % 8) for i in range(8)])
-    total = total + lax.ppermute(total, RING, [(0, 3), (3, 0), (1, 6), (6, 1), (2, 5), (5, 2), (4, 7), (7, 4)])
+    across = [(0, 3), (3, 0), (1, 6), (6, 1), (2, 5), (5, 2), (4, 7), (7, 4)]
+    total = total + lax.ppermute(total, RING, across)
     design_gradient = lax.dynamic_slice(total, (0, lax.axis_index("yz_1") * 32), (1, 32))[0]
 
-    inner = pl.pallas_call(
-        inner_residual_kernel, out_shape=field, in_specs=[SMEM] + [VMEM] * 3, out_specs=VMEM, name="inner_residual"
-    )(flux_blocks, smoothed, source, diagonal)
-    residual = pl.pallas_call(
-        outer_residual_kernel, out_shape=field, in_specs=[SMEM] + [VMEM] * 5, out_specs=VMEM, name="outer_residual"
-    )(flux_blocks, inner, *halo)
+    inner = call(
+        inner_residual_kernel,
+        out_shape=field,
+        in_specs=[SMEM] + [VMEM] * 3,
+        out_specs=VMEM,
+        name="inner_residual",
+    )(blocks, near_core(smoothed), source, diagonal)
+    residual = call(
+        outer_residual_kernel,
+        out_shape=f32(nvar, nx, ny, nz),
+        in_specs=[SMEM] + [VMEM] * 5,
+        out_specs=VMEM,
+        name="outer_residual",
+    )(blocks, near_core(inner), *halo)
     return smoothed[None], residual[None], design_gradient
 
 
@@ -286,4 +317,4 @@
         P(),
     )
     out_specs = (P("cond", None, GX, YZ, None), P("cond", None, GX, YZ, None), P(GX + YZ))
-    return jax.shard_map(local, mesh=torus, in_specs=in_specs, out_specs=out_specs, check_vma=False)
+    return jax.shard_map(step, mesh=torus, in_specs=in_specs, out_specs=out_specs, check_vma=False)

time: 69.9 us -> 61.3 us (0.88)
  Pallas kernels: 20.7 us -> 11.8 us
  waiting for transfers between devices: 3.2 us -> 4.66 us
    pallas_call x7, Pallas kernels: 20.7 us -> 11.8 us  [the longest x1 2.4 us: step(): inner = inner_sweep(blocks, near_core(relaxed), source, diagonal)]
    ppermute x3, starting transfers between devices: 9.77 us -> 11.4 us  [exchange(): far = lax.ppermute(yb, YZ, swap_b(16))]
    ppermute x3, starting transfers between devices: 2.66 us -> 1.21 us  [exchange(): near = lax.ppermute(ya, YZ, swap_a(16))]
    ppermute x3, waiting for transfers between devices: 0.01 us -> 1.14 us  [exchange(): far = lax.ppermute(yb, YZ, swap_b(16))]
    unnamed x31 -> x23, local copies, waits for them, and re-layouts: 3.91 us -> 4.01 us
  transfers between devices with their start and end apart: 15 -> 15, of which waited for: 2 -> 4; matrix products, arithmetic and copies ran while one was open for 3% -> 2% of each run, Pallas kernels for 16% -> 12%
where the time goes in v2:
time: 61.3 us; the launch traced here: 61.1 us
  starting transfers between devices  27.5 us (45%)
  Pallas kernels  11.8 us (19%)
  blocking collectives  11.7 us (19%)
  waiting for transfers between devices  4.66 us (8%)
  local copies, waits for them, and re-layouts  4.59 us (7%)
  between operations  0.81 us (1%)
    all_to_all x1, blocking collectives, step(): parts = lax.all_to_all(gradient, SPREAD, 0, 0, tiled=True)  11.7 us
    ppermute x3, starting transfers between devices, exchange(): far = lax.ppermute(yb, YZ, swap_b(16))  11.4 us
    ppermute x3, starting transfers between devices, exchange(): core = lax.ppermute(xa, GX, swap_a(8))  8.92 us
    ppermute x1, starting transfers between devices, step(): lax.ppermute(total, RING, [(i, ((i + 1 ^ 1) - 1) % 8) for i in range(8)])  5.1 us
    unnamed x23, local copies, waits for them, and re-layouts  4.01 us
    ppermute x1, waiting for transfers between devices, step(): total = total + lax.ppermute(total, RING, [(i, i ^ 1) for i in range(8)])  2.4 us
    pallas_call x1, Pallas kernels, step(): inner = inner_sweep(blocks, near_core(relaxed), source, diagonal)  2.4 us
    pallas_call x1, Pallas kernels, step(): inner = inner_sweep(blocks, v, source, diagonal)  2.4 us
  transfers between devices with their start and end apart: 15, of which 4 were waited for; matrix products, arithmetic and copies ran while one was open for 2% of the time, Pallas kernels for 12%

profile of v2, /device:TPU:1, one launch (start us, length us, event | category | flops | bytes accessed | tf_op | source)
XLA Modules:
  0.0 61.1 jit_solution(963727548590107924)
XLA Ops:
  0.7 1.1 %copy-done.3 = f32[1,5,8,16,256]{4,3,2,1,0:T(8,128)S(1)} copy-done((f32[1,5,8,16,256]{4,3,2,1,0:T(8,128)S(1)}, f32[1,5,8,16,256]{4,3,2,1,0:T(8,128)}, u32[]{:S(2)}) %copy-start.3) | copy-done | bytes 655384
  1.9 3.3 %collective-permute-start = (f32[5,16,256]{2,1,0:T(8,128)S(1)}, f32[5,16,256]{2,1,0:T(8,128)S(1)}, u32[]{:S(2)}, u32[]{:S(2)}) collective-permute-start(f32[5,16,256]{2,1,0:T(8,128)S(1)} %get-tuple-element.18), channel_id=1, source_target_pairs={{0,16},{16,0},{32,48},{48,32},{64,80},{80,64},{96,112},{112,96},{1... | collective-permute-start | bytes 245768 | tf_op jit(solution)/shard_map/ppermute | solution.py:227
  5.2 1.2 %collective-permute-start.2 = (f32[5,8,256]{2,1,0:T(8,128)S(1)}, f32[5,8,256]{2,1,0:T(8,128)S(1)}, u32[]{:S(2)}, u32[]{:S(2)}) collective-permute-start(f32[5,8,256]{2,1,0:T(8,128)S(1)} %get-tuple-element.20), channel_id=1, source_target_pairs={{0,1},{1,0},{2,3},{3,2},{4,5},{5,4},{6,7},{7,6},{8,9},{9,8},{10,11... | collective-permute-start | bytes 122888 | tf_op jit(solution)/shard_map/ppermute | solution.py:225
  6.4 4.9 %collective-permute-start.3 = (f32[5,8,256]{2,1,0:T(8,128)S(1)}, f32[5,8,256]{2,1,0:T(8,128)S(1)}, u32[]{:S(2)}, u32[]{:S(2)}) collective-permute-start(f32[5,8,256]{2,1,0:T(8,128)S(1)} %get-tuple-element.21), channel_id=1, source_target_pairs={{0,15},{1,2},{2,1},{3,4},{4,3},{5,6},{6,5},{7,8},{8,7},{9,10},{10,... | collective-permute-start | bytes 122888 | tf_op jit(solution)/shard_map/ppermute | solution.py:224
  11.3 0.9 %copy-done.1 = f32[8,16,256]{2,1,0:T(8,128)S(1)} copy-done((f32[8,16,256]{2,1,0:T(8,128)S(1)}, f32[8,16,256]{2,1,0:T(8,128)}, u32[]{:S(2)}) %copy-start.1) | copy-done | bytes 131096
  12.2 1.1 %copy-done.4 = f32[1,5,8,16,256]{4,3,2,1,0:T(8,128)S(1)} copy-done((f32[1,5,8,16,256]{4,3,2,1,0:T(8,128)S(1)}, f32[1,5,8,16,256]{4,3,2,1,0:T(8,128)}, u32[]{:S(2)}) %copy-start.4) | copy-done | bytes 655384
  13.3 2.4 %inner_sweep.2.inner_ref = f32[5,8,16,256]{3,2,1,0:T(8,128)S(1)} custom-call(f32[5,5,1,6]{3,2,1,0:T(1,128)S(1)} %bitcast.19, f32[5,8,16,256]{3,2,1,0:T(8,128)S(1)} %bitcast.18, f32[5,8,16,256]{3,2,1,0:T(8,128)S(1)} %bitcast.14, f32[8,16,256]{2,1,0:T(8,128)S(1)} %copy-done.1), custom_call_target="tpu_custom_call" | custom-call | tf_op jit(solution)/shard_map/inner_sweep/pallas_call | solution.py:257
  15.8 1.1 %outer_sweep.1 = (f32[5,8,16,256]{3,2,1,0:T(8,128)S(1)}, f32[5,16,256]{2,1,0:T(8,128)S(1)}, f32[5,16,256]{2,1,0:T(8,128)S(1)}, f32[5,8,256]{2,1,0:T(8,128)S(1)}, f32[5,8,256]{2,1,0:T(8,128)S(1)}) custom-call(f32[5,5,1,6]{3,2,1,0:T(1,128)S(1)} %bitcast.20, f32[5,8,16,256]{3,2,1,0:T(8,128)S(1)} %inner_sweep.2.inner_ref, f32[8,16,256]{2,1,0:T(8,128)S(1)} %copy-done.2, ...), custom_call_target="tpu_custom_call" | custom-call | tf_op jit(solution)/shard_map/outer_sweep/pallas_call | solution.py:258
  16.8 2.3 %collective-permute-start.4 = (f32[5,16,256]{2,1,0:T(8,128)S(1)}, f32[5,16,256]{2,1,0:T(8,128)S(1)}, u32[]{:S(2)}, u32[]{:S(2)}) collective-permute-start(f32[5,16,256]{2,1,0:T(8,128)S(1)} %get-tuple-element.23), channel_id=1, source_target_pairs={{0,16},{16,0},{32,48},{48,32},{64,80},{80,64},{96,112},{112,96},{1... | collective-permute-start | bytes 245768 | tf_op jit(solution)/shard_map/ppermute | solution.py:227
  19.2 3.2 %collective-permute-start.7 = (f32[5,8,256]{2,1,0:T(8,128)S(1)}, f32[5,8,256]{2,1,0:T(8,128)S(1)}, u32[]{:S(2)}, u32[]{:S(2)}) collective-permute-start(f32[5,8,256]{2,1,0:T(8,128)S(1)} %get-tuple-element.26), channel_id=1, source_target_pairs={{0,15},{1,2},{2,1},{3,4},{4,3},{5,6},{6,5},{7,8},{8,7},{9,10},{10,... | collective-permute-start | bytes 122888 | tf_op jit(solution)/shard_map/ppermute | solution.py:224
  22.4 2.4 %inner_sweep.3.inner_ref = f32[5,8,16,256]{3,2,1,0:T(8,128)S(1)} custom-call(f32[5,5,1,6]{3,2,1,0:T(1,128)S(1)} %bitcast.21, f32[5,8,16,256]{3,2,1,0:T(8,128)S(1)} %get-tuple-element.22.v_ref, f32[5,8,16,256]{3,2,1,0:T(8,128)S(1)} %bitcast.15, f32[8,16,256]{2,1,0:T(8,128)S(1)} %copy-done.2), custom_call_target="tpu_custom_call" | custom-call | tf_op jit(solution)/shard_map/inner_sweep/pallas_call | solution.py:267
  24.8 1.1 %collective-permute-done.7.yb_ref = f32[5,8,256]{2,1,0:T(8,128)S(1)} collective-permute-done((f32[5,8,256]{2,1,0:T(8,128)S(1)}, f32[5,8,256]{2,1,0:T(8,128)S(1)}, u32[]{:S(2)}, u32[]{:S(2)}) %collective-permute-start.7) | collective-permute-done | bytes 40992 | tf_op jit(solution)/shard_map/ppermute | solution.py:224
  26.0 1.7 %last_sweep.1 = (f32[5,8,16,256]{3,2,1,0:T(8,128)S(1)}, f32[5,16,256]{2,1,0:T(8,128)S(1)}, f32[5,16,256]{2,1,0:T(8,128)S(1)}, f32[5,8,256]{2,1,0:T(8,128)S(1)}, ...) custom-call(f32[5,5,1,6]{3,2,1,0:T(1,128)S(1)} %bitcast.22, s32[2]{0:T(128)S(1)} %copy-done.10, ...), custom_call_target="tpu_custom_call" | custom-call | tf_op jit(solution)/shard_map/last_sweep/pallas_call | solution.py:268
  27.7 11.7 %all_to_all.9 = f32[32,1,128]{2,1,0:T(1,128)S(1)} all-to-all(f32[32,1,128]{2,1,0:T(1,128)S(1)} %bitcast.26), channel_id=1, replica_groups=mesh['cond'=2,'gx_0'=4,'gx_1'=2,'yz_0'=4,'yz_1'=4] {'gx_0','gx_1','yz_0'}, dimensions={0} | all-to-all | bytes 32768 | tf_op jit(solution)/shard_map/all_to_all | solution.py:277
  39.6 2.4 %collective-permute-done.12 = f32[1,128]{1,0:T(1,128)S(1)} collective-permute-done((f32[1,128]{1,0:T(1,128)S(1)}, f32[1,128]{1,0:T(1,128)S(1)}, u32[]{:S(2)}, u32[]{:S(2)}) %collective-permute-start.12) | collective-permute-done | bytes 544 | tf_op jit(solution)/shard_map/ppermute | solution.py:279
  42.0 5.1 %collective-permute-start.13 = (f32[1,128]{1,0:T(1,128)S(1)}, f32[1,128]{1,0:T(1,128)S(1)}, u32[]{:S(2)}, u32[]{:S(2)}) collective-permute-start(f32[1,128]{1,0:T(1,128)S(1)} %bitcast_add_fusion), channel_id=1, source_target_pairs={{0,131},{1,2},{2,1},{3,128},{128,3},{129,130},{130,129},{131,0},{4... | collective-permute-start | bytes 1544 | tf_op jit(solution)/shard_map/ppermute | solution.py:281
  47.1 1.0 %collective-permute-done.13 = f32[1,128]{1,0:T(1,128)S(1)} collective-permute-done((f32[1,128]{1,0:T(1,128)S(1)}, f32[1,128]{1,0:T(1,128)S(1)}, u32[]{:S(2)}, u32[]{:S(2)}) %collective-permute-start.13) | collective-permute-done | bytes 544 | tf_op jit(solution)/shard_map/ppermute | solution.py:281
  48.0 0.5 collective-permute-start.14
  48.6 3.3 %collective-permute-start.11 = (f32[5,8,256]{2,1,0:T(8,128)S(1)}, f32[5,8,256]{2,1,0:T(8,128)S(1)}, u32[]{:S(2)}, u32[]{:S(2)}) collective-permute-start(f32[5,8,256]{2,1,0:T(8,128)S(1)} %get-tuple-element.31), channel_id=1, source_target_pairs={{0,15},{1,2},{2,1},{3,4},{4,3},{5,6},{6,5},{7,8},{8,7},{9,10},{10,... | collective-permute-start | bytes 122888 | tf_op jit(solution)/shard_map/ppermute | solution.py:224
  51.9 3.3 %collective-permute-start.8 = (f32[5,16,256]{2,1,0:T(8,128)S(1)}, f32[5,16,256]{2,1,0:T(8,128)S(1)}, u32[]{:S(2)}, u32[]{:S(2)}) collective-permute-start(f32[5,16,256]{2,1,0:T(8,128)S(1)} %get-tuple-element.28), channel_id=1, source_target_pairs={{0,16},{16,0},{32,48},{48,32},{64,80},{80,64},{96,112},{112,96},{1... | collective-permute-start | bytes 245768 | tf_op jit(solution)/shard_map/ppermute | solution.py:227
  55.4 2.4 %inner_residual.1.inner_ref = f32[5,8,16,256]{3,2,1,0:T(8,128)S(1)} custom-call(f32[5,5,1,6]{3,2,1,0:T(1,128)S(1)} %bitcast.23, f32[5,8,16,256]{3,2,1,0:T(8,128)S(1)} %get-tuple-element.27.v_ref, f32[5,8,16,256]{3,2,1,0:T(8,128)S(1)} %bitcast.16, f32[8,16,256]{2,1,0:T(8,128)S(1)} %copy-done.2), custom_call_target="tpu_custom_call" | custom-call | tf_op jit(solution)/shard_map/inner_residual/pallas_call | solution.py:286
  57.8 0.8 %copy.13 = f32[1,5,8,16,256]{4,3,2,1,0:T(8,128)} copy(f32[1,5,8,16,256]{4,3,2,1,0:T(8,128)S(1)} %bitcast.13) | data formatting | bytes 1310720
  58.6 0.6 dynamic-slice_bitcast_fusion
  59.3 1.8 %outer_residual.1 = f32[5,8,16,256]{3,2,1,0:T(8,128)} custom-call(f32[5,5,1,6]{3,2,1,0:T(1,128)S(1)} %bitcast.24, f32[5,8,16,256]{3,2,1,0:T(8,128)S(1)} %inner_residual.1.inner_ref, f32[5,16,256]{2,1,0:T(8,128)S(1)} %collective-permute-done.8.xa_ref, f32[5,16,256]{2,1,0:T(8,128)S(1)} %collective-permute-done.9.xb_ref, ...), custom_call_target="tpu_custom_call" | custom-call | tf_op jit(solution)/shard_map/outer_residual/pallas_call | solution.py:293
  (42 shorter events, 0.7 us)
Async XLA Ops:
  0.6 10.7 %copy-start = (f32[1,5,8,16,256]{4,3,2,1,0:T(8,128)S(1)}, f32[1,5,8,16,256]{4,3,2,1,0:T(8,128)}, u32[]{:S(2)}) copy-start(f32[1,5,8,16,256]{4,3,2,1,0:T(8,128)} %param.10) | copy-start | bytes 1966084
  0.6 1.2 %copy-start.3 = (f32[1,5,8,16,256]{4,3,2,1,0:T(8,128)S(1)}, f32[1,5,8,16,256]{4,3,2,1,0:T(8,128)}, u32[]{:S(2)}) copy-start(f32[1,5,8,16,256]{4,3,2,1,0:T(8,128)} %param.9) | copy-start | bytes 1966084
  1.8 9.5 %copy-start.5 = (f32[1,6,5,5]{1,0,3,2:T(1,128)S(1)}, f32[1,6,5,5]{1,0,3,2:T(1,128)}, u32[]{:S(2)}) copy-start(f32[1,6,5,5]{1,0,3,2:T(1,128)} %param.12) | copy-start | bytes 1804
  1.9 13.8 %collective-permute-start = (f32[5,16,256]{2,1,0:T(8,128)S(1)}, f32[5,16,256]{2,1,0:T(8,128)S(1)}, u32[]{:S(2)}, u32[]{:S(2)}) collective-permute-start(f32[5,16,256]{2,1,0:T(8,128)S(1)} %get-tuple-element.18), channel_id=1, source_target_pairs={{0,16},{16,0},{32,48},{48,32},{64,80},{80,64},{96,112},{112,96},{1... | collective-permute-start | bytes 245768 | tf_op jit(solution)/shard_map/ppermute | solution.py:227
  5.2 10.6 %collective-permute-start.1 = (f32[5,16,256]{2,1,0:T(8,128)S(1)}, f32[5,16,256]{2,1,0:T(8,128)S(1)}, u32[]{:S(2)}, u32[]{:S(2)}) collective-permute-start(f32[5,16,256]{2,1,0:T(8,128)S(1)} %get-tuple-element.19), channel_id=1, source_target_pairs={{0,112},{16,32},{32,16},{48,64},{64,48},{80,96},{96,80},{112,0},{1... | collective-permute-start | bytes 245768 | tf_op jit(solution)/shard_map/ppermute | solution.py:226
  5.2 10.5 %collective-permute-start.2 = (f32[5,8,256]{2,1,0:T(8,128)S(1)}, f32[5,8,256]{2,1,0:T(8,128)S(1)}, u32[]{:S(2)}, u32[]{:S(2)}) collective-permute-start(f32[5,8,256]{2,1,0:T(8,128)S(1)} %get-tuple-element.20), channel_id=1, source_target_pairs={{0,1},{1,0},{2,3},{3,2},{4,5},{5,4},{6,7},{7,6},{8,9},{9,8},{10,11... | collective-permute-start | bytes 122888 | tf_op jit(solution)/shard_map/ppermute | solution.py:225
  6.4 9.3 %collective-permute-start.3 = (f32[5,8,256]{2,1,0:T(8,128)S(1)}, f32[5,8,256]{2,1,0:T(8,128)S(1)}, u32[]{:S(2)}, u32[]{:S(2)}) collective-permute-start(f32[5,8,256]{2,1,0:T(8,128)S(1)} %get-tuple-element.21), channel_id=1, source_target_pairs={{0,15},{1,2},{2,1},{3,4},{4,3},{5,6},{6,5},{7,8},{8,7},{9,10},{10,... | collective-permute-start | bytes 122888 | tf_op jit(solution)/shard_map/ppermute | solution.py:224
  13.3 2.5 %copy-start.2 = (f32[8,16,256]{2,1,0:T(8,128)S(1)}, f32[8,16,256]{2,1,0:T(8,128)}, u32[]{:S(2)}) copy-start(f32[8,16,256]{2,1,0:T(8,128)} %diagonal_ref.9) | copy-start | bytes 393220
  16.8 9.1 %collective-permute-start.4 = (f32[5,16,256]{2,1,0:T(8,128)S(1)}, f32[5,16,256]{2,1,0:T(8,128)S(1)}, u32[]{:S(2)}, u32[]{:S(2)}) collective-permute-start(f32[5,16,256]{2,1,0:T(8,128)S(1)} %get-tuple-element.23), channel_id=1, source_target_pairs={{0,16},{16,0},{32,48},{48,32},{64,80},{80,64},{96,112},{112,96},{1... | collective-permute-start | bytes 245768 | tf_op jit(solution)/shard_map/ppermute | solution.py:227
  19.2 6.8 %collective-permute-start.5 = (f32[5,16,256]{2,1,0:T(8,128)S(1)}, f32[5,16,256]{2,1,0:T(8,128)S(1)}, u32[]{:S(2)}, u32[]{:S(2)}) collective-permute-start(f32[5,16,256]{2,1,0:T(8,128)S(1)} %get-tuple-element.24), channel_id=1, source_target_pairs={{0,112},{16,32},{32,16},{48,64},{64,48},{80,96},{96,80},{112,0},{1... | collective-permute-start | bytes 245768 | tf_op jit(solution)/shard_map/ppermute | solution.py:226
  19.2 5.6 %collective-permute-start.6 = (f32[5,8,256]{2,1,0:T(8,128)S(1)}, f32[5,8,256]{2,1,0:T(8,128)S(1)}, u32[]{:S(2)}, u32[]{:S(2)}) collective-permute-start(f32[5,8,256]{2,1,0:T(8,128)S(1)} %get-tuple-element.25), channel_id=1, source_target_pairs={{0,1},{1,0},{2,3},{3,2},{4,5},{5,4},{6,7},{7,6},{8,9},{9,8},{10,11... | collective-permute-start | bytes 122888 | tf_op jit(solution)/shard_map/ppermute | solution.py:225
  19.2 6.8 %collective-permute-start.7 = (f32[5,8,256]{2,1,0:T(8,128)S(1)}, f32[5,8,256]{2,1,0:T(8,128)S(1)}, u32[]{:S(2)}, u32[]{:S(2)}) collective-permute-start(f32[5,8,256]{2,1,0:T(8,128)S(1)} %get-tuple-element.26), channel_id=1, source_target_pairs={{0,15},{1,2},{2,1},{3,4},{4,3},{5,6},{6,5},{7,8},{8,7},{9,10},{10,... | collective-permute-start | bytes 122888 | tf_op jit(solution)/shard_map/ppermute | solution.py:224
  22.4 3.6 %copy-start.6 = (bf16[1,5,8,16,256]{4,3,2,1,0:T(8,128)(2,1)S(1)}, bf16[1,5,8,16,256]{4,3,2,1,0:T(8,128)(2,1)}, u32[]{:S(2)}) copy-start(bf16[1,5,8,16,256]{4,3,2,1,0:T(8,128)(2,1)} %param.13) | copy-start | bytes 983044
  22.4 3.6 %copy-start.7 = (s32[8,16,256]{2,1,0:T(8,128)S(1)}, s32[8,16,256]{2,1,0:T(8,128)}, u32[]{:S(2)}) copy-start(s32[8,16,256]{2,1,0:T(8,128)} %mask_ref.1) | copy-start | bytes 393220
  22.4 3.6 %copy-start.8 = (f32[256,128]{1,0:T(8,128)S(1)}, f32[256,128]{1,0:T(8,128)}, u32[]{:S(2)}) copy-start(f32[256,128]{1,0:T(8,128)} %basis_ref.1) | copy-start | bytes 393220
  22.4 3.6 %copy-start.9 = (s32[8,16]{1,0:T(8,128)S(1)}, s32[8,16]{1,0:T(8,128)}, u32[]{:S(2)}) copy-start(s32[8,16]{1,0:T(8,128)} %slot_ref.1) | copy-start | bytes 1540
  24.8 1.2 %copy-start.10 = (s32[2]{0:T(128)S(1)}, s32[2]{0:T(128)}, u32[]{:S(2)}) copy-start(s32[2]{0:T(128)} %weights_ref.1) | copy-start | bytes 28
  39.5 2.5 %collective-permute-start.12 = (f32[1,128]{1,0:T(1,128)S(1)}, f32[1,128]{1,0:T(1,128)S(1)}, u32[]{:S(2)}, u32[]{:S(2)}) collective-permute-start(f32[1,128]{1,0:T(1,128)S(1)} %bitcast.28), channel_id=1, source_target_pairs={{0,1},{1,0},{2,3},{3,2},{128,129},{129,128},{130,131},{131,130},{4... | collective-permute-start | bytes 1544 | tf_op jit(solution)/shard_map/ppermute | solution.py:279
  42.0 6.1 %collective-permute-start.13 = (f32[1,128]{1,0:T(1,128)S(1)}, f32[1,128]{1,0:T(1,128)S(1)}, u32[]{:S(2)}, u32[]{:S(2)}) collective-permute-start(f32[1,128]{1,0:T(1,128)S(1)} %bitcast_add_fusion), channel_id=1, source_target_pairs={{0,131},{1,2},{2,1},{3,128},{128,3},{129,130},{130,129},{131,0},{4... | collective-permute-start | bytes 1544 | tf_op jit(solution)/shard_map/ppermute | solution.py:281
  47.1 12.1 %collective-permute-start.10 = (f32[5,8,256]{2,1,0:T(8,128)S(1)}, f32[5,8,256]{2,1,0:T(8,128)S(1)}, u32[]{:S(2)}, u32[]{:S(2)}) collective-permute-start(f32[5,8,256]{2,1,0:T(8,128)S(1)} %get-tuple-element.30), channel_id=1, source_target_pairs={{0,1},{1,0},{2,3},{3,2},{4,5},{5,4},{6,7},{7,6},{8,9},{9,8},{10,11... | collective-permute-start | bytes 122888 | tf_op jit(solution)/shard_map/ppermute | solution.py:225
  48.0 10.6 %collective-permute-start.14 = (f32[1,128]{1,0:T(1,128)S(1)}, f32[1,128]{1,0:T(1,128)S(1)}, u32[]{:S(2)}, u32[]{:S(2)}) collective-permute-start(f32[1,128]{1,0:T(1,128)S(1)} %add.13), channel_id=1, source_target_pairs={{0,3},{3,0},{1,130},{130,1},{2,129},{129,2},{128,131},{131,128},{4... | collective-permute-start | bytes 1544 | tf_op jit(solution)/shard_map/ppermute | solution.py:283
  48.6 10.6 %collective-permute-start.11 = (f32[5,8,256]{2,1,0:T(8,128)S(1)}, f32[5,8,256]{2,1,0:T(8,128)S(1)}, u32[]{:S(2)}, u32[]{:S(2)}) collective-permute-start(f32[5,8,256]{2,1,0:T(8,128)S(1)} %get-tuple-element.31), channel_id=1, source_target_pairs={{0,15},{1,2},{2,1},{3,4},{4,3},{5,6},{6,5},{7,8},{8,7},{9,10},{10,... | collective-permute-start | bytes 122888 | tf_op jit(solution)/shard_map/ppermute | solution.py:224
  51.9 7.3 %collective-permute-start.8 = (f32[5,16,256]{2,1,0:T(8,128)S(1)}, f32[5,16,256]{2,1,0:T(8,128)S(1)}, u32[]{:S(2)}, u32[]{:S(2)}) collective-permute-start(f32[5,16,256]{2,1,0:T(8,128)S(1)} %get-tuple-element.28), channel_id=1, source_target_pairs={{0,16},{16,0},{32,48},{48,32},{64,80},{80,64},{96,112},{112,96},{1... | collective-permute-start | bytes 245768 | tf_op jit(solution)/shard_map/ppermute | solution.py:227
  55.2 4.2 %collective-permute-start.9 = (f32[5,16,256]{2,1,0:T(8,128)S(1)}, f32[5,16,256]{2,1,0:T(8,128)S(1)}, u32[]{:S(2)}, u32[]{:S(2)}) collective-permute-start(f32[5,16,256]{2,1,0:T(8,128)S(1)} %get-tuple-element.29), channel_id=1, source_target_pairs={{0,112},{16,32},{32,16},{48,64},{64,48},{80,96},{96,80},{112,0},{1... | collective-permute-start | bytes 245768 | tf_op jit(solution)/shard_map/ppermute | solution.py:226
  (2 other events, 2.0 us)

commit v3 on v2

--- a/solution.py
+++ b/solution.py
@@ -16,6 +16,7 @@
 HIGHEST = lax.Precision.HIGHEST
 
 VMEM = pl.BlockSpec(memory_space=pltpu.VMEM)
+HBM = pl.BlockSpec(memory_space=pltpu.HBM)
 SMEM = pl.BlockSpec(memory_space=pltpu.SMEM)
 
 
@@ -25,6 +26,10 @@
 
 def kept(*shape):
     return pltpu.VMEM(shape, jnp.float32)
+
+
+def far_from_core(x):
+    return pltpu.with_memory_space_constraint(x, pltpu.HBM)
 
 
 def near_core(x):
@@ -56,9 +61,48 @@
             yb_ref[k, x : x + 1, :] = jnp.where(yz_even, first, last)
 
 
-def sides_kernel(v_ref, xa_ref, xb_ref, ya_ref, yb_ref):
+def coefficient(table_ref, d, e, k, nvar, shape):
+    tile = table_ref[pl.ds((d * nvar + e) * nvar + k, 8, stride=0), :]
+    rows = jnp.concatenate([tile] * (shape[0] // 8), axis=0)
+    return jnp.concatenate([rows] * (shape[1] // 128), axis=1)
+
+
+def first_sides_kernel(v_hbm, v_ref, xa_ref, xb_ref, ya_ref, yb_ref, sem):
+    copy = pltpu.make_async_copy(v_hbm, v_ref, sem)
+    copy.start()
+    copy.wait()
     nvar, nx, ny, _ = v_ref.shape
     write_sides(lambda k, x: v_ref[k, x], nvar, nx, ny, xa_ref, xb_ref, ya_ref, yb_ref)
+
+
+def load_kernel(
+    blocks_hbm, weights_hbm, source_hbm, diagonal_hbm, source_ref, diagonal_ref, table_ref,
+    blocks_ref, weights_ref, sems,
+):
+    pairs = (
+        (blocks_hbm, blocks_ref),
+        (weights_hbm, weights_ref),
+        (source_hbm, source_ref),
+        (diagonal_hbm, diagonal_ref),
+    )
+    copies = [pltpu.make_async_copy(a, b, sems.at[i]) for i, (a, b) in enumerate(pairs)]
+    for copy in copies:
+        copy.start()
+    nvar = source_ref.shape[0]
+    for copy in copies[:2]:
+        copy.wait()
+    for d in range(6):
+        for e in range(nvar):
+            for k in range(nvar):
+                row = (d * nvar + e) * nvar + k
+                table_ref[row : row + 1, :] = jnp.full((1, 128), blocks_ref[e, k, 0, d])
+    mine = jnp.where(lax.axis_index("cond") == 0, weights_ref[0], weights_ref[1])
+    total = weights_ref[0].astype(jnp.float32) + weights_ref[1].astype(jnp.float32)
+    one = jnp.ones((1, 128), jnp.float32)
+    last = 6 * nvar * nvar
+    table_ref[last : last + 1, :] = (one * mine.astype(jnp.float32)) / (one * total)
+    for copy in copies[2:]:
+        copy.wait()
 
 
 def neighbour_sums(v_ref, blocks_ref, x):
@@ -79,7 +123,7 @@
         shifted[5] = jnp.where(lane == 0, 0.0, pltpu.roll(centre, 1, 1))
         for d, values in shifted.items():
             for k in range(nvar):
-                term = blocks_ref[e, k, 0, d] * values
+                term = coefficient(blocks_ref, d, e, k, nvar, values.shape) * values
                 sums[k] = term if sums[k] is None else sums[k] + term
     return sums
 
@@ -95,13 +139,16 @@
             out_ref[k, x] = value + scale * (source_ref[k, x] - diagonal * value + sums[k])
 
 
-def inner_residual_kernel(blocks_ref, v_ref, source_ref, diagonal_ref, out_ref):
+def inner_residual_kernel(blocks_ref, v_ref, source_ref, diagonal_ref, out_ref, v_hbm, sem):
+    copy = pltpu.make_async_copy(v_ref, v_hbm, sem)
+    copy.start()
     nvar, nx, _, _ = v_ref.shape
     for x in range(nx):
         sums = neighbour_sums(v_ref, blocks_ref, x)
         diagonal = diagonal_ref[x]
         for k in range(nvar):
             out_ref[k, x] = source_ref[k, x] - diagonal * v_ref[k, x] + sums[k]
+    copy.wait()
 
 
 def add_halo(blocks_ref, inner_ref, diagonal_ref, xa_ref, xb_ref, ya_ref, yb_ref, out_ref):
@@ -116,7 +163,7 @@
         for e in range(nvar):
             values = pick(e)
             for k in range(nvar):
-                term = blocks_ref[e, k, 0, direction] * values
+                term = coefficient(blocks_ref, direction, e, k, nvar, values.shape) * values
                 sums[k] = term if sums[k] is None else sums[k] + term
         return sums
 
@@ -163,7 +210,7 @@
 
 
 def last_sweep_kernel(
-    blocks_ref, weights_ref, inner_ref, diagonal_ref, xa_ref, xb_ref, ya_ref, yb_ref,
+    blocks_ref, inner_ref, diagonal_ref, xa_ref, xb_ref, ya_ref, yb_ref,
     sensitivity_ref, mask_ref, slot_ref, basis_ref,
     out_ref, next_xa_ref, next_xb_ref, next_ya_ref, next_yb_ref, gradient_ref, surface_ref,
 ):
@@ -200,16 +247,21 @@
     lane = lax.broadcasted_iota(jnp.int32, (pairs, band), 1)
     before = jnp.where(row == 0, 0.0, pltpu.roll(odd, 1, 0))
     gradient = even + jnp.where(lane < half, before, odd)
-    mine = jnp.where(lax.axis_index("cond") == 0, weights_ref[0], weights_ref[1])
-    total = weights_ref[0].astype(jnp.float32) + weights_ref[1].astype(jnp.float32)
-    one = jnp.ones((pairs, band), jnp.float32)
-    gradient_ref[...] = gradient * ((one * mine.astype(jnp.float32)) / (one * total))
+    share = blocks_ref[pl.ds(6 * nvar * nvar, 8, stride=0), :]
+    gradient_ref[...] = gradient * jnp.concatenate([share] * (pairs // 8), axis=0)
 
 
 def outer_residual_kernel(
-    blocks_ref, inner_ref, xa_ref, xb_ref, ya_ref, yb_ref, out_ref,
+    blocks_ref, inner_ref, xa_ref, xb_ref, ya_ref, yb_ref, part_ref, other_ref, out_ref, piece_ref,
 ):
     add_halo(blocks_ref, inner_ref, None, xa_ref, xb_ref, ya_ref, yb_ref, out_ref)
+    size = piece_ref.shape[1]
+    total = part_ref[...] + other_ref[...]
+    which = lax.axis_index("yz_1")
+    piece = total[:, :size]
+    for i in range(1, total.shape[1] // size):
+        piece = jnp.where(which == i, total[:, i * size : (i + 1) * size], piece)
+    piece_ref[...] = piece
 
 
 def swap_a(n):
@@ -239,26 +291,44 @@
     design_basis,
     condition_weights,
 ):
-    v, source = near_core(adjoint[0]), near_core(objective_gradient[0])
     sensitivity, mask = near_core(flux_sensitivity[0]), near_core(surface_mask)
-    diagonal, basis = near_core(diagonal), near_core(design_basis)
-    blocks = flux_blocks.transpose(2, 3, 0, 1)
-    nvar, nx, ny, nz = v.shape
+    basis = near_core(design_basis)
+    _, nvar, nx, ny, nz = adjoint.shape
     field = kept(nvar, nx, ny, nz)
     sides = (kept(nvar, ny, nz), kept(nvar, ny, nz), kept(nvar, nx, nz), kept(nvar, nx, nz))
 
-    first = call(
-        sides_kernel, out_shape=sides, in_specs=[VMEM], out_specs=[VMEM] * 4, name="sides"
-    )(v)
+    v, *first = call(
+        first_sides_kernel,
+        out_shape=(field, *sides),
+        in_specs=[HBM],
+        out_specs=[VMEM] * 5,
+        scratch_shapes=[pltpu.SemaphoreType.DMA],
+        name="first_sides",
+    )(far_from_core(adjoint[0]))
+    v = near_core(v)
     halo = exchange(*first)
+    arrays = (flux_blocks.transpose(2, 3, 0, 1), condition_weights, objective_gradient[0], diagonal)
+    source, diagonal, table = call(
+        load_kernel,
+        out_shape=(field, kept(nx, ny, nz), kept(6 * nvar * nvar + 1, 128)),
+        in_specs=[HBM] * 4,
+        out_specs=[VMEM] * 3,
+        scratch_shapes=[
+            pltpu.SMEM((nvar, nvar, 1, 6), jnp.float32),
+            pltpu.SMEM(condition_weights.shape, jnp.int32),
+            pltpu.SemaphoreType.DMA((4,)),
+        ],
+        name="load",
+    )(*(far_from_core(x) for x in arrays))
+    source, diagonal, blocks = near_core(source), near_core(diagonal), near_core(table)
     inner_sweep = call(
-        inner_sweep_kernel, out_shape=field, in_specs=[SMEM] + [VMEM] * 3, out_specs=VMEM, name="inner_sweep"
+        inner_sweep_kernel, out_shape=field, in_specs=[VMEM] * 4, out_specs=VMEM, name="inner_sweep"
     )
     inner = inner_sweep(blocks, v, source, diagonal)
     relaxed, *second = call(
         outer_sweep_kernel,
         out_shape=(field, *sides),
-        in_specs=[SMEM] + [VMEM] * 6,
+        in_specs=[VMEM] * 7,
         out_specs=[VMEM] * 5,
         name="outer_sweep",
     )(blocks, near_core(inner), diagonal, *halo)
@@ -268,11 +338,11 @@
     smoothed, xa, xb, ya, yb, gradient = call(
         last_sweep_kernel,
         out_shape=(field, *sides, kept(NDES // 128, 128)),
-        in_specs=[SMEM, SMEM] + [VMEM] * 10,
+        in_specs=[VMEM] * 11,
         out_specs=[VMEM] * 6,
         scratch_shapes=[pltpu.VMEM((nx * ny, nz), jnp.float32)],
         name="last_sweep",
-    )(blocks, condition_weights, near_core(inner), diagonal, *halo, sensitivity, mask, near_core(patch_band_slot), basis)
+    )(blocks, near_core(inner), diagonal, *halo, sensitivity, mask, near_core(patch_band_slot), basis)
 
     parts = lax.all_to_all(gradient, SPREAD, 0, 0, tiled=True)
     total = jnp.sum(parts, axis=0, keepdims=True)
@@ -280,24 +350,24 @@
     halo = exchange(xa, xb, ya, yb)
     total = total + lax.ppermute(total, RING, [(i, (((i + 1) ^ 1) - 1) % 8) for i in range(8)])
     across = [(0, 3), (3, 0), (1, 6), (6, 1), (2, 5), (5, 2), (4, 7), (7, 4)]
-    total = total + lax.ppermute(total, RING, across)
-    design_gradient = lax.dynamic_slice(total, (0, lax.axis_index("yz_1") * 32), (1, 32))[0]
-
-    inner = call(
+    other = lax.ppermute(total, RING, across)
+
+    inner, smoothed = call(
         inner_residual_kernel,
-        out_shape=field,
-        in_specs=[SMEM] + [VMEM] * 3,
-        out_specs=VMEM,
+        out_shape=(field, pltpu.HBM((nvar, nx, ny, nz), jnp.float32)),
+        in_specs=[VMEM] * 4,
+        out_specs=[VMEM, HBM],
+        scratch_shapes=[pltpu.SemaphoreType.DMA],
         name="inner_residual",
     )(blocks, near_core(smoothed), source, diagonal)
-    residual = call(
+    residual, design_gradient = call(
         outer_residual_kernel,
-        out_shape=f32(nvar, nx, ny, nz),
-        in_specs=[SMEM] + [VMEM] * 5,
-        out_specs=VMEM,
+        out_shape=(f32(nvar, nx, ny, nz), f32(1, 32)),
+        in_specs=[VMEM] * 8,
+        out_specs=[VMEM] * 2,
         name="outer_residual",
-    )(blocks, near_core(inner), *halo)
-    return smoothed[None], residual[None], design_gradient
+    )(blocks, near_core(inner), *halo, near_core(total), near_core(other))
+    return smoothed[None], residual[None], design_gradient.reshape(-1)
 
 
 def solution(mesh):

time: 61.3 us -> 55.2 us (0.900)
  the two profiles are of different devices: /device:TPU:1 before, /device:TPU:2 now
where the time goes in v3:
time: 55.2 us; the launch traced here: 55 us
  starting transfers between devices  24.9 us (45%)
  blocking collectives  11.8 us (21%)
  Pallas kernels  9.43 us (17%)
  waiting for transfers between devices  8.02 us (15%)
  between operations  0.77 us (1%)
    all_to_all x1, blocking collectives, step(): parts = lax.all_to_all(gradient, SPREAD, 0, 0, tiled=True)  11.8 us
    ppermute x3, starting transfers between devices, exchange(): far = lax.ppermute(yb, YZ, swap_b(16))  11.3 us
    ppermute x3, starting transfers between devices, exchange(): chip = lax.ppermute(xb, GX, swap_b(8))  5.24 us
    ppermute x3, waiting for transfers between devices, exchange(): far = lax.ppermute(yb, YZ, swap_b(16))  3.61 us
    ppermute x3, starting transfers between devices, exchange(): near = lax.ppermute(ya, YZ, swap_a(16))  3.36 us
    ppermute x1, waiting for transfers between devices, step(): lax.ppermute(total, RING, [(i, ((i + 1 ^ 1) - 1) % 8) for i in range(8)])  3.29 us
    ppermute x1, starting transfers between devices, step(): other = lax.ppermute(total, RING, across)  2.72 us
    pallas_call x1, Pallas kernels, step(): inner = inner_sweep(blocks, near_core(relaxed), source, diagonal)  1.59 us
  transfers between devices with their start and end apart: 15, of which 4 were waited for; matrix products, arithmetic and copies ran while one was open for 0% of the time, Pallas kernels for 11%

profile of v3, /device:TPU:2, one launch (start us, length us, event | category | flops | bytes accessed | tf_op | source)
XLA Modules:
  0.0 55.0 jit_solution(15442241244520255214)
XLA Ops:
  0.6 1.2 %first_sides.1 = (f32[5,8,16,256]{3,2,1,0:T(8,128)S(1)}, f32[5,16,256]{2,1,0:T(8,128)S(1)}, f32[5,16,256]{2,1,0:T(8,128)S(1)}, f32[5,8,256]{2,1,0:T(8,128)S(1)}, f32[5,8,256]{2,1,0:T(8,128)S(1)}) custom-call(f32[5,8,16,256]{3,2,1,0:T(8,128)} %bitcast.14), custom_call_target="tpu_custom_call" | custom-call | tf_op jit(solution)/shard_map/first_sides/pallas_call | solution.py:300
  1.9 3.1 %collective-permute-start.1 = (f32[5,16,256]{2,1,0:T(8,128)S(1)}, f32[5,16,256]{2,1,0:T(8,128)S(1)}, u32[]{:S(2)}, u32[]{:S(2)}) collective-permute-start(f32[5,16,256]{2,1,0:T(8,128)S(1)} %get-tuple-element.31), channel_id=1, source_target_pairs={{0,112},{16,32},{32,16},{48,64},{64,48},{80,96},{96,80},{112,0},{1... | collective-permute-start | bytes 245768 | tf_op jit(solution)/shard_map/ppermute | solution.py:278
  5.1 1.9 %collective-permute-start.2 = (f32[5,8,256]{2,1,0:T(8,128)S(1)}, f32[5,8,256]{2,1,0:T(8,128)S(1)}, u32[]{:S(2)}, u32[]{:S(2)}) collective-permute-start(f32[5,8,256]{2,1,0:T(8,128)S(1)} %get-tuple-element.32), channel_id=1, source_target_pairs={{0,1},{1,0},{2,3},{3,2},{4,5},{5,4},{6,7},{7,6},{8,9},{9,8},{10,11... | collective-permute-start | bytes 122888 | tf_op jit(solution)/shard_map/ppermute | solution.py:277
  7.0 2.8 %collective-permute-start.3 = (f32[5,8,256]{2,1,0:T(8,128)S(1)}, f32[5,8,256]{2,1,0:T(8,128)S(1)}, u32[]{:S(2)}, u32[]{:S(2)}) collective-permute-start(f32[5,8,256]{2,1,0:T(8,128)S(1)} %get-tuple-element.33), channel_id=1, source_target_pairs={{0,15},{1,2},{2,1},{3,4},{4,3},{5,6},{6,5},{7,8},{8,7},{9,10},{10,... | collective-permute-start | bytes 122888 | tf_op jit(solution)/shard_map/ppermute | solution.py:276
  9.8 1.1 %load.1 = (f32[5,8,16,256]{3,2,1,0:T(8,128)S(1)}, f32[8,16,256]{2,1,0:T(8,128)S(1)}, f32[151,128]{1,0:T(8,128)S(1)}) custom-call(f32[5,5,1,6]{3,2,1,0:T(1,128)} %bitcast.16, s32[2]{0:T(128)} %weights_hbm.1, f32[5,8,16,256]{3,2,1,0:T(8,128)} %bitcast.15, f32[8,16,256]{2,1,0:T(8,128)} %diagonal_hbm.1), custom_call_target="tpu_custom_call" | custom-call | tf_op jit(solution)/shard_map/load/pallas_call | solution.py:311
  10.9 1.5 %inner_sweep.2.inner_ref = f32[5,8,16,256]{3,2,1,0:T(8,128)S(1)} custom-call(f32[151,128]{1,0:T(8,128)S(1)} %get-tuple-element.26.blocks_ref, f32[5,8,16,256]{3,2,1,0:T(8,128)S(1)} %get-tuple-element.27.v_ref, f32[5,8,16,256]{3,2,1,0:T(8,128)S(1)} %get-tuple-element.28.source_ref, f32[8,16,256]{2,1,0:T(8,128)S(1)} %get-tuple-element.29.diagonal_ref), custom_call_target="tpu_custom_call" | custom-call | tf_op jit(solution)/shard_map/inner_sweep/pallas_call | solution.py:327
  12.5 1.2 %collective-permute-done.3.yb_ref = f32[5,8,256]{2,1,0:T(8,128)S(1)} collective-permute-done((f32[5,8,256]{2,1,0:T(8,128)S(1)}, f32[5,8,256]{2,1,0:T(8,128)S(1)}, u32[]{:S(2)}, u32[]{:S(2)}) %collective-permute-start.3) | collective-permute-done | bytes 40992 | tf_op jit(solution)/shard_map/ppermute | solution.py:276
  13.7 0.3 outer_sweep.1
  14.1 0.8 %collective-permute-start.5 = (f32[5,16,256]{2,1,0:T(8,128)S(1)}, f32[5,16,256]{2,1,0:T(8,128)S(1)}, u32[]{:S(2)}, u32[]{:S(2)}) collective-permute-start(f32[5,16,256]{2,1,0:T(8,128)S(1)} %get-tuple-element.36), channel_id=1, source_target_pairs={{0,112},{16,32},{32,16},{48,64},{64,48},{80,96},{96,80},{112,0},{1... | collective-permute-start | bytes 245768 | tf_op jit(solution)/shard_map/ppermute | solution.py:278
  14.9 2.8 %collective-permute-start.7 = (f32[5,8,256]{2,1,0:T(8,128)S(1)}, f32[5,8,256]{2,1,0:T(8,128)S(1)}, u32[]{:S(2)}, u32[]{:S(2)}) collective-permute-start(f32[5,8,256]{2,1,0:T(8,128)S(1)} %get-tuple-element.38), channel_id=1, source_target_pairs={{0,15},{1,2},{2,1},{3,4},{4,3},{5,6},{6,5},{7,8},{8,7},{9,10},{10,... | collective-permute-start | bytes 122888 | tf_op jit(solution)/shard_map/ppermute | solution.py:276
  17.8 1.6 %inner_sweep.3.inner_ref = f32[5,8,16,256]{3,2,1,0:T(8,128)S(1)} custom-call(f32[151,128]{1,0:T(8,128)S(1)} %get-tuple-element.26.blocks_ref, f32[5,8,16,256]{3,2,1,0:T(8,128)S(1)} %get-tuple-element.34.v_ref, f32[5,8,16,256]{3,2,1,0:T(8,128)S(1)} %get-tuple-element.28.source_ref, f32[8,16,256]{2,1,0:T(8,128)S(1)} %get-tuple-element.29.diagonal_ref), custom_call_target="tpu_custom_call" | custom-call | tf_op jit(solution)/shard_map/inner_sweep/pallas_call | solution.py:337
  19.4 2.4 %collective-permute-done.7.yb_ref = f32[5,8,256]{2,1,0:T(8,128)S(1)} collective-permute-done((f32[5,8,256]{2,1,0:T(8,128)S(1)}, f32[5,8,256]{2,1,0:T(8,128)S(1)}, u32[]{:S(2)}, u32[]{:S(2)}) %collective-permute-start.7) | collective-permute-done | bytes 40992 | tf_op jit(solution)/shard_map/ppermute | solution.py:276
  21.8 0.9 %last_sweep.1 = (f32[5,8,16,256]{3,2,1,0:T(8,128)S(1)}, f32[5,16,256]{2,1,0:T(8,128)S(1)}, f32[5,16,256]{2,1,0:T(8,128)S(1)}, f32[5,8,256]{2,1,0:T(8,128)S(1)}, ...) custom-call(f32[151,128]{1,0:T(8,128)S(1)} %get-tuple-element.26.blocks_ref, f32[5,8,16,256]{3,2,1,0:T(8,128)S(1)} %inner_sweep.3.inner_ref, ...), custom_call_target="tpu_custom_call" | custom-call | tf_op jit(solution)/shard_map/last_sweep/pallas_call | solution.py:338
  22.7 11.8 %all_to_all.9 = f32[32,1,128]{2,1,0:T(1,128)S(1)} all-to-all(f32[32,1,128]{2,1,0:T(1,128)S(1)} %bitcast.13), channel_id=1, replica_groups=mesh['cond'=2,'gx_0'=4,'gx_1'=2,'yz_0'=4,'yz_1'=4] {'gx_0','gx_1','yz_0'}, dimensions={0} | all-to-all | bytes 32768 | tf_op jit(solution)/shard_map/all_to_all | solution.py:347
  34.6 0.6 %collective-permute-start.12 = (f32[1,128]{1,0:T(1,128)S(1)}, f32[1,128]{1,0:T(1,128)S(1)}, u32[]{:S(2)}, u32[]{:S(2)}) collective-permute-start(f32[1,128]{1,0:T(1,128)S(1)} %bitcast.17), channel_id=1, source_target_pairs={{0,1},{1,0},{2,3},{3,2},{128,129},{129,128},{130,131},{131,130},{4... | collective-permute-start | bytes 1544 | tf_op jit(solution)/shard_map/ppermute | solution.py:349
  35.2 1.3 %collective-permute-start.9 = (f32[5,16,256]{2,1,0:T(8,128)S(1)}, f32[5,16,256]{2,1,0:T(8,128)S(1)}, u32[]{:S(2)}, u32[]{:S(2)}) collective-permute-start(f32[5,16,256]{2,1,0:T(8,128)S(1)} %get-tuple-element.43), channel_id=1, source_target_pairs={{0,112},{16,32},{32,16},{48,64},{64,48},{80,96},{96,80},{112,0},{1... | collective-permute-start | bytes 245768 | tf_op jit(solution)/shard_map/ppermute | solution.py:278
  36.5 1.4 %collective-permute-start.10 = (f32[5,8,256]{2,1,0:T(8,128)S(1)}, f32[5,8,256]{2,1,0:T(8,128)S(1)}, u32[]{:S(2)}, u32[]{:S(2)}) collective-permute-start(f32[5,8,256]{2,1,0:T(8,128)S(1)} %get-tuple-element.44), channel_id=1, source_target_pairs={{0,1},{1,0},{2,3},{3,2},{4,5},{5,4},{6,7},{7,6},{8,9},{9,8},{10,11... | collective-permute-start | bytes 122888 | tf_op jit(solution)/shard_map/ppermute | solution.py:277
  38.0 5.7 %collective-permute-start.11 = (f32[5,8,256]{2,1,0:T(8,128)S(1)}, f32[5,8,256]{2,1,0:T(8,128)S(1)}, u32[]{:S(2)}, u32[]{:S(2)}) collective-permute-start(f32[5,8,256]{2,1,0:T(8,128)S(1)} %get-tuple-element.45), channel_id=1, source_target_pairs={{0,15},{1,2},{2,1},{3,4},{4,3},{5,6},{6,5},{7,8},{8,7},{9,10},{10,... | collective-permute-start | bytes 122888 | tf_op jit(solution)/shard_map/ppermute | solution.py:276
  43.6 1.5 %collective-permute-start.13 = (f32[1,128]{1,0:T(1,128)S(1)}, f32[1,128]{1,0:T(1,128)S(1)}, u32[]{:S(2)}, u32[]{:S(2)}) collective-permute-start(f32[1,128]{1,0:T(1,128)S(1)} %bitcast_add_fusion), channel_id=1, source_target_pairs={{0,131},{1,2},{2,1},{3,128},{128,3},{129,130},{130,129},{131,0},{4... | collective-permute-start | bytes 1544 | tf_op jit(solution)/shard_map/ppermute | solution.py:351
  45.1 3.3 %collective-permute-done.13 = f32[1,128]{1,0:T(1,128)S(1)} collective-permute-done((f32[1,128]{1,0:T(1,128)S(1)}, f32[1,128]{1,0:T(1,128)S(1)}, u32[]{:S(2)}, u32[]{:S(2)}) %collective-permute-start.13) | collective-permute-done | bytes 544 | tf_op jit(solution)/shard_map/ppermute | solution.py:351
  48.4 2.7 %collective-permute-start.14 = (f32[1,128]{1,0:T(1,128)S(1)}, f32[1,128]{1,0:T(1,128)S(1)}, u32[]{:S(2)}, u32[]{:S(2)}) collective-permute-start(f32[1,128]{1,0:T(1,128)S(1)} %add.7.part_ref), channel_id=1, source_target_pairs={{0,3},{3,0},{1,130},{130,1},{2,129},{129,2},{128,131},{131,128},{4... | collective-permute-start | bytes 1544 | tf_op jit(solution)/shard_map/ppermute | solution.py:353
  51.1 1.5 %inner_residual.1 = (f32[5,8,16,256]{3,2,1,0:T(8,128)S(1)}, f32[5,8,16,256]{3,2,1,0:T(8,128)}) custom-call(f32[151,128]{1,0:T(8,128)S(1)} %get-tuple-element.26.blocks_ref, f32[5,8,16,256]{3,2,1,0:T(8,128)S(1)} %get-tuple-element.39.v_ref, f32[5,8,16,256]{3,2,1,0:T(8,128)S(1)} %get-tuple-element.28.source_ref, f32[8,16,256]{2,1,0:T(8,128)S(1)} %get-tuple-element.29.diagonal_ref), custom_call_target="tpu_custom_call" | custom-call | tf_op jit(solution)/shard_map/inner_residual/pallas_call | solution.py:355
  52.7 1.1 %collective-permute-done.14.other_ref = f32[1,128]{1,0:T(1,128)S(1)} collective-permute-done((f32[1,128]{1,0:T(1,128)S(1)}, f32[1,128]{1,0:T(1,128)S(1)}, u32[]{:S(2)}, u32[]{:S(2)}) %collective-permute-start.14) | collective-permute-done | bytes 544 | tf_op jit(solution)/shard_map/ppermute | solution.py:353
  53.8 1.2 %outer_residual.1 = (f32[5,8,16,256]{3,2,1,0:T(8,128)}, f32[1,32]{1,0:T(1,128)}) custom-call(f32[151,128]{1,0:T(8,128)S(1)} %get-tuple-element.26.blocks_ref, f32[5,8,16,256]{3,2,1,0:T(8,128)S(1)} %get-tuple-element.41.inner_ref, f32[5,16,256]{2,1,0:T(8,128)S(1)} %collective-permute-done.8.xa_ref, f32[5,16,256]{2,1,0:T(8,128)S(1)} %collective-permute-done.9.xb_ref, ...), custom_call_target="tpu_custom_call" | custom-call | tf_op jit(solution)/shard_map/outer_residual/pallas_call | solution.py:363
  (26 shorter events, 0.3 us)
Async XLA Ops:
  1.8 11.8 %collective-permute-start = (f32[5,16,256]{2,1,0:T(8,128)S(1)}, f32[5,16,256]{2,1,0:T(8,128)S(1)}, u32[]{:S(2)}, u32[]{:S(2)}) collective-permute-start(f32[5,16,256]{2,1,0:T(8,128)S(1)} %get-tuple-element.30), channel_id=1, source_target_pairs={{0,16},{16,0},{32,48},{48,32},{64,80},{80,64},{96,112},{112,96},{1... | collective-permute-start | bytes 245768 | tf_op jit(solution)/shard_map/ppermute | solution.py:279
  1.9 11.7 %collective-permute-start.1 = (f32[5,16,256]{2,1,0:T(8,128)S(1)}, f32[5,16,256]{2,1,0:T(8,128)S(1)}, u32[]{:S(2)}, u32[]{:S(2)}) collective-permute-start(f32[5,16,256]{2,1,0:T(8,128)S(1)} %get-tuple-element.31), channel_id=1, source_target_pairs={{0,112},{16,32},{32,16},{48,64},{64,48},{80,96},{96,80},{112,0},{1... | collective-permute-start | bytes 245768 | tf_op jit(solution)/shard_map/ppermute | solution.py:278
  5.1 7.4 %collective-permute-start.2 = (f32[5,8,256]{2,1,0:T(8,128)S(1)}, f32[5,8,256]{2,1,0:T(8,128)S(1)}, u32[]{:S(2)}, u32[]{:S(2)}) collective-permute-start(f32[5,8,256]{2,1,0:T(8,128)S(1)} %get-tuple-element.32), channel_id=1, source_target_pairs={{0,1},{1,0},{2,3},{3,2},{4,5},{5,4},{6,7},{7,6},{8,9},{9,8},{10,11... | collective-permute-start | bytes 122888 | tf_op jit(solution)/shard_map/ppermute | solution.py:277
  7.0 6.7 %collective-permute-start.3 = (f32[5,8,256]{2,1,0:T(8,128)S(1)}, f32[5,8,256]{2,1,0:T(8,128)S(1)}, u32[]{:S(2)}, u32[]{:S(2)}) collective-permute-start(f32[5,8,256]{2,1,0:T(8,128)S(1)} %get-tuple-element.33), channel_id=1, source_target_pairs={{0,15},{1,2},{2,1},{3,4},{4,3},{5,6},{6,5},{7,8},{8,7},{9,10},{10,... | collective-permute-start | bytes 122888 | tf_op jit(solution)/shard_map/ppermute | solution.py:276
  14.0 7.8 %collective-permute-start.4 = (f32[5,16,256]{2,1,0:T(8,128)S(1)}, f32[5,16,256]{2,1,0:T(8,128)S(1)}, u32[]{:S(2)}, u32[]{:S(2)}) collective-permute-start(f32[5,16,256]{2,1,0:T(8,128)S(1)} %get-tuple-element.35), channel_id=1, source_target_pairs={{0,16},{16,0},{32,48},{48,32},{64,80},{80,64},{96,112},{112,96},{1... | collective-permute-start | bytes 245768 | tf_op jit(solution)/shard_map/ppermute | solution.py:279
  14.1 7.7 %collective-permute-start.5 = (f32[5,16,256]{2,1,0:T(8,128)S(1)}, f32[5,16,256]{2,1,0:T(8,128)S(1)}, u32[]{:S(2)}, u32[]{:S(2)}) collective-permute-start(f32[5,16,256]{2,1,0:T(8,128)S(1)} %get-tuple-element.36), channel_id=1, source_target_pairs={{0,112},{16,32},{32,16},{48,64},{64,48},{80,96},{96,80},{112,0},{1... | collective-permute-start | bytes 245768 | tf_op jit(solution)/shard_map/ppermute | solution.py:278
  14.9 4.4 %collective-permute-start.6 = (f32[5,8,256]{2,1,0:T(8,128)S(1)}, f32[5,8,256]{2,1,0:T(8,128)S(1)}, u32[]{:S(2)}, u32[]{:S(2)}) collective-permute-start(f32[5,8,256]{2,1,0:T(8,128)S(1)} %get-tuple-element.37), channel_id=1, source_target_pairs={{0,1},{1,0},{2,3},{3,2},{4,5},{5,4},{6,7},{7,6},{8,9},{9,8},{10,11... | collective-permute-start | bytes 122888 | tf_op jit(solution)/shard_map/ppermute | solution.py:277
  14.9 6.8 %collective-permute-start.7 = (f32[5,8,256]{2,1,0:T(8,128)S(1)}, f32[5,8,256]{2,1,0:T(8,128)S(1)}, u32[]{:S(2)}, u32[]{:S(2)}) collective-permute-start(f32[5,8,256]{2,1,0:T(8,128)S(1)} %get-tuple-element.38), channel_id=1, source_target_pairs={{0,15},{1,2},{2,1},{3,4},{4,3},{5,6},{6,5},{7,8},{8,7},{9,10},{10,... | collective-permute-start | bytes 122888 | tf_op jit(solution)/shard_map/ppermute | solution.py:276
  17.8 4.0 %copy-start = (bf16[1,5,8,16,256]{4,3,2,1,0:T(8,128)(2,1)S(1)}, bf16[1,5,8,16,256]{4,3,2,1,0:T(8,128)(2,1)}, u32[]{:S(2)}) copy-start(bf16[1,5,8,16,256]{4,3,2,1,0:T(8,128)(2,1)} %param.13) | copy-start | bytes 983044
  17.8 4.0 %copy-start.1 = (s32[8,16,256]{2,1,0:T(8,128)S(1)}, s32[8,16,256]{2,1,0:T(8,128)}, u32[]{:S(2)}) copy-start(s32[8,16,256]{2,1,0:T(8,128)} %mask_ref.1) | copy-start | bytes 393220
  17.8 4.0 %copy-start.2 = (f32[256,128]{1,0:T(8,128)S(1)}, f32[256,128]{1,0:T(8,128)}, u32[]{:S(2)}) copy-start(f32[256,128]{1,0:T(8,128)} %basis_ref.1) | copy-start | bytes 393220
  17.8 4.0 %copy-start.3 = (s32[8,16]{1,0:T(8,128)S(1)}, s32[8,16]{1,0:T(8,128)}, u32[]{:S(2)}) copy-start(s32[8,16]{1,0:T(8,128)} %slot_ref.1) | copy-start | bytes 1540
  34.6 9.0 %collective-permute-start.12 = (f32[1,128]{1,0:T(1,128)S(1)}, f32[1,128]{1,0:T(1,128)S(1)}, u32[]{:S(2)}, u32[]{:S(2)}) collective-permute-start(f32[1,128]{1,0:T(1,128)S(1)} %bitcast.17), channel_id=1, source_target_pairs={{0,1},{1,0},{2,3},{3,2},{128,129},{129,128},{130,131},{131,130},{4... | collective-permute-start | bytes 1544 | tf_op jit(solution)/shard_map/ppermute | solution.py:349
  35.2 18.5 %collective-permute-start.8 = (f32[5,16,256]{2,1,0:T(8,128)S(1)}, f32[5,16,256]{2,1,0:T(8,128)S(1)}, u32[]{:S(2)}, u32[]{:S(2)}) collective-permute-start(f32[5,16,256]{2,1,0:T(8,128)S(1)} %get-tuple-element.42), channel_id=1, source_target_pairs={{0,16},{16,0},{32,48},{48,32},{64,80},{80,64},{96,112},{112,96},{1... | collective-permute-start | bytes 245768 | tf_op jit(solution)/shard_map/ppermute | solution.py:279
  35.2 18.6 %collective-permute-start.9 = (f32[5,16,256]{2,1,0:T(8,128)S(1)}, f32[5,16,256]{2,1,0:T(8,128)S(1)}, u32[]{:S(2)}, u32[]{:S(2)}) collective-permute-start(f32[5,16,256]{2,1,0:T(8,128)S(1)} %get-tuple-element.43), channel_id=1, source_target_pairs={{0,112},{16,32},{32,16},{48,64},{64,48},{80,96},{96,80},{112,0},{1... | collective-permute-start | bytes 245768 | tf_op jit(solution)/shard_map/ppermute | solution.py:278
  36.5 17.3 %collective-permute-start.10 = (f32[5,8,256]{2,1,0:T(8,128)S(1)}, f32[5,8,256]{2,1,0:T(8,128)S(1)}, u32[]{:S(2)}, u32[]{:S(2)}) collective-permute-start(f32[5,8,256]{2,1,0:T(8,128)S(1)} %get-tuple-element.44), channel_id=1, source_target_pairs={{0,1},{1,0},{2,3},{3,2},{4,5},{5,4},{6,7},{7,6},{8,9},{9,8},{10,11... | collective-permute-start | bytes 122888 | tf_op jit(solution)/shard_map/ppermute | solution.py:277
  38.0 15.8 %collective-permute-start.11 = (f32[5,8,256]{2,1,0:T(8,128)S(1)}, f32[5,8,256]{2,1,0:T(8,128)S(1)}, u32[]{:S(2)}, u32[]{:S(2)}) collective-permute-start(f32[5,8,256]{2,1,0:T(8,128)S(1)} %get-tuple-element.45), channel_id=1, source_target_pairs={{0,15},{1,2},{2,1},{3,4},{4,3},{5,6},{6,5},{7,8},{8,7},{9,10},{10,... | collective-permute-start | bytes 122888 | tf_op jit(solution)/shard_map/ppermute | solution.py:276
  43.6 4.8 %collective-permute-start.13 = (f32[1,128]{1,0:T(1,128)S(1)}, f32[1,128]{1,0:T(1,128)S(1)}, u32[]{:S(2)}, u32[]{:S(2)}) collective-permute-start(f32[1,128]{1,0:T(1,128)S(1)} %bitcast_add_fusion), channel_id=1, source_target_pairs={{0,131},{1,2},{2,1},{3,128},{128,3},{129,130},{130,129},{131,0},{4... | collective-permute-start | bytes 1544 | tf_op jit(solution)/shard_map/ppermute | solution.py:351
  48.4 5.4 %collective-permute-start.14 = (f32[1,128]{1,0:T(1,128)S(1)}, f32[1,128]{1,0:T(1,128)S(1)}, u32[]{:S(2)}, u32[]{:S(2)}) collective-permute-start(f32[1,128]{1,0:T(1,128)S(1)} %add.7.part_ref), channel_id=1, source_target_pairs={{0,3},{3,0},{1,130},{130,1},{2,129},{129,2},{128,131},{131,128},{4... | collective-permute-start | bytes 1544 | tf_op jit(solution)/shard_map/ppermute | solution.py:353

commit v4 on v3

--- a/solution.py
+++ b/solution.py
@@ -67,28 +67,22 @@
     return jnp.concatenate([rows] * (shape[1] // 128), axis=1)
 
 
-def first_sides_kernel(v_hbm, v_ref, xa_ref, xb_ref, ya_ref, yb_ref, sem):
-    copy = pltpu.make_async_copy(v_hbm, v_ref, sem)
-    copy.start()
-    copy.wait()
-    nvar, nx, ny, _ = v_ref.shape
-    write_sides(lambda k, x: v_ref[k, x], nvar, nx, ny, xa_ref, xb_ref, ya_ref, yb_ref)
-
-
 def load_kernel(
-    blocks_hbm, weights_hbm, source_hbm, diagonal_hbm, source_ref, diagonal_ref, table_ref,
-    blocks_ref, weights_ref, sems,
+    blocks_hbm, weights_hbm, v_hbm, source_hbm, diagonal_hbm,
+    v_ref, source_ref, diagonal_ref, table_ref, xa_ref, xb_ref, ya_ref, yb_ref,
+    blocks_ref, weights_ref, next_ref, wanted_ref, sems,
 ):
     pairs = (
         (blocks_hbm, blocks_ref),
         (weights_hbm, weights_ref),
+        (v_hbm, v_ref),
         (source_hbm, source_ref),
         (diagonal_hbm, diagonal_ref),
     )
     copies = [pltpu.make_async_copy(a, b, sems.at[i]) for i, (a, b) in enumerate(pairs)]
     for copy in copies:
         copy.start()
-    nvar = source_ref.shape[0]
+    nvar, nx, ny, nz = v_ref.shape
     for copy in copies[:2]:
         copy.wait()
     for d in range(6):
@@ -103,6 +97,37 @@
     table_ref[last : last + 1, :] = (one * mine.astype(jnp.float32)) / (one * total)
     for copy in copies[2:]:
         copy.wait()
+    write_sides(lambda k, x: v_ref[k, x], nvar, nx, ny, xa_ref, xb_ref, ya_ref, yb_ref)
+    even = lax.rem(position()[1], 2) == 0
+    for x in range(nx):
+        here = slice(x, x + 1)
+        yb_ref[2 * nvar, here, :] = jnp.where(even, diagonal_ref[x, 0:1], diagonal_ref[x, ny - 1 : ny])
+        for k in range(nvar):
+            next_ref[k, here, :] = jnp.where(even, v_ref[k, x, 1:2], v_ref[k, x, ny - 2 : ny - 1])
+            wanted_ref[k, here, :] = jnp.where(even, source_ref[k, x, 0:1], source_ref[k, x, ny - 1 : ny])
+    row = lax.broadcasted_iota(jnp.int32, (nx, nz), 0)
+    lane = lax.broadcasted_iota(jnp.int32, (nx, nz), 1)
+    sums = [0.0] * nvar
+    for e in range(nvar):
+        edge = yb_ref[e]
+        shifted = {
+            0: jnp.where(row == nx - 1, 0.0, pltpu.roll(edge, nx - 1, 0)),
+            1: jnp.where(row == 0, 0.0, pltpu.roll(edge, 1, 0)),
+            4: jnp.where(lane == nz - 1, 0.0, pltpu.roll(edge, nz - 1, 1)),
+            5: jnp.where(lane == 0, 0.0, pltpu.roll(edge, 1, 1)),
+        }
+        inward = next_ref[e]
+        for k in range(nvar):
+            for d, values in shifted.items():
+                sums[k] = sums[k] + coefficient(table_ref, d, e, k, nvar, values.shape) * values
+            both = [coefficient(table_ref, d, e, k, nvar, inward.shape) for d in (2, 3)]
+            sums[k] = sums[k] + jnp.where(even, both[0], both[1]) * inward
+    diagonal = yb_ref[2 * nvar]
+    scale = RELAXATION / diagonal
+    for k in range(nvar):
+        edge = yb_ref[k]
+        yb_ref[nvar + k] = edge + scale * (wanted_ref[k] - diagonal * edge + sums[k])
+    yb_ref[2 * nvar] = scale
 
 
 def neighbour_sums(v_ref, blocks_ref, x):
@@ -151,7 +176,7 @@
     copy.wait()
 
 
-def add_halo(blocks_ref, inner_ref, diagonal_ref, xa_ref, xb_ref, ya_ref, yb_ref, out_ref):
+def add_halo(blocks_ref, inner_ref, diagonal_ref, xa, xb, ya, yb, out_ref):
     nvar, nx, ny, nz = inner_ref.shape
     gx, yz = position()
     gx_even, yz_even = lax.rem(gx, 2) == 0, lax.rem(yz, 2) == 0
@@ -167,17 +192,17 @@
                 sums[k] = term if sums[k] is None else sums[k] + term
         return sums
 
-    def picker(even, a_ref, b_ref, exists):
-        return lambda e: jnp.where(exists, jnp.where(even, a_ref[e], b_ref[e]), 0.0)
-
-    high_y = halo_sums(2, picker(yz_even, ya_ref, yb_ref, has_high_y))
-    low_y = halo_sums(3, picker(yz_even, yb_ref, ya_ref, has_low_y))
+    def picker(even, a, b, exists):
+        return lambda e: jnp.where(exists, jnp.where(even, a(e), b(e)), 0.0)
+
+    high_y = halo_sums(2, picker(yz_even, ya, yb, has_high_y))
+    low_y = halo_sums(3, picker(yz_even, yb, ya, has_low_y))
     row = lax.broadcasted_iota(jnp.int32, (8, nz), 0)
     for x in range(nx):
         if x == 0:
-            at_x = halo_sums(1, picker(gx_even, xb_ref, xa_ref, has_low_x))
+            at_x = halo_sums(1, picker(gx_even, xb, xa, has_low_x))
         elif x == nx - 1:
-            at_x = halo_sums(0, picker(gx_even, xa_ref, xb_ref, has_high_x))
+            at_x = halo_sums(0, picker(gx_even, xa, xb, has_high_x))
         else:
             at_x = None
         for start in range(0, ny, 8):
@@ -198,25 +223,71 @@
                 out_ref[k, x, rows] = value
 
 
+def reader(ref):
+    return lambda e: ref[e]
+
+
 def outer_sweep_kernel(
     blocks_ref, inner_ref, diagonal_ref, xa_ref, xb_ref, ya_ref, yb_ref,
-    out_ref, next_xa_ref, next_xb_ref, next_ya_ref, next_yb_ref,
+    out_ref, next_xa_ref, next_xb_ref, next_ya_ref,
+):
+    nvar, nx, ny, nz = inner_ref.shape
+    halo = [reader(ref) for ref in (xa_ref, xb_ref, ya_ref, yb_ref)]
+    add_halo(blocks_ref, inner_ref, diagonal_ref, *halo, out_ref)
+    gx, yz = position()
+    gx_even, yz_even = lax.rem(gx, 2) == 0, lax.rem(yz, 2) == 0
+    top = nvar * ny
+    next_xa_ref[top:, :] = jnp.zeros((next_xa_ref.shape[0] - top, nz), jnp.float32)
+    next_xb_ref[top:, :] = jnp.zeros((next_xb_ref.shape[0] - top, nz), jnp.float32)
+    for k in range(nvar):
+        low, high = out_ref[k, 0], out_ref[k, nx - 1]
+        next_xa_ref[k * ny : (k + 1) * ny, :] = jnp.where(gx_even, high, low)
+        next_xb_ref[k * ny : (k + 1) * ny, :] = jnp.where(gx_even, low, high)
+        low, high = yb_ref[k, 0:1], yb_ref[k, nx - 1 : nx]
+        next_xa_ref[top + k : top + k + 1, :] = jnp.where(gx_even, high, low)
+        next_xb_ref[top + k : top + k + 1, :] = jnp.where(gx_even, low, high)
+        for x in range(nx):
+            slab = out_ref[k, x]
+            next_ya_ref[k, x : x + 1, :] = jnp.where(yz_even, slab[ny - 1 : ny], slab[0:1])
+
+
+def complete_far_row(blocks_ref, xa_ref, xb_ref, far_ref, edge_ref, out_ref):
+    nvar, nx, nz = out_ref.shape
+    top = xa_ref.shape[0] - 8
+    gx, yz = position()
+    gx_even, yz_even = lax.rem(gx, 2) == 0, lax.rem(yz, 2) == 0
+    row = lax.broadcasted_iota(jnp.int32, (nx, nz), 0)
+    at_low, at_high = (row == 0) & (gx > 0), (row == nx - 1) & (gx < 7)
+    sums = [0.0] * nvar
+    for e in range(nvar):
+        edge = edge_ref[e]
+        a, b = xa_ref[top + e : top + e + 1, :], xb_ref[top + e : top + e + 1, :]
+        low = jnp.where(at_low, jnp.where(gx_even, b, a), 0.0)
+        high = jnp.where(at_high, jnp.where(gx_even, a, b), 0.0)
+        for k in range(nvar):
+            both = [coefficient(blocks_ref, d, e, k, nvar, edge.shape) for d in (2, 3)]
+            sums[k] = sums[k] + jnp.where(yz_even, both[0], both[1]) * edge
+            sums[k] = sums[k] + coefficient(blocks_ref, 1, e, k, nvar, edge.shape) * low
+            sums[k] = sums[k] + coefficient(blocks_ref, 0, e, k, nvar, edge.shape) * high
+    for k in range(nvar):
+        out_ref[k] = far_ref[nvar + k] + far_ref[2 * nvar] * sums[k]
+
+
+def last_sweep_kernel(
+    blocks_ref, inner_ref, diagonal_ref, xa_ref, xb_ref, ya_ref, far_ref, edge_ref,
+    sensitivity_ref, mask_ref, slot_ref, basis_ref,
+    out_ref, next_xa_ref, next_xb_ref, next_ya_ref, next_yb_ref, gradient_ref, surface_ref, row_ref,
 ):
     nvar, nx, ny, _ = inner_ref.shape
-    add_halo(blocks_ref, inner_ref, diagonal_ref, xa_ref, xb_ref, ya_ref, yb_ref, out_ref)
+    complete_far_row(blocks_ref, xa_ref, xb_ref, far_ref, edge_ref, row_ref)
+    add_halo(
+        blocks_ref, inner_ref, diagonal_ref,
+        lambda e: xa_ref[e * ny : (e + 1) * ny, :],
+        lambda e: xb_ref[e * ny : (e + 1) * ny, :],
+        reader(ya_ref), reader(row_ref), out_ref,
+    )
     write_sides(
         lambda k, x: out_ref[k, x], nvar, nx, ny, next_xa_ref, next_xb_ref, next_ya_ref, next_yb_ref
-    )
-
-
-def last_sweep_kernel(
-    blocks_ref, inner_ref, diagonal_ref, xa_ref, xb_ref, ya_ref, yb_ref,
-    sensitivity_ref, mask_ref, slot_ref, basis_ref,
-    out_ref, next_xa_ref, next_xb_ref, next_ya_ref, next_yb_ref, gradient_ref, surface_ref,
-):
-    outer_sweep_kernel(
-        blocks_ref, inner_ref, diagonal_ref, xa_ref, xb_ref, ya_ref, yb_ref,
-        out_ref, next_xa_ref, next_xb_ref, next_ya_ref, next_yb_ref,
     )
     nvar, nx, ny, _ = inner_ref.shape
     for x in range(nx):
@@ -251,10 +322,12 @@
     gradient_ref[...] = gradient * jnp.concatenate([share] * (pairs // 8), axis=0)
 
 
-def outer_residual_kernel(
-    blocks_ref, inner_ref, xa_ref, xb_ref, ya_ref, yb_ref, part_ref, other_ref, out_ref, piece_ref,
-):
-    add_halo(blocks_ref, inner_ref, None, xa_ref, xb_ref, ya_ref, yb_ref, out_ref)
+def outer_residual_kernel(blocks_ref, inner_ref, xa_ref, xb_ref, ya_ref, yb_ref, out_ref):
+    halo = [reader(ref) for ref in (xa_ref, xb_ref, ya_ref, yb_ref)]
+    add_halo(blocks_ref, inner_ref, None, *halo, out_ref)
+
+
+def finish_kernel(part_ref, other_ref, piece_ref):
     size = piece_ref.shape[1]
     total = part_ref[...] + other_ref[...]
     which = lax.axis_index("yz_1")
@@ -272,12 +345,12 @@
     return [(i, (((i + 1) ^ 1) - 1) % n) for i in range(n)]
 
 
-def exchange(xa, xb, ya, yb):
-    far = lax.ppermute(yb, YZ, swap_b(16))
-    near = lax.ppermute(ya, YZ, swap_a(16))
+def exchange(xa, xb, ya, yb=None):
+    far = [] if yb is None else [lax.ppermute(yb, YZ, swap_b(16))]
     chip = lax.ppermute(xb, GX, swap_b(8))
     core = lax.ppermute(xa, GX, swap_a(8))
-    return tuple(near_core(x) for x in (core, chip, near, far))
+    near = lax.ppermute(ya, YZ, swap_a(16))
+    return [near_core(x) for x in (core, chip, near, *far)]
 
 
 def step(
@@ -297,52 +370,59 @@
     field = kept(nvar, nx, ny, nz)
     sides = (kept(nvar, ny, nz), kept(nvar, ny, nz), kept(nvar, nx, nz), kept(nvar, nx, nz))
 
-    v, *first = call(
-        first_sides_kernel,
-        out_shape=(field, *sides),
-        in_specs=[HBM],
-        out_specs=[VMEM] * 5,
-        scratch_shapes=[pltpu.SemaphoreType.DMA],
-        name="first_sides",
-    )(far_from_core(adjoint[0]))
-    v = near_core(v)
-    halo = exchange(*first)
-    arrays = (flux_blocks.transpose(2, 3, 0, 1), condition_weights, objective_gradient[0], diagonal)
-    source, diagonal, table = call(
+    arrays = (flux_blocks.transpose(2, 3, 0, 1), condition_weights, adjoint[0], objective_gradient[0], diagonal)
+    v, source, diagonal, blocks, *first = call(
         load_kernel,
-        out_shape=(field, kept(nx, ny, nz), kept(6 * nvar * nvar + 1, 128)),
-        in_specs=[HBM] * 4,
-        out_specs=[VMEM] * 3,
+        out_shape=(
+            field,
+            field,
+            kept(nx, ny, nz),
+            kept(6 * nvar * nvar + 1, 128),
+            *sides[:3],
+            kept(2 * nvar + 1, nx, nz),
+        ),
+        in_specs=[HBM] * 5,
+        out_specs=[VMEM] * 8,
         scratch_shapes=[
             pltpu.SMEM((nvar, nvar, 1, 6), jnp.float32),
             pltpu.SMEM(condition_weights.shape, jnp.int32),
-            pltpu.SemaphoreType.DMA((4,)),
+            pltpu.VMEM((nvar, nx, nz), jnp.float32),
+            pltpu.VMEM((nvar, nx, nz), jnp.float32),
+            pltpu.SemaphoreType.DMA((5,)),
         ],
         name="load",
     )(*(far_from_core(x) for x in arrays))
-    source, diagonal, blocks = near_core(source), near_core(diagonal), near_core(table)
+    v, source, diagonal, blocks = (near_core(x) for x in (v, source, diagonal, blocks))
+    halo = exchange(*first)
     inner_sweep = call(
         inner_sweep_kernel, out_shape=field, in_specs=[VMEM] * 4, out_specs=VMEM, name="inner_sweep"
     )
     inner = inner_sweep(blocks, v, source, diagonal)
     relaxed, *second = call(
         outer_sweep_kernel,
-        out_shape=(field, *sides),
+        out_shape=(field, kept(nvar * ny + 8, nz), kept(nvar * ny + 8, nz), sides[2]),
         in_specs=[VMEM] * 7,
-        out_specs=[VMEM] * 5,
+        out_specs=[VMEM] * 4,
         name="outer_sweep",
     )(blocks, near_core(inner), diagonal, *halo)
+    far, edge = halo[3], near_core(first[3])
 
     halo = exchange(*second)
     inner = inner_sweep(blocks, near_core(relaxed), source, diagonal)
     smoothed, xa, xb, ya, yb, gradient = call(
         last_sweep_kernel,
         out_shape=(field, *sides, kept(NDES // 128, 128)),
-        in_specs=[VMEM] * 11,
+        in_specs=[VMEM] * 12,
         out_specs=[VMEM] * 6,
-        scratch_shapes=[pltpu.VMEM((nx * ny, nz), jnp.float32)],
+        scratch_shapes=[
+            pltpu.VMEM((nx * ny, nz), jnp.float32),
+            pltpu.VMEM((nvar, nx, nz), jnp.float32),
+        ],
         name="last_sweep",
-    )(blocks, near_core(inner), diagonal, *halo, sensitivity, mask, near_core(patch_band_slot), basis)
+    )(
+        blocks, near_core(inner), diagonal, *halo, far, edge,
+        sensitivity, mask, near_core(patch_band_slot), basis,
+    )
 
     parts = lax.all_to_all(gradient, SPREAD, 0, 0, tiled=True)
     total = jnp.sum(parts, axis=0, keepdims=True)
@@ -360,13 +440,16 @@
         scratch_shapes=[pltpu.SemaphoreType.DMA],
         name="inner_residual",
     )(blocks, near_core(smoothed), source, diagonal)
-    residual, design_gradient = call(
+    residual = call(
         outer_residual_kernel,
-        out_shape=(f32(nvar, nx, ny, nz), f32(1, 32)),
-        in_specs=[VMEM] * 8,
-        out_specs=[VMEM] * 2,
+        out_shape=f32(nvar, nx, ny, nz),
+        in_specs=[VMEM] * 6,
+        out_specs=VMEM,
         name="outer_residual",
-    )(blocks, near_core(inner), *halo, near_core(total), near_core(other))
+    )(blocks, near_core(inner), *halo)
+    design_gradient = call(
+        finish_kernel, out_shape=f32(1, 32), in_specs=[VMEM] * 2, out_specs=VMEM, name="finish"
+    )(near_core(total), near_core(other))
     return smoothed[None], residual[None], design_gradient.reshape(-1)
 
 

time: 55.2 us -> 50.9 us (0.922)
  the two profiles are of different devices: /device:TPU:2 before, /device:TPU:32 now
where the time goes in v4:
time: 50.9 us; the launch traced here: 50.7 us
  starting transfers between devices  23.6 us (46%)
  blocking collectives  10.4 us (20%)
  Pallas kernels  9.34 us (18%)
  waiting for transfers between devices  6.52 us (13%)
  between operations  0.73 us (1%)
    all_to_all x1, blocking collectives, step(): parts = lax.all_to_all(gradient, SPREAD, 0, 0, tiled=True)  10.4 us
    ppermute x3, starting transfers between devices, exchange(): near = lax.ppermute(ya, YZ, swap_a(16))  8.61 us
    ppermute x3, starting transfers between devices, exchange(): chip = lax.ppermute(xb, GX, swap_b(8))  5.57 us
    ppermute x2, starting transfers between devices, exchange(): far = [] if yb is None else [lax.ppermute(yb, YZ, swap_b(16))]  4.23 us
    ppermute x1, waiting for transfers between devices, step(): lax.ppermute(total, RING, [(i, ((i + 1 ^ 1) - 1) % 8) for i in range(8)])  3.56 us
    ppermute x1, starting transfers between devices, step(): other = lax.ppermute(total, RING, across)  3.03 us
    ppermute x1, starting transfers between devices, step(): total = total + lax.ppermute(total, RING, [(i, i ^ 1) for i in range(8)])  2.1 us
    ppermute x1, waiting for transfers between devices, step(): other = lax.ppermute(total, RING, across)  2 us
  transfers between devices with their start and end apart: 14, of which 4 were waited for; matrix products, arithmetic and copies ran while one was open for 0% of the time, Pallas kernels for 11%

profile of v4, /device:TPU:32, one launch (start us, length us, event | category | flops | bytes accessed | tf_op | source)
XLA Modules:
  0.0 50.7 jit_solution(1696474709194963803)
XLA Ops:
  0.6 1.6 %load.1 = (f32[5,8,16,256]{3,2,1,0:T(8,128)S(1)}, f32[5,8,16,256]{3,2,1,0:T(8,128)S(1)}, f32[8,16,256]{2,1,0:T(8,128)S(1)}, f32[151,128]{1,0:T(8,128)S(1)}, f32[...) custom-call(f32[5,5,1,6]{3,2,1,0:T(1,128)} %bitcast.17, ...), custom_call_target="tpu_custom_call" | custom-call | tf_op jit(solution)/shard_map/load/pallas_call | solution.py:374
  2.2 2.0 %collective-permute-start.3 = (f32[11,8,256]{2,1,0:T(8,128)S(1)}, f32[11,8,256]{2,1,0:T(8,128)S(1)}, u32[]{:S(2)}, u32[]{:S(2)}) collective-permute-start(f32[11,8,256]{2,1,0:T(8,128)S(1)} %get-tuple-element.30.edge_ref), channel_id=1, source_target_pairs={{0,15},{1,2},{2,1},{3,4},{4,3},{5,6},{6,5},{7,8},{8,7},{9,10},{10,... | collective-permute-start | bytes 270344 | tf_op jit(solution)/shard_map/ppermute | solution.py:349
  4.2 3.1 %collective-permute-start.1 = (f32[5,16,256]{2,1,0:T(8,128)S(1)}, f32[5,16,256]{2,1,0:T(8,128)S(1)}, u32[]{:S(2)}, u32[]{:S(2)}) collective-permute-start(f32[5,16,256]{2,1,0:T(8,128)S(1)} %get-tuple-element.28), channel_id=1, source_target_pairs={{0,112},{16,32},{32,16},{48,64},{64,48},{80,96},{96,80},{112,0},{1... | collective-permute-start | bytes 245768 | tf_op jit(solution)/shard_map/ppermute | solution.py:350
  7.4 5.0 %collective-permute-start.2 = (f32[5,8,256]{2,1,0:T(8,128)S(1)}, f32[5,8,256]{2,1,0:T(8,128)S(1)}, u32[]{:S(2)}, u32[]{:S(2)}) collective-permute-start(f32[5,8,256]{2,1,0:T(8,128)S(1)} %get-tuple-element.29), channel_id=1, source_target_pairs={{0,1},{1,0},{2,3},{3,2},{4,5},{5,4},{6,7},{7,6},{8,9},{9,8},{10,11... | collective-permute-start | bytes 122888 | tf_op jit(solution)/shard_map/ppermute | solution.py:352
  12.4 1.5 %inner_sweep.2.inner_ref = f32[5,8,16,256]{3,2,1,0:T(8,128)S(1)} custom-call(f32[151,128]{1,0:T(8,128)S(1)} %get-tuple-element.23.blocks_ref, f32[5,8,16,256]{3,2,1,0:T(8,128)S(1)} %get-tuple-element.24.v_ref, f32[5,8,16,256]{3,2,1,0:T(8,128)S(1)} %get-tuple-element.25.source_ref, f32[8,16,256]{2,1,0:T(8,128)S(1)} %get-tuple-element.26.diagonal_ref), custom_call_target="tpu_custom_call" | custom-call | tf_op jit(solution)/shard_map/inner_sweep/pallas_call | solution.py:400
  13.9 0.5 collective-permute-done.2.ya_ref
  14.4 0.3 outer_sweep.1
  14.7 0.1 collective-permute-start.4
  14.8 1.2 %collective-permute-start.5 = (f32[88,256]{1,0:T(8,128)S(1)}, f32[88,256]{1,0:T(8,128)S(1)}, u32[]{:S(2)}, u32[]{:S(2)}) collective-permute-start(f32[88,256]{1,0:T(8,128)S(1)} %get-tuple-element.33), channel_id=1, source_target_pairs={{0,112},{16,32},{32,16},{48,64},{64,48},{80,96},{96,80},{112,0},{1... | collective-permute-start | bytes 270344 | tf_op jit(solution)/shard_map/ppermute | solution.py:350
  16.0 1.9 %collective-permute-start.6 = (f32[5,8,256]{2,1,0:T(8,128)S(1)}, f32[5,8,256]{2,1,0:T(8,128)S(1)}, u32[]{:S(2)}, u32[]{:S(2)}) collective-permute-start(f32[5,8,256]{2,1,0:T(8,128)S(1)} %get-tuple-element.34), channel_id=1, source_target_pairs={{0,1},{1,0},{2,3},{3,2},{4,5},{5,4},{6,7},{7,6},{8,9},{9,8},{10,11... | collective-permute-start | bytes 122888 | tf_op jit(solution)/shard_map/ppermute | solution.py:352
  17.9 1.6 %inner_sweep.3.inner_ref = f32[5,8,16,256]{3,2,1,0:T(8,128)S(1)} custom-call(f32[151,128]{1,0:T(8,128)S(1)} %get-tuple-element.23.blocks_ref, f32[5,8,16,256]{3,2,1,0:T(8,128)S(1)} %get-tuple-element.31.v_ref, f32[5,8,16,256]{3,2,1,0:T(8,128)S(1)} %get-tuple-element.25.source_ref, f32[8,16,256]{2,1,0:T(8,128)S(1)} %get-tuple-element.26.diagonal_ref), custom_call_target="tpu_custom_call" | custom-call | tf_op jit(solution)/shard_map/inner_sweep/pallas_call | solution.py:411
  19.5 0.5 collective-permute-done.6.ya_ref
  20.0 1.0 %last_sweep.1 = (f32[5,8,16,256]{3,2,1,0:T(8,128)S(1)}, f32[5,16,256]{2,1,0:T(8,128)S(1)}, f32[5,16,256]{2,1,0:T(8,128)S(1)}, f32[5,8,256]{2,1,0:T(8,128)S(1)}, ...) custom-call(f32[151,128]{1,0:T(8,128)S(1)} %get-tuple-element.23.blocks_ref, f32[5,8,16,256]{3,2,1,0:T(8,128)S(1)} %inner_sweep.3.inner_ref, ...), custom_call_target="tpu_custom_call" | custom-call | tf_op jit(solution)/shard_map/last_sweep/pallas_call | solution.py:412
  21.0 10.4 %all_to_all.9 = f32[32,1,128]{2,1,0:T(1,128)S(1)} all-to-all(f32[32,1,128]{2,1,0:T(1,128)S(1)} %bitcast.13), channel_id=1, replica_groups=mesh['cond'=2,'gx_0'=4,'gx_1'=2,'yz_0'=4,'yz_1'=4] {'gx_0','gx_1','yz_0'}, dimensions={0} | all-to-all | bytes 32768 | tf_op jit(solution)/shard_map/all_to_all | solution.py:427
  31.5 2.1 %collective-permute-start.11 = (f32[1,128]{1,0:T(1,128)S(1)}, f32[1,128]{1,0:T(1,128)S(1)}, u32[]{:S(2)}, u32[]{:S(2)}) collective-permute-start(f32[1,128]{1,0:T(1,128)S(1)} %bitcast.18), channel_id=1, source_target_pairs={{0,1},{1,0},{2,3},{3,2},{128,129},{129,128},{130,131},{131,130},{4... | collective-permute-start | bytes 1544 | tf_op jit(solution)/shard_map/ppermute | solution.py:429
  33.6 1.2 %collective-permute-start.8 = (f32[5,16,256]{2,1,0:T(8,128)S(1)}, f32[5,16,256]{2,1,0:T(8,128)S(1)}, u32[]{:S(2)}, u32[]{:S(2)}) collective-permute-start(f32[5,16,256]{2,1,0:T(8,128)S(1)} %get-tuple-element.39), channel_id=1, source_target_pairs={{0,112},{16,32},{32,16},{48,64},{64,48},{80,96},{96,80},{112,0},{1... | collective-permute-start | bytes 245768 | tf_op jit(solution)/shard_map/ppermute | solution.py:350
  34.8 2.2 %collective-permute-start.10 = (f32[5,8,256]{2,1,0:T(8,128)S(1)}, f32[5,8,256]{2,1,0:T(8,128)S(1)}, u32[]{:S(2)}, u32[]{:S(2)}) collective-permute-start(f32[5,8,256]{2,1,0:T(8,128)S(1)} %get-tuple-element.41), channel_id=1, source_target_pairs={{0,15},{1,2},{2,1},{3,4},{4,3},{5,6},{6,5},{7,8},{8,7},{9,10},{10,... | collective-permute-start | bytes 122888 | tf_op jit(solution)/shard_map/ppermute | solution.py:349
  37.0 1.7 %collective-permute-start.9 = (f32[5,8,256]{2,1,0:T(8,128)S(1)}, f32[5,8,256]{2,1,0:T(8,128)S(1)}, u32[]{:S(2)}, u32[]{:S(2)}) collective-permute-start(f32[5,8,256]{2,1,0:T(8,128)S(1)} %get-tuple-element.40), channel_id=1, source_target_pairs={{0,1},{1,0},{2,3},{3,2},{4,5},{5,4},{6,7},{7,6},{8,9},{9,8},{10,11... | collective-permute-start | bytes 122888 | tf_op jit(solution)/shard_map/ppermute | solution.py:352
  38.7 3.6 %collective-permute-done.12 = f32[1,128]{1,0:T(1,128)S(1)} collective-permute-done((f32[1,128]{1,0:T(1,128)S(1)}, f32[1,128]{1,0:T(1,128)S(1)}, u32[]{:S(2)}, u32[]{:S(2)}) %collective-permute-start.12) | collective-permute-done | bytes 544 | tf_op jit(solution)/shard_map/ppermute | solution.py:431
  42.2 3.0 %collective-permute-start.13 = (f32[1,128]{1,0:T(1,128)S(1)}, f32[1,128]{1,0:T(1,128)S(1)}, u32[]{:S(2)}, u32[]{:S(2)}) collective-permute-start(f32[1,128]{1,0:T(1,128)S(1)} %add.7.part_ref), channel_id=1, source_target_pairs={{0,3},{3,0},{1,130},{130,1},{2,129},{129,2},{128,131},{131,128},{4... | collective-permute-start | bytes 1544 | tf_op jit(solution)/shard_map/ppermute | solution.py:433
  45.3 1.5 %inner_residual.1 = (f32[5,8,16,256]{3,2,1,0:T(8,128)S(1)}, f32[5,8,16,256]{3,2,1,0:T(8,128)}) custom-call(f32[151,128]{1,0:T(8,128)S(1)} %get-tuple-element.23.blocks_ref, f32[5,8,16,256]{3,2,1,0:T(8,128)S(1)} %get-tuple-element.35.v_ref, f32[5,8,16,256]{3,2,1,0:T(8,128)S(1)} %get-tuple-element.25.source_ref, f32[8,16,256]{2,1,0:T(8,128)S(1)} %get-tuple-element.26.diagonal_ref), custom_call_target="tpu_custom_call" | custom-call | tf_op jit(solution)/shard_map/inner_residual/pallas_call | solution.py:435
  46.8 2.0 %collective-permute-done.13.other_ref = f32[1,128]{1,0:T(1,128)S(1)} collective-permute-done((f32[1,128]{1,0:T(1,128)S(1)}, f32[1,128]{1,0:T(1,128)S(1)}, u32[]{:S(2)}, u32[]{:S(2)}) %collective-permute-start.13) | collective-permute-done | bytes 544 | tf_op jit(solution)/shard_map/ppermute | solution.py:433
  48.8 0.8 %finish.1 = f32[1,32]{1,0:T(1,128)} custom-call(f32[1,128]{1,0:T(1,128)S(1)} %add.7.part_ref, f32[1,128]{1,0:T(1,128)S(1)} %collective-permute-done.13.other_ref), custom_call_target="tpu_custom_call" | custom-call | tf_op jit(solution)/shard_map/finish/pallas_call | solution.py:450
  49.6 1.0 %outer_residual.1 = f32[5,8,16,256]{3,2,1,0:T(8,128)} custom-call(f32[151,128]{1,0:T(8,128)S(1)} %get-tuple-element.23.blocks_ref, f32[5,8,16,256]{3,2,1,0:T(8,128)S(1)} %get-tuple-element.37.inner_ref, f32[5,16,256]{2,1,0:T(8,128)S(1)} %collective-permute-done.7.xa_ref, f32[5,16,256]{2,1,0:T(8,128)S(1)} %collective-permute-done.8.xb_ref, ...), custom_call_target="tpu_custom_call" | custom-call | tf_op jit(solution)/shard_map/outer_residual/pallas_call | solution.py:443
  (24 shorter events, 0.1 us)
Async XLA Ops:
  2.2 12.1 %collective-permute-start.3 = (f32[11,8,256]{2,1,0:T(8,128)S(1)}, f32[11,8,256]{2,1,0:T(8,128)S(1)}, u32[]{:S(2)}, u32[]{:S(2)}) collective-permute-start(f32[11,8,256]{2,1,0:T(8,128)S(1)} %get-tuple-element.30.edge_ref), channel_id=1, source_target_pairs={{0,15},{1,2},{2,1},{3,4},{4,3},{5,6},{6,5},{7,8},{8,7},{9,10},{10,... | collective-permute-start | bytes 270344 | tf_op jit(solution)/shard_map/ppermute | solution.py:349
  4.2 10.1 %collective-permute-start = (f32[5,16,256]{2,1,0:T(8,128)S(1)}, f32[5,16,256]{2,1,0:T(8,128)S(1)}, u32[]{:S(2)}, u32[]{:S(2)}) collective-permute-start(f32[5,16,256]{2,1,0:T(8,128)S(1)} %get-tuple-element.27), channel_id=1, source_target_pairs={{0,16},{16,0},{32,48},{48,32},{64,80},{80,64},{96,112},{112,96},{1... | collective-permute-start | bytes 245768 | tf_op jit(solution)/shard_map/ppermute | solution.py:351
  4.2 10.1 %collective-permute-start.1 = (f32[5,16,256]{2,1,0:T(8,128)S(1)}, f32[5,16,256]{2,1,0:T(8,128)S(1)}, u32[]{:S(2)}, u32[]{:S(2)}) collective-permute-start(f32[5,16,256]{2,1,0:T(8,128)S(1)} %get-tuple-element.28), channel_id=1, source_target_pairs={{0,112},{16,32},{32,16},{48,64},{64,48},{80,96},{96,80},{112,0},{1... | collective-permute-start | bytes 245768 | tf_op jit(solution)/shard_map/ppermute | solution.py:350
  7.4 7.0 %collective-permute-start.2 = (f32[5,8,256]{2,1,0:T(8,128)S(1)}, f32[5,8,256]{2,1,0:T(8,128)S(1)}, u32[]{:S(2)}, u32[]{:S(2)}) collective-permute-start(f32[5,8,256]{2,1,0:T(8,128)S(1)} %get-tuple-element.29), channel_id=1, source_target_pairs={{0,1},{1,0},{2,3},{3,2},{4,5},{5,4},{6,7},{7,6},{8,9},{9,8},{10,11... | collective-permute-start | bytes 122888 | tf_op jit(solution)/shard_map/ppermute | solution.py:352
  14.7 5.3 %collective-permute-start.4 = (f32[88,256]{1,0:T(8,128)S(1)}, f32[88,256]{1,0:T(8,128)S(1)}, u32[]{:S(2)}, u32[]{:S(2)}) collective-permute-start(f32[88,256]{1,0:T(8,128)S(1)} %get-tuple-element.32), channel_id=1, source_target_pairs={{0,16},{16,0},{32,48},{48,32},{64,80},{80,64},{96,112},{112,96},{1... | collective-permute-start | bytes 270344 | tf_op jit(solution)/shard_map/ppermute | solution.py:351
  14.8 5.3 %collective-permute-start.5 = (f32[88,256]{1,0:T(8,128)S(1)}, f32[88,256]{1,0:T(8,128)S(1)}, u32[]{:S(2)}, u32[]{:S(2)}) collective-permute-start(f32[88,256]{1,0:T(8,128)S(1)} %get-tuple-element.33), channel_id=1, source_target_pairs={{0,112},{16,32},{32,16},{48,64},{64,48},{80,96},{96,80},{112,0},{1... | collective-permute-start | bytes 270344 | tf_op jit(solution)/shard_map/ppermute | solution.py:350
  16.0 4.0 %collective-permute-start.6 = (f32[5,8,256]{2,1,0:T(8,128)S(1)}, f32[5,8,256]{2,1,0:T(8,128)S(1)}, u32[]{:S(2)}, u32[]{:S(2)}) collective-permute-start(f32[5,8,256]{2,1,0:T(8,128)S(1)} %get-tuple-element.34), channel_id=1, source_target_pairs={{0,1},{1,0},{2,3},{3,2},{4,5},{5,4},{6,7},{7,6},{8,9},{9,8},{10,11... | collective-permute-start | bytes 122888 | tf_op jit(solution)/shard_map/ppermute | solution.py:352
  17.9 2.1 %copy-start = (bf16[1,5,8,16,256]{4,3,2,1,0:T(8,128)(2,1)S(1)}, bf16[1,5,8,16,256]{4,3,2,1,0:T(8,128)(2,1)}, u32[]{:S(2)}) copy-start(bf16[1,5,8,16,256]{4,3,2,1,0:T(8,128)(2,1)} %param.13) | copy-start | bytes 983044
  17.9 2.1 %copy-start.1 = (s32[8,16,256]{2,1,0:T(8,128)S(1)}, s32[8,16,256]{2,1,0:T(8,128)}, u32[]{:S(2)}) copy-start(s32[8,16,256]{2,1,0:T(8,128)} %mask_ref.1) | copy-start | bytes 393220
  17.9 2.1 %copy-start.2 = (f32[256,128]{1,0:T(8,128)S(1)}, f32[256,128]{1,0:T(8,128)}, u32[]{:S(2)}) copy-start(f32[256,128]{1,0:T(8,128)} %basis_ref.1) | copy-start | bytes 393220
  17.9 2.1 %copy-start.3 = (s32[8,16]{1,0:T(8,128)S(1)}, s32[8,16]{1,0:T(8,128)}, u32[]{:S(2)}) copy-start(s32[8,16]{1,0:T(8,128)} %slot_ref.1) | copy-start | bytes 1540
  31.5 7.2 %collective-permute-start.11 = (f32[1,128]{1,0:T(1,128)S(1)}, f32[1,128]{1,0:T(1,128)S(1)}, u32[]{:S(2)}, u32[]{:S(2)}) collective-permute-start(f32[1,128]{1,0:T(1,128)S(1)} %bitcast.18), channel_id=1, source_target_pairs={{0,1},{1,0},{2,3},{3,2},{128,129},{129,128},{130,131},{131,130},{4... | collective-permute-start | bytes 1544 | tf_op jit(solution)/shard_map/ppermute | solution.py:429
  33.6 16.1 %collective-permute-start.7 = (f32[5,16,256]{2,1,0:T(8,128)S(1)}, f32[5,16,256]{2,1,0:T(8,128)S(1)}, u32[]{:S(2)}, u32[]{:S(2)}) collective-permute-start(f32[5,16,256]{2,1,0:T(8,128)S(1)} %get-tuple-element.38), channel_id=1, source_target_pairs={{0,16},{16,0},{32,48},{48,32},{64,80},{80,64},{96,112},{112,96},{1... | collective-permute-start | bytes 245768 | tf_op jit(solution)/shard_map/ppermute | solution.py:351
  33.6 16.1 %collective-permute-start.8 = (f32[5,16,256]{2,1,0:T(8,128)S(1)}, f32[5,16,256]{2,1,0:T(8,128)S(1)}, u32[]{:S(2)}, u32[]{:S(2)}) collective-permute-start(f32[5,16,256]{2,1,0:T(8,128)S(1)} %get-tuple-element.39), channel_id=1, source_target_pairs={{0,112},{16,32},{32,16},{48,64},{64,48},{80,96},{96,80},{112,0},{1... | collective-permute-start | bytes 245768 | tf_op jit(solution)/shard_map/ppermute | solution.py:350
  34.8 14.8 %collective-permute-start.10 = (f32[5,8,256]{2,1,0:T(8,128)S(1)}, f32[5,8,256]{2,1,0:T(8,128)S(1)}, u32[]{:S(2)}, u32[]{:S(2)}) collective-permute-start(f32[5,8,256]{2,1,0:T(8,128)S(1)} %get-tuple-element.41), channel_id=1, source_target_pairs={{0,15},{1,2},{2,1},{3,4},{4,3},{5,6},{6,5},{7,8},{8,7},{9,10},{10,... | collective-permute-start | bytes 122888 | tf_op jit(solution)/shard_map/ppermute | solution.py:349
  37.0 12.6 %collective-permute-start.9 = (f32[5,8,256]{2,1,0:T(8,128)S(1)}, f32[5,8,256]{2,1,0:T(8,128)S(1)}, u32[]{:S(2)}, u32[]{:S(2)}) collective-permute-start(f32[5,8,256]{2,1,0:T(8,128)S(1)} %get-tuple-element.40), channel_id=1, source_target_pairs={{0,1},{1,0},{2,3},{3,2},{4,5},{5,4},{6,7},{7,6},{8,9},{9,8},{10,11... | collective-permute-start | bytes 122888 | tf_op jit(solution)/shard_map/ppermute | solution.py:352
  38.7 3.6 %collective-permute-start.12 = (f32[1,128]{1,0:T(1,128)S(1)}, f32[1,128]{1,0:T(1,128)S(1)}, u32[]{:S(2)}, u32[]{:S(2)}) collective-permute-start(f32[1,128]{1,0:T(1,128)S(1)} %bitcast_add_fusion), channel_id=1, source_target_pairs={{0,131},{1,2},{2,1},{3,128},{128,3},{129,130},{130,129},{131,0},{4... | collective-permute-start | bytes 1544 | tf_op jit(solution)/shard_map/ppermute | solution.py:431
  42.2 6.6 %collective-permute-start.13 = (f32[1,128]{1,0:T(1,128)S(1)}, f32[1,128]{1,0:T(1,128)S(1)}, u32[]{:S(2)}, u32[]{:S(2)}) collective-permute-start(f32[1,128]{1,0:T(1,128)S(1)} %add.7.part_ref), channel_id=1, source_target_pairs={{0,3},{3,0},{1,130},{130,1},{2,129},{129,2},{128,131},{131,128},{4... | collective-permute-start | bytes 1544 | tf_op jit(solution)/shard_map/ppermute | solution.py:433

commit v5 on v4

--- a/solution.py
+++ b/solution.py
@@ -69,7 +69,7 @@
 
 def load_kernel(
     blocks_hbm, weights_hbm, v_hbm, source_hbm, diagonal_hbm,
-    v_ref, source_ref, diagonal_ref, table_ref, xa_ref, xb_ref, ya_ref, yb_ref,
+    v_ref, source_ref, diagonal_ref, table_ref, yb_ref,
     blocks_ref, weights_ref, next_ref, wanted_ref, sems,
 ):
     pairs = (
@@ -82,7 +82,7 @@
     copies = [pltpu.make_async_copy(a, b, sems.at[i]) for i, (a, b) in enumerate(pairs)]
     for copy in copies:
         copy.start()
-    nvar, nx, ny, nz = v_ref.shape
+    nvar, _, _, _ = v_ref.shape
     for copy in copies[:2]:
         copy.wait()
     for d in range(6):
@@ -97,19 +97,37 @@
     table_ref[last : last + 1, :] = (one * mine.astype(jnp.float32)) / (one * total)
     for copy in copies[2:]:
         copy.wait()
-    write_sides(lambda k, x: v_ref[k, x], nvar, nx, ny, xa_ref, xb_ref, ya_ref, yb_ref)
     even = lax.rem(position()[1], 2) == 0
+    relax_edge(table_ref, v_ref, source_ref, diagonal_ref, even, yb_ref, next_ref, wanted_ref)
+
+
+def other_sides_kernel(
+    table_ref, v_ref, source_ref, diagonal_ref, xa_ref, xb_ref, ya_ref, next_ref, wanted_ref
+):
+    nvar, nx, _, _ = v_ref.shape
+    gx, yz = position()
+    gx_even, yz_even = lax.rem(gx, 2) == 0, lax.rem(yz, 2) == 0
+    for k in range(nvar):
+        low, high = v_ref[k, 0], v_ref[k, nx - 1]
+        xa_ref[k] = jnp.where(gx_even, high, low)
+        xb_ref[k] = jnp.where(gx_even, low, high)
+    relax_edge(table_ref, v_ref, source_ref, diagonal_ref, ~yz_even, ya_ref, next_ref, wanted_ref)
+
+
+def relax_edge(table_ref, v_ref, source_ref, diagonal_ref, is_low, out_ref, next_ref, wanted_ref):
+    nvar, nx, ny, nz = v_ref.shape
     for x in range(nx):
         here = slice(x, x + 1)
-        yb_ref[2 * nvar, here, :] = jnp.where(even, diagonal_ref[x, 0:1], diagonal_ref[x, ny - 1 : ny])
+        out_ref[2 * nvar, here, :] = jnp.where(is_low, diagonal_ref[x, 0:1], diagonal_ref[x, ny - 1 : ny])
         for k in range(nvar):
-            next_ref[k, here, :] = jnp.where(even, v_ref[k, x, 1:2], v_ref[k, x, ny - 2 : ny - 1])
-            wanted_ref[k, here, :] = jnp.where(even, source_ref[k, x, 0:1], source_ref[k, x, ny - 1 : ny])
+            out_ref[k, here, :] = jnp.where(is_low, v_ref[k, x, 0:1], v_ref[k, x, ny - 1 : ny])
+            next_ref[k, here, :] = jnp.where(is_low, v_ref[k, x, 1:2], v_ref[k, x, ny - 2 : ny - 1])
+            wanted_ref[k, here, :] = jnp.where(is_low, source_ref[k, x, 0:1], source_ref[k, x, ny - 1 : ny])
     row = lax.broadcasted_iota(jnp.int32, (nx, nz), 0)
     lane = lax.broadcasted_iota(jnp.int32, (nx, nz), 1)
     sums = [0.0] * nvar
     for e in range(nvar):
-        edge = yb_ref[e]
+        edge = out_ref[e]
         shifted = {
             0: jnp.where(row == nx - 1, 0.0, pltpu.roll(edge, nx - 1, 0)),
             1: jnp.where(row == 0, 0.0, pltpu.roll(edge, 1, 0)),
@@ -121,13 +139,13 @@
             for d, values in shifted.items():
                 sums[k] = sums[k] + coefficient(table_ref, d, e, k, nvar, values.shape) * values
             both = [coefficient(table_ref, d, e, k, nvar, inward.shape) for d in (2, 3)]
-            sums[k] = sums[k] + jnp.where(even, both[0], both[1]) * inward
-    diagonal = yb_ref[2 * nvar]
+            sums[k] = sums[k] + jnp.where(is_low, both[0], both[1]) * inward
+    diagonal = out_ref[2 * nvar]
     scale = RELAXATION / diagonal
     for k in range(nvar):
-        edge = yb_ref[k]
-        yb_ref[nvar + k] = edge + scale * (wanted_ref[k] - diagonal * edge + sums[k])
-    yb_ref[2 * nvar] = scale
+        edge = out_ref[k]
+        out_ref[nvar + k] = edge + scale * (wanted_ref[k] - diagonal * edge + sums[k])
+    out_ref[2 * nvar] = scale
 
 
 def neighbour_sums(v_ref, blocks_ref, x):
@@ -228,14 +246,12 @@
 
 
 def outer_sweep_kernel(
-    blocks_ref, inner_ref, diagonal_ref, xa_ref, xb_ref, ya_ref, yb_ref,
-    out_ref, next_xa_ref, next_xb_ref, next_ya_ref,
+    blocks_ref, inner_ref, diagonal_ref, xa_ref, xb_ref, ya_ref, yb_ref, out_ref, next_xa_ref, next_xb_ref,
 ):
     nvar, nx, ny, nz = inner_ref.shape
     halo = [reader(ref) for ref in (xa_ref, xb_ref, ya_ref, yb_ref)]
     add_halo(blocks_ref, inner_ref, diagonal_ref, *halo, out_ref)
-    gx, yz = position()
-    gx_even, yz_even = lax.rem(gx, 2) == 0, lax.rem(yz, 2) == 0
+    gx_even = lax.rem(position()[0], 2) == 0
     top = nvar * ny
     next_xa_ref[top:, :] = jnp.zeros((next_xa_ref.shape[0] - top, nz), jnp.float32)
     next_xb_ref[top:, :] = jnp.zeros((next_xb_ref.shape[0] - top, nz), jnp.float32)
@@ -243,19 +259,16 @@
         low, high = out_ref[k, 0], out_ref[k, nx - 1]
         next_xa_ref[k * ny : (k + 1) * ny, :] = jnp.where(gx_even, high, low)
         next_xb_ref[k * ny : (k + 1) * ny, :] = jnp.where(gx_even, low, high)
-        low, high = yb_ref[k, 0:1], yb_ref[k, nx - 1 : nx]
-        next_xa_ref[top + k : top + k + 1, :] = jnp.where(gx_even, high, low)
-        next_xb_ref[top + k : top + k + 1, :] = jnp.where(gx_even, low, high)
-        for x in range(nx):
-            slab = out_ref[k, x]
-            next_ya_ref[k, x : x + 1, :] = jnp.where(yz_even, slab[ny - 1 : ny], slab[0:1])
-
-
-def complete_far_row(blocks_ref, xa_ref, xb_ref, far_ref, edge_ref, out_ref):
+        for start, ref in ((top, ya_ref), (top + nvar, yb_ref)):
+            low, high = ref[k, 0:1], ref[k, nx - 1 : nx]
+            next_xa_ref[start + k : start + k + 1, :] = jnp.where(gx_even, high, low)
+            next_xb_ref[start + k : start + k + 1, :] = jnp.where(gx_even, low, high)
+
+
+def complete_row(blocks_ref, xa_ref, xb_ref, top, is_low, far_ref, edge_ref, out_ref):
     nvar, nx, nz = out_ref.shape
-    top = xa_ref.shape[0] - 8
-    gx, yz = position()
-    gx_even, yz_even = lax.rem(gx, 2) == 0, lax.rem(yz, 2) == 0
+    gx = position()[0]
+    gx_even = lax.rem(gx, 2) == 0
     row = lax.broadcasted_iota(jnp.int32, (nx, nz), 0)
     at_low, at_high = (row == 0) & (gx > 0), (row == nx - 1) & (gx < 7)
     sums = [0.0] * nvar
@@ -266,7 +279,7 @@
         high = jnp.where(at_high, jnp.where(gx_even, a, b), 0.0)
         for k in range(nvar):
             both = [coefficient(blocks_ref, d, e, k, nvar, edge.shape) for d in (2, 3)]
-            sums[k] = sums[k] + jnp.where(yz_even, both[0], both[1]) * edge
+            sums[k] = sums[k] + jnp.where(is_low, both[0], both[1]) * edge
             sums[k] = sums[k] + coefficient(blocks_ref, 1, e, k, nvar, edge.shape) * low
             sums[k] = sums[k] + coefficient(blocks_ref, 0, e, k, nvar, edge.shape) * high
     for k in range(nvar):
@@ -274,17 +287,19 @@
 
 
 def last_sweep_kernel(
-    blocks_ref, inner_ref, diagonal_ref, xa_ref, xb_ref, ya_ref, far_ref, edge_ref,
+    blocks_ref, inner_ref, diagonal_ref, xa_ref, xb_ref, ya_ref, yb_ref, sent_ya_ref, sent_yb_ref,
     sensitivity_ref, mask_ref, slot_ref, basis_ref,
-    out_ref, next_xa_ref, next_xb_ref, next_ya_ref, next_yb_ref, gradient_ref, surface_ref, row_ref,
+    out_ref, next_xa_ref, next_xb_ref, next_ya_ref, next_yb_ref, gradient_ref, surface_ref, row_a_ref, row_b_ref,
 ):
     nvar, nx, ny, _ = inner_ref.shape
-    complete_far_row(blocks_ref, xa_ref, xb_ref, far_ref, edge_ref, row_ref)
+    even, top = lax.rem(position()[1], 2) == 0, nvar * ny
+    complete_row(blocks_ref, xa_ref, xb_ref, top, ~even, ya_ref, sent_ya_ref, row_a_ref)
+    complete_row(blocks_ref, xa_ref, xb_ref, top + nvar, even, yb_ref, sent_yb_ref, row_b_ref)
     add_halo(
         blocks_ref, inner_ref, diagonal_ref,
         lambda e: xa_ref[e * ny : (e + 1) * ny, :],
         lambda e: xb_ref[e * ny : (e + 1) * ny, :],
-        reader(ya_ref), reader(row_ref), out_ref,
+        reader(row_a_ref), reader(row_b_ref), out_ref,
     )
     write_sides(
         lambda k, x: out_ref[k, x], nvar, nx, ny, next_xa_ref, next_xb_ref, next_ya_ref, next_yb_ref
@@ -327,16 +342,6 @@
     add_halo(blocks_ref, inner_ref, None, *halo, out_ref)
 
 
-def finish_kernel(part_ref, other_ref, piece_ref):
-    size = piece_ref.shape[1]
-    total = part_ref[...] + other_ref[...]
-    which = lax.axis_index("yz_1")
-    piece = total[:, :size]
-    for i in range(1, total.shape[1] // size):
-        piece = jnp.where(which == i, total[:, i * size : (i + 1) * size], piece)
-    piece_ref[...] = piece
-
-
 def swap_a(n):
     return [(i, i ^ 1) for i in range(n)]
 
@@ -345,12 +350,12 @@
     return [(i, (((i + 1) ^ 1) - 1) % n) for i in range(n)]
 
 
-def exchange(xa, xb, ya, yb=None):
+def exchange(xa, xb, ya=None, yb=None):
     far = [] if yb is None else [lax.ppermute(yb, YZ, swap_b(16))]
+    near = [] if ya is None else [lax.ppermute(ya, YZ, swap_a(16))]
     chip = lax.ppermute(xb, GX, swap_b(8))
     core = lax.ppermute(xa, GX, swap_a(8))
-    near = lax.ppermute(ya, YZ, swap_a(16))
-    return [near_core(x) for x in (core, chip, near, *far)]
+    return [near_core(x) for x in (core, chip, *near, *far)]
 
 
 def step(
@@ -371,56 +376,59 @@
     sides = (kept(nvar, ny, nz), kept(nvar, ny, nz), kept(nvar, nx, nz), kept(nvar, nx, nz))
 
     arrays = (flux_blocks.transpose(2, 3, 0, 1), condition_weights, adjoint[0], objective_gradient[0], diagonal)
-    v, source, diagonal, blocks, *first = call(
+    row = kept(2 * nvar + 1, nx, nz)
+    rows_scratch = [pltpu.VMEM((nvar, nx, nz), jnp.float32)] * 2
+    v, source, diagonal, blocks, yb = call(
         load_kernel,
-        out_shape=(
-            field,
-            field,
-            kept(nx, ny, nz),
-            kept(6 * nvar * nvar + 1, 128),
-            *sides[:3],
-            kept(2 * nvar + 1, nx, nz),
-        ),
+        out_shape=(field, field, kept(nx, ny, nz), kept(6 * nvar * nvar + 1, 128), row),
         in_specs=[HBM] * 5,
-        out_specs=[VMEM] * 8,
+        out_specs=[VMEM] * 5,
         scratch_shapes=[
             pltpu.SMEM((nvar, nvar, 1, 6), jnp.float32),
             pltpu.SMEM(condition_weights.shape, jnp.int32),
-            pltpu.VMEM((nvar, nx, nz), jnp.float32),
-            pltpu.VMEM((nvar, nx, nz), jnp.float32),
+            *rows_scratch,
             pltpu.SemaphoreType.DMA((5,)),
         ],
         name="load",
     )(*(far_from_core(x) for x in arrays))
     v, source, diagonal, blocks = (near_core(x) for x in (v, source, diagonal, blocks))
-    halo = exchange(*first)
+    xa, xb, ya = call(
+        other_sides_kernel,
+        out_shape=(*sides[:2], row),
+        in_specs=[VMEM] * 4,
+        out_specs=[VMEM] * 3,
+        scratch_shapes=rows_scratch,
+        name="other_sides",
+    )(blocks, v, source, diagonal)
+    halo = exchange(xa, xb, ya, yb)
     inner_sweep = call(
         inner_sweep_kernel, out_shape=field, in_specs=[VMEM] * 4, out_specs=VMEM, name="inner_sweep"
     )
     inner = inner_sweep(blocks, v, source, diagonal)
     relaxed, *second = call(
         outer_sweep_kernel,
-        out_shape=(field, kept(nvar * ny + 8, nz), kept(nvar * ny + 8, nz), sides[2]),
+        out_shape=(field, kept(nvar * ny + 16, nz), kept(nvar * ny + 16, nz)),
         in_specs=[VMEM] * 7,
-        out_specs=[VMEM] * 4,
+        out_specs=[VMEM] * 3,
         name="outer_sweep",
     )(blocks, near_core(inner), diagonal, *halo)
-    far, edge = halo[3], near_core(first[3])
+    rows = halo[2], halo[3], near_core(ya), near_core(yb)
 
     halo = exchange(*second)
     inner = inner_sweep(blocks, near_core(relaxed), source, diagonal)
     smoothed, xa, xb, ya, yb, gradient = call(
         last_sweep_kernel,
         out_shape=(field, *sides, kept(NDES // 128, 128)),
-        in_specs=[VMEM] * 12,
+        in_specs=[VMEM] * 13,
         out_specs=[VMEM] * 6,
         scratch_shapes=[
             pltpu.VMEM((nx * ny, nz), jnp.float32),
             pltpu.VMEM((nvar, nx, nz), jnp.float32),
+            pltpu.VMEM((nvar, nx, nz), jnp.float32),
         ],
         name="last_sweep",
     )(
-        blocks, near_core(inner), diagonal, *halo, far, edge,
+        blocks, near_core(inner), diagonal, *halo, *rows,
         sensitivity, mask, near_core(patch_band_slot), basis,
     )
 
@@ -447,9 +455,9 @@
         out_specs=VMEM,
         name="outer_residual",
     )(blocks, near_core(inner), *halo)
-    design_gradient = call(
-        finish_kernel, out_shape=f32(1, 32), in_specs=[VMEM] * 2, out_specs=VMEM, name="finish"
-    )(near_core(total), near_core(other))
+    piece = NDES // 128
+    start = lax.axis_index("yz_1") * piece
+    design_gradient = lax.dynamic_slice(total + other, (0, start), (1, piece))
     return smoothed[None], residual[None], design_gradient.reshape(-1)
 
 

time: 50.9 us -> 58.1 us (1.14)
  the two profiles are of different devices: /device:TPU:32 before, /device:TPU:8 now
where the time goes in v5:
time: 58.1 us; the launch traced here: 57.9 us
  starting transfers between devices  21.3 us (37%)
  waiting for transfers between devices  13.5 us (23%)
  blocking collectives  13.1 us (23%)
  Pallas kernels  8.7 us (15%)
  between operations  0.73 us (1%)
  local copies, waits for them, and re-layouts  0.6 us (1%)
    all_to_all x1, blocking collectives, step(): parts = lax.all_to_all(gradient, SPREAD, 0, 0, tiled=True)  13.1 us
    ppermute x2, starting transfers between devices, exchange(): far = [] if yb is None else [lax.ppermute(yb, YZ, swap_b(16))]  6.63 us
    ppermute x2, waiting for transfers between devices, exchange(): far = [] if yb is None else [lax.ppermute(yb, YZ, swap_b(16))]  6.36 us
    ppermute x1, starting transfers between devices, step(): lax.ppermute(total, RING, [(i, ((i + 1 ^ 1) - 1) % 8) for i in range(8)])  5.11 us
    ppermute x2, starting transfers between devices, exchange(): near = [] if ya is None else [lax.ppermute(ya, YZ, swap_a(16))]  3.83 us
    ppermute x3, starting transfers between devices, exchange(): chip = lax.ppermute(xb, GX, swap_b(8))  3.29 us
    ppermute x3, waiting for transfers between devices, exchange(): chip = lax.ppermute(xb, GX, swap_b(8))  3.01 us
    ppermute x1, waiting for transfers between devices, step(): total = total + lax.ppermute(total, RING, [(i, i ^ 1) for i in range(8)])  2.55 us
  transfers between devices with their start and end apart: 13, of which 6 were waited for; matrix products, arithmetic and copies ran while one was open for 1% of the time, Pallas kernels for 8%

profile of v5, /device:TPU:8, one launch (start us, length us, event | category | flops | bytes accessed | tf_op | source)
XLA Modules:
  0.0 57.9 jit_solution(8644149538481786635)
XLA Ops:
  0.6 1.5 %load.1 = (f32[5,8,16,256]{3,2,1,0:T(8,128)S(1)}, f32[5,8,16,256]{3,2,1,0:T(8,128)S(1)}, f32[8,16,256]{2,1,0:T(8,128)S(1)}, f32[151,128]{1,0:T(8,128)S(1)}, f32[11,8,256]{2,1,0:T(8,128)S(1)}) custom-call(f32[5,5,1,6]{3,2,1,0:T(1,128)} %bitcast.18, s32[2]{0:T(128)} %weights_hbm.1, f32[5,8,16,256]{3,2,1,0:T(8,128)} %bitcast.16, f32[5,8,16,256]{3,2,1,0:T(8,128)} %bitcast.17, ...), custom_call_target="tpu_custom_call" | custom-call | tf_op jit(solution)/shard_map/load/pallas_call | solution.py:381
  2.4 2.0 %collective-permute-start.2 = (f32[11,8,256]{2,1,0:T(8,128)S(1)}, f32[11,8,256]{2,1,0:T(8,128)S(1)}, u32[]{:S(2)}, u32[]{:S(2)}) collective-permute-start(f32[11,8,256]{2,1,0:T(8,128)S(1)} %get-tuple-element.28.sent_ya_ref), channel_id=1, source_target_pairs={{0,1},{1,0},{2,3},{3,2},{4,5},{5,4},{6,7},{7,6},{8,9},{9,8},{10,11... | collective-permute-start | bytes 270344 | tf_op jit(solution)/shard_map/ppermute | solution.py:355
  4.4 5.0 %collective-permute-start.3 = (f32[11,8,256]{2,1,0:T(8,128)S(1)}, f32[11,8,256]{2,1,0:T(8,128)S(1)}, u32[]{:S(2)}, u32[]{:S(2)}) collective-permute-start(f32[11,8,256]{2,1,0:T(8,128)S(1)} %get-tuple-element.29.sent_yb_ref), channel_id=1, source_target_pairs={{0,15},{1,2},{2,1},{3,4},{4,3},{5,6},{6,5},{7,8},{8,7},{9,10},{10,... | collective-permute-start | bytes 270344 | tf_op jit(solution)/shard_map/ppermute | solution.py:354
  9.4 0.6 collective-permute-start.1
  10.0 1.5 %inner_sweep.2.inner_ref = f32[5,8,16,256]{3,2,1,0:T(8,128)S(1)} custom-call(f32[151,128]{1,0:T(8,128)S(1)} %get-tuple-element.22.blocks_ref.table_ref, f32[5,8,16,256]{3,2,1,0:T(8,128)S(1)} %get-tuple-element.23.v_ref, f32[5,8,16,256]{3,2,1,0:T(8,128)S(1)} %get-tuple-element.24.source_ref, f32[8,16,256]{2,1,0:T(8,128)S(1)} %get-tuple-element.25.diagonal_ref), custom_call_target="tpu_custom_call" | custom-call | tf_op jit(solution)/shard_map/inner_sweep/pallas_call | solution.py:407
  11.5 1.8 %collective-permute-done.1.xb_ref = f32[5,16,256]{2,1,0:T(8,128)S(1)} collective-permute-done((f32[5,16,256]{2,1,0:T(8,128)S(1)}, f32[5,16,256]{2,1,0:T(8,128)S(1)}, u32[]{:S(2)}, u32[]{:S(2)}) %collective-permute-start.1) | collective-permute-done | bytes 81952 | tf_op jit(solution)/shard_map/ppermute | solution.py:356
  13.3 0.7 %collective-permute-done.3.yb_ref = f32[11,8,256]{2,1,0:T(8,128)S(1)} collective-permute-done((f32[11,8,256]{2,1,0:T(8,128)S(1)}, f32[11,8,256]{2,1,0:T(8,128)S(1)}, u32[]{:S(2)}, u32[]{:S(2)}) %collective-permute-start.3) | collective-permute-done | bytes 90144 | tf_op jit(solution)/shard_map/ppermute | solution.py:354
  14.4 1.2 %collective-permute-start.5 = (f32[96,256]{1,0:T(8,128)S(1)}, f32[96,256]{1,0:T(8,128)S(1)}, u32[]{:S(2)}, u32[]{:S(2)}) collective-permute-start(f32[96,256]{1,0:T(8,128)S(1)} %get-tuple-element.32), channel_id=1, source_target_pairs={{0,112},{16,32},{32,16},{48,64},{64,48},{80,96},{96,80},{112,0},{1... | collective-permute-start | bytes 294920 | tf_op jit(solution)/shard_map/ppermute | solution.py:356
  15.6 1.6 %inner_sweep.3.inner_ref = f32[5,8,16,256]{3,2,1,0:T(8,128)S(1)} custom-call(f32[151,128]{1,0:T(8,128)S(1)} %get-tuple-element.22.blocks_ref.table_ref, f32[5,8,16,256]{3,2,1,0:T(8,128)S(1)} %get-tuple-element.30.v_ref, f32[5,8,16,256]{3,2,1,0:T(8,128)S(1)} %get-tuple-element.24.source_ref, f32[8,16,256]{2,1,0:T(8,128)S(1)} %get-tuple-element.25.diagonal_ref), custom_call_target="tpu_custom_call" | custom-call | tf_op jit(solution)/shard_map/inner_sweep/pallas_call | solution.py:418
  17.2 1.2 %collective-permute-done.5.xb_ref = f32[96,256]{1,0:T(8,128)S(1)} collective-permute-done((f32[96,256]{1,0:T(8,128)S(1)}, f32[96,256]{1,0:T(8,128)S(1)}, u32[]{:S(2)}, u32[]{:S(2)}) %collective-permute-start.5) | collective-permute-done | bytes 98336 | tf_op jit(solution)/shard_map/ppermute | solution.py:356
  18.4 1.0 %last_sweep.1 = (f32[5,8,16,256]{3,2,1,0:T(8,128)S(1)}, f32[5,16,256]{2,1,0:T(8,128)S(1)}, f32[5,16,256]{2,1,0:T(8,128)S(1)}, f32[5,8,256]{2,1,0:T(8,128)S(1)}, ...) custom-call(f32[151,128]{1,0:T(8,128)S(1)} %get-tuple-element.22.blocks_ref.table_ref, ...), custom_call_target="tpu_custom_call" | custom-call | tf_op jit(solution)/shard_map/last_sweep/pallas_call | solution.py:419
  19.5 13.1 %all_to_all.9 = f32[32,1,128]{2,1,0:T(1,128)S(1)} all-to-all(f32[32,1,128]{2,1,0:T(1,128)S(1)} %bitcast.14), channel_id=1, replica_groups=mesh['cond'=2,'gx_0'=4,'gx_1'=2,'yz_0'=4,'yz_1'=4] {'gx_0','gx_1','yz_0'}, dimensions={0} | all-to-all | bytes 32768 | tf_op jit(solution)/shard_map/all_to_all | solution.py:435
  32.6 1.1 %collective-permute-start.10 = (f32[1,128]{1,0:T(1,128)S(1)}, f32[1,128]{1,0:T(1,128)S(1)}, u32[]{:S(2)}, u32[]{:S(2)}) collective-permute-start(f32[1,128]{1,0:T(1,128)S(1)} %bitcast.19), channel_id=1, source_target_pairs={{0,1},{1,0},{2,3},{3,2},{128,129},{129,128},{130,131},{131,130},{4... | collective-permute-start | bytes 1544 | tf_op jit(solution)/shard_map/ppermute | solution.py:437
  33.7 2.5 %collective-permute-done.10 = f32[1,128]{1,0:T(1,128)S(1)} collective-permute-done((f32[1,128]{1,0:T(1,128)S(1)}, f32[1,128]{1,0:T(1,128)S(1)}, u32[]{:S(2)}, u32[]{:S(2)}) %collective-permute-start.10) | collective-permute-done | bytes 544 | tf_op jit(solution)/shard_map/ppermute | solution.py:437
  36.3 5.1 %collective-permute-start.11 = (f32[1,128]{1,0:T(1,128)S(1)}, f32[1,128]{1,0:T(1,128)S(1)}, u32[]{:S(2)}, u32[]{:S(2)}) collective-permute-start(f32[1,128]{1,0:T(1,128)S(1)} %bitcast_add_fusion), channel_id=1, source_target_pairs={{0,131},{1,2},{2,1},{3,128},{128,3},{129,130},{130,129},{131,0},{4... | collective-permute-start | bytes 1544 | tf_op jit(solution)/shard_map/ppermute | solution.py:439
  41.4 1.5 %collective-permute-done.11 = f32[1,128]{1,0:T(1,128)S(1)} collective-permute-done((f32[1,128]{1,0:T(1,128)S(1)}, f32[1,128]{1,0:T(1,128)S(1)}, u32[]{:S(2)}, u32[]{:S(2)}) %collective-permute-start.11) | collective-permute-done | bytes 544 | tf_op jit(solution)/shard_map/ppermute | solution.py:439
  42.9 1.1 %collective-permute-start.12 = (f32[1,128]{1,0:T(1,128)S(1)}, f32[1,128]{1,0:T(1,128)S(1)}, u32[]{:S(2)}, u32[]{:S(2)}) collective-permute-start(f32[1,128]{1,0:T(1,128)S(1)} %add.13), channel_id=1, source_target_pairs={{0,3},{3,0},{1,130},{130,1},{2,129},{129,2},{128,131},{131,128},{4... | collective-permute-start | bytes 1544 | tf_op jit(solution)/shard_map/ppermute | solution.py:441
  44.0 1.5 %inner_residual.1 = (f32[5,8,16,256]{3,2,1,0:T(8,128)S(1)}, f32[5,8,16,256]{3,2,1,0:T(8,128)}) custom-call(f32[151,128]{1,0:T(8,128)S(1)} %get-tuple-element.22.blocks_ref.table_ref, f32[5,8,16,256]{3,2,1,0:T(8,128)S(1)} %get-tuple-element.33.v_ref, f32[5,8,16,256]{3,2,1,0:T(8,128)S(1)} %get-tuple-element.24.source_ref, ...), custom_call_target="tpu_custom_call" | custom-call | tf_op jit(solution)/shard_map/inner_residual/pallas_call | solution.py:443
  45.7 1.5 %collective-permute-start.7 = (f32[5,16,256]{2,1,0:T(8,128)S(1)}, f32[5,16,256]{2,1,0:T(8,128)S(1)}, u32[]{:S(2)}, u32[]{:S(2)}) collective-permute-start(f32[5,16,256]{2,1,0:T(8,128)S(1)} %get-tuple-element.37), channel_id=1, source_target_pairs={{0,112},{16,32},{32,16},{48,64},{64,48},{80,96},{96,80},{112,0},{1... | collective-permute-start | bytes 245768 | tf_op jit(solution)/shard_map/ppermute | solution.py:356
  47.2 1.8 %collective-permute-start.8 = (f32[5,8,256]{2,1,0:T(8,128)S(1)}, f32[5,8,256]{2,1,0:T(8,128)S(1)}, u32[]{:S(2)}, u32[]{:S(2)}) collective-permute-start(f32[5,8,256]{2,1,0:T(8,128)S(1)} %get-tuple-element.38), channel_id=1, source_target_pairs={{0,1},{1,0},{2,3},{3,2},{4,5},{5,4},{6,7},{7,6},{8,9},{9,8},{10,11... | collective-permute-start | bytes 122888 | tf_op jit(solution)/shard_map/ppermute | solution.py:355
  49.0 1.6 %collective-permute-start.9 = (f32[5,8,256]{2,1,0:T(8,128)S(1)}, f32[5,8,256]{2,1,0:T(8,128)S(1)}, u32[]{:S(2)}, u32[]{:S(2)}) collective-permute-start(f32[5,8,256]{2,1,0:T(8,128)S(1)} %get-tuple-element.39), channel_id=1, source_target_pairs={{0,15},{1,2},{2,1},{3,4},{4,3},{5,6},{6,5},{7,8},{8,7},{9,10},{10,... | collective-permute-start | bytes 122888 | tf_op jit(solution)/shard_map/ppermute | solution.py:354
  50.6 0.6 %dynamic-slice_bitcast_fusion = f32[32]{0:T(128)} fusion(f32[1,128]{1,0:T(1,128)S(1)} %add.14, s32[]{:T(128)S(6)} %select_n.3), kind=kLoop, calls=%fused_computation | loop fusion | bytes 260 | tf_op jit(solution)/shard_map/reshape | solution.py:461
  51.2 5.7 %collective-permute-done.9.yb_ref = f32[5,8,256]{2,1,0:T(8,128)S(1)} collective-permute-done((f32[5,8,256]{2,1,0:T(8,128)S(1)}, f32[5,8,256]{2,1,0:T(8,128)S(1)}, u32[]{:S(2)}, u32[]{:S(2)}) %collective-permute-start.9) | collective-permute-done | bytes 40992 | tf_op jit(solution)/shard_map/ppermute | solution.py:354
  56.9 1.0 %outer_residual.1 = f32[5,8,16,256]{3,2,1,0:T(8,128)} custom-call(f32[151,128]{1,0:T(8,128)S(1)} %get-tuple-element.22.blocks_ref.table_ref, f32[5,8,16,256]{3,2,1,0:T(8,128)S(1)} %get-tuple-element.35.inner_ref, f32[5,16,256]{2,1,0:T(8,128)S(1)} %collective-permute-done.6.xa_ref, f32[5,16,256]{2,1,0:T(8,128)S(1)} %collective-permute-done.7.xb_ref, ...), custom_call_target="tpu_custom_call" | custom-call | tf_op jit(solution)/shard_map/outer_residual/pallas_call | solution.py:451
  (24 shorter events, 0.8 us)
Async XLA Ops:
  2.4 10.9 %collective-permute-start.2 = (f32[11,8,256]{2,1,0:T(8,128)S(1)}, f32[11,8,256]{2,1,0:T(8,128)S(1)}, u32[]{:S(2)}, u32[]{:S(2)}) collective-permute-start(f32[11,8,256]{2,1,0:T(8,128)S(1)} %get-tuple-element.28.sent_ya_ref), channel_id=1, source_target_pairs={{0,1},{1,0},{2,3},{3,2},{4,5},{5,4},{6,7},{7,6},{8,9},{9,8},{10,11... | collective-permute-start | bytes 270344 | tf_op jit(solution)/shard_map/ppermute | solution.py:355
  4.4 9.6 %collective-permute-start.3 = (f32[11,8,256]{2,1,0:T(8,128)S(1)}, f32[11,8,256]{2,1,0:T(8,128)S(1)}, u32[]{:S(2)}, u32[]{:S(2)}) collective-permute-start(f32[11,8,256]{2,1,0:T(8,128)S(1)} %get-tuple-element.29.sent_yb_ref), channel_id=1, source_target_pairs={{0,15},{1,2},{2,1},{3,4},{4,3},{5,6},{6,5},{7,8},{8,7},{9,10},{10,... | collective-permute-start | bytes 270344 | tf_op jit(solution)/shard_map/ppermute | solution.py:354
  9.4 2.1 %collective-permute-start = (f32[5,16,256]{2,1,0:T(8,128)S(1)}, f32[5,16,256]{2,1,0:T(8,128)S(1)}, u32[]{:S(2)}, u32[]{:S(2)}) collective-permute-start(f32[5,16,256]{2,1,0:T(8,128)S(1)} %get-tuple-element.26), channel_id=1, source_target_pairs={{0,16},{16,0},{32,48},{48,32},{64,80},{80,64},{96,112},{112,96},{1... | collective-permute-start | bytes 245768 | tf_op jit(solution)/shard_map/ppermute | solution.py:357
  9.4 3.9 %collective-permute-start.1 = (f32[5,16,256]{2,1,0:T(8,128)S(1)}, f32[5,16,256]{2,1,0:T(8,128)S(1)}, u32[]{:S(2)}, u32[]{:S(2)}) collective-permute-start(f32[5,16,256]{2,1,0:T(8,128)S(1)} %get-tuple-element.27), channel_id=1, source_target_pairs={{0,112},{16,32},{32,16},{48,64},{64,48},{80,96},{96,80},{112,0},{1... | collective-permute-start | bytes 245768 | tf_op jit(solution)/shard_map/ppermute | solution.py:356
  14.2 3.0 %collective-permute-start.4 = (f32[96,256]{1,0:T(8,128)S(1)}, f32[96,256]{1,0:T(8,128)S(1)}, u32[]{:S(2)}, u32[]{:S(2)}) collective-permute-start(f32[96,256]{1,0:T(8,128)S(1)} %get-tuple-element.31), channel_id=1, source_target_pairs={{0,16},{16,0},{32,48},{48,32},{64,80},{80,64},{96,112},{112,96},{1... | collective-permute-start | bytes 294920 | tf_op jit(solution)/shard_map/ppermute | solution.py:357
  14.4 4.1 %collective-permute-start.5 = (f32[96,256]{1,0:T(8,128)S(1)}, f32[96,256]{1,0:T(8,128)S(1)}, u32[]{:S(2)}, u32[]{:S(2)}) collective-permute-start(f32[96,256]{1,0:T(8,128)S(1)} %get-tuple-element.32), channel_id=1, source_target_pairs={{0,112},{16,32},{32,16},{48,64},{64,48},{80,96},{96,80},{112,0},{1... | collective-permute-start | bytes 294920 | tf_op jit(solution)/shard_map/ppermute | solution.py:356
  15.6 2.9 %copy-start = (bf16[1,5,8,16,256]{4,3,2,1,0:T(8,128)(2,1)S(1)}, bf16[1,5,8,16,256]{4,3,2,1,0:T(8,128)(2,1)}, u32[]{:S(2)}) copy-start(bf16[1,5,8,16,256]{4,3,2,1,0:T(8,128)(2,1)} %param.13) | copy-start | bytes 983044
  15.6 2.9 %copy-start.1 = (s32[8,16,256]{2,1,0:T(8,128)S(1)}, s32[8,16,256]{2,1,0:T(8,128)}, u32[]{:S(2)}) copy-start(s32[8,16,256]{2,1,0:T(8,128)} %mask_ref.1) | copy-start | bytes 393220
  15.6 2.9 %copy-start.2 = (f32[256,128]{1,0:T(8,128)S(1)}, f32[256,128]{1,0:T(8,128)}, u32[]{:S(2)}) copy-start(f32[256,128]{1,0:T(8,128)} %basis_ref.1) | copy-start | bytes 393220
  15.6 2.9 %copy-start.3 = (s32[8,16]{1,0:T(8,128)S(1)}, s32[8,16]{1,0:T(8,128)}, u32[]{:S(2)}) copy-start(s32[8,16]{1,0:T(8,128)} %slot_ref.1) | copy-start | bytes 1540
  32.6 3.6 %collective-permute-start.10 = (f32[1,128]{1,0:T(1,128)S(1)}, f32[1,128]{1,0:T(1,128)S(1)}, u32[]{:S(2)}, u32[]{:S(2)}) collective-permute-start(f32[1,128]{1,0:T(1,128)S(1)} %bitcast.19), channel_id=1, source_target_pairs={{0,1},{1,0},{2,3},{3,2},{128,129},{129,128},{130,131},{131,130},{4... | collective-permute-start | bytes 1544 | tf_op jit(solution)/shard_map/ppermute | solution.py:437
  36.3 6.7 %collective-permute-start.11 = (f32[1,128]{1,0:T(1,128)S(1)}, f32[1,128]{1,0:T(1,128)S(1)}, u32[]{:S(2)}, u32[]{:S(2)}) collective-permute-start(f32[1,128]{1,0:T(1,128)S(1)} %bitcast_add_fusion), channel_id=1, source_target_pairs={{0,131},{1,2},{2,1},{3,128},{128,3},{129,130},{130,129},{131,0},{4... | collective-permute-start | bytes 1544 | tf_op jit(solution)/shard_map/ppermute | solution.py:439
  42.9 7.7 %collective-permute-start.12 = (f32[1,128]{1,0:T(1,128)S(1)}, f32[1,128]{1,0:T(1,128)S(1)}, u32[]{:S(2)}, u32[]{:S(2)}) collective-permute-start(f32[1,128]{1,0:T(1,128)S(1)} %add.13), channel_id=1, source_target_pairs={{0,3},{3,0},{1,130},{130,1},{2,129},{129,2},{128,131},{131,128},{4... | collective-permute-start | bytes 1544 | tf_op jit(solution)/shard_map/ppermute | solution.py:441
  45.6 11.4 %collective-permute-start.6 = (f32[5,16,256]{2,1,0:T(8,128)S(1)}, f32[5,16,256]{2,1,0:T(8,128)S(1)}, u32[]{:S(2)}, u32[]{:S(2)}) collective-permute-start(f32[5,16,256]{2,1,0:T(8,128)S(1)} %get-tuple-element.36), channel_id=1, source_target_pairs={{0,16},{16,0},{32,48},{48,32},{64,80},{80,64},{96,112},{112,96},{1... | collective-permute-start | bytes 245768 | tf_op jit(solution)/shard_map/ppermute | solution.py:357
  45.7 11.3 %collective-permute-start.7 = (f32[5,16,256]{2,1,0:T(8,128)S(1)}, f32[5,16,256]{2,1,0:T(8,128)S(1)}, u32[]{:S(2)}, u32[]{:S(2)}) collective-permute-start(f32[5,16,256]{2,1,0:T(8,128)S(1)} %get-tuple-element.37), channel_id=1, source_target_pairs={{0,112},{16,32},{32,16},{48,64},{64,48},{80,96},{96,80},{112,0},{1... | collective-permute-start | bytes 245768 | tf_op jit(solution)/shard_map/ppermute | solution.py:356
  47.2 4.0 %collective-permute-start.8 = (f32[5,8,256]{2,1,0:T(8,128)S(1)}, f32[5,8,256]{2,1,0:T(8,128)S(1)}, u32[]{:S(2)}, u32[]{:S(2)}) collective-permute-start(f32[5,8,256]{2,1,0:T(8,128)S(1)} %get-tuple-element.38), channel_id=1, source_target_pairs={{0,1},{1,0},{2,3},{3,2},{4,5},{5,4},{6,7},{7,6},{8,9},{9,8},{10,11... | collective-permute-start | bytes 122888 | tf_op jit(solution)/shard_map/ppermute | solution.py:355
  49.0 7.9 %collective-permute-start.9 = (f32[5,8,256]{2,1,0:T(8,128)S(1)}, f32[5,8,256]{2,1,0:T(8,128)S(1)}, u32[]{:S(2)}, u32[]{:S(2)}) collective-permute-start(f32[5,8,256]{2,1,0:T(8,128)S(1)} %get-tuple-element.39), channel_id=1, source_target_pairs={{0,15},{1,2},{2,1},{3,4},{4,3},{5,6},{6,5},{7,8},{8,7},{9,10},{10,... | collective-permute-start | bytes 122888 | tf_op jit(solution)/shard_map/ppermute | solution.py:354

commit v6 on v5

--- a/solution.py
+++ b/solution.py
@@ -286,9 +286,26 @@
         out_ref[k] = far_ref[nvar + k] + far_ref[2 * nvar] * sums[k]
 
 
+def select_kernel(slot_ref, onehot_ref):
+    nx, ny = slot_ref.shape
+    slots, patches = onehot_ref.shape
+    pairs = slots // 2
+    wanted = lax.broadcasted_iota(jnp.int32, (slots, patches), 0)
+    wanted = jnp.where(wanted < pairs, 2 * wanted, 2 * (wanted - pairs) + 1)
+    lane = lax.broadcasted_iota(jnp.int32, (ny, patches), 1)
+    repeat = lax.rem(lane, ny) == lax.broadcasted_iota(jnp.int32, (ny, patches), 0)
+    spread = jnp.dot(
+        slot_ref[...].astype(jnp.float32), repeat.astype(jnp.float32), preferred_element_type=jnp.float32
+    )
+    lane = lax.broadcasted_iota(jnp.int32, (nx, patches), 1)
+    own = lax.div(lane, ny) == lax.broadcasted_iota(jnp.int32, (nx, patches), 0)
+    spread = jnp.sum(jnp.where(own, spread, 0.0), axis=0, keepdims=True)
+    onehot_ref[...] = (wanted.astype(jnp.float32) == spread).astype(jnp.float32)
+
+
 def last_sweep_kernel(
     blocks_ref, inner_ref, diagonal_ref, xa_ref, xb_ref, ya_ref, yb_ref, sent_ya_ref, sent_yb_ref,
-    sensitivity_ref, mask_ref, slot_ref, basis_ref,
+    sensitivity_ref, mask_ref, onehot_ref, basis_ref,
     out_ref, next_xa_ref, next_xb_ref, next_ya_ref, next_yb_ref, gradient_ref, surface_ref, row_a_ref, row_b_ref,
 ):
     nvar, nx, ny, _ = inner_ref.shape
@@ -313,21 +330,16 @@
     projected = jnp.dot(
         surface_ref[...], basis_ref[...], precision=HIGHEST, preferred_element_type=jnp.float32
     )
-    patches, band = projected.shape
+    _, band = projected.shape
     half = band // 2
     pairs = NDES // band
-    wanted = lax.broadcasted_iota(jnp.int32, (2 * pairs, patches), 0)
-    wanted = jnp.where(wanted < pairs, 2 * wanted, 2 * (wanted - pairs) + 1)
-    lane = lax.broadcasted_iota(jnp.int32, (ny, patches), 1)
-    repeat = lax.rem(lane, ny) == lax.broadcasted_iota(jnp.int32, (ny, patches), 0)
-    slots = jnp.dot(
-        slot_ref[...].astype(jnp.float32), repeat.astype(jnp.float32), preferred_element_type=jnp.float32
-    )
-    lane = lax.broadcasted_iota(jnp.int32, (nx, patches), 1)
-    own = lax.div(lane, ny) == lax.broadcasted_iota(jnp.int32, (nx, patches), 0)
-    slots = jnp.sum(jnp.where(own, slots, 0.0), axis=0, keepdims=True)
-    onehot = (wanted.astype(jnp.float32) == slots).astype(jnp.float32)
-    by_slot = jnp.dot(onehot, projected, precision=HIGHEST, preferred_element_type=jnp.float32)
+    onehot = onehot_ref[...].astype(jnp.bfloat16)
+    by_slot, rest = None, projected
+    for _ in range(3):
+        part = rest.astype(jnp.bfloat16)
+        rest = rest - part.astype(jnp.float32)
+        term = jnp.dot(onehot, part, preferred_element_type=jnp.float32)
+        by_slot = term if by_slot is None else by_slot + term
     even, odd = by_slot[:pairs], pltpu.roll(by_slot[pairs:], half, 1)
     row = lax.broadcasted_iota(jnp.int32, (pairs, band), 0)
     lane = lax.broadcasted_iota(jnp.int32, (pairs, band), 1)
@@ -416,6 +428,13 @@
 
     halo = exchange(*second)
     inner = inner_sweep(blocks, near_core(relaxed), source, diagonal)
+    onehot = call(
+        select_kernel,
+        out_shape=kept(2 * NDES // 128, nx * ny),
+        in_specs=[VMEM],
+        out_specs=VMEM,
+        name="select",
+    )(near_core(patch_band_slot))
     smoothed, xa, xb, ya, yb, gradient = call(
         last_sweep_kernel,
         out_shape=(field, *sides, kept(NDES // 128, 128)),
@@ -429,7 +448,7 @@
         name="last_sweep",
     )(
         blocks, near_core(inner), diagonal, *halo, *rows,
-        sensitivity, mask, near_core(patch_band_slot), basis,
+        sensitivity, mask, near_core(onehot), basis,
     )
 
     parts = lax.all_to_all(gradient, SPREAD, 0, 0, tiled=True)

time: 58.1 us -> 58.1 us (level)
  no operation moved by 1% of the time
where the time goes in v6:
time: 58.1 us; the launch traced here: 57.9 us
  starting transfers between devices  21.3 us (37%)
  waiting for transfers between devices  13.3 us (23%)
  blocking collectives  13 us (22%)
  Pallas kernels  8.77 us (15%)
  between operations  0.72 us (1%)
  local copies, waits for them, and re-layouts  0.6 us (1%)
    all_to_all x1, blocking collectives, step(): parts = lax.all_to_all(gradient, SPREAD, 0, 0, tiled=True)  13 us
    ppermute x2, starting transfers between devices, exchange(): far = [] if yb is None else [lax.ppermute(yb, YZ, swap_b(16))]  6.63 us
    ppermute x2, waiting for transfers between devices, exchange(): far = [] if yb is None else [lax.ppermute(yb, YZ, swap_b(16))]  6.36 us
    ppermute x1, starting transfers between devices, step(): lax.ppermute(total, RING, [(i, ((i + 1 ^ 1) - 1) % 8) for i in range(8)])  5.11 us
    ppermute x2, starting transfers between devices, exchange(): near = [] if ya is None else [lax.ppermute(ya, YZ, swap_a(16))]  3.83 us
    ppermute x3, starting transfers between devices, exchange(): chip = lax.ppermute(xb, GX, swap_b(8))  3.29 us
    ppermute x3, waiting for transfers between devices, exchange(): chip = lax.ppermute(xb, GX, swap_b(8))  2.86 us
    ppermute x1, waiting for transfers between devices, step(): total = total + lax.ppermute(total, RING, [(i, i ^ 1) for i in range(8)])  2.55 us
  transfers between devices with their start and end apart: 13, of which 6 were waited for; matrix products, arithmetic and copies ran while one was open for 1% of the time, Pallas kernels for 8%

profile of v6, /device:TPU:8, one launch (start us, length us, event | category | flops | bytes accessed | tf_op | source)
XLA Modules:
  0.0 57.9 jit_solution(16843591888892152808)
XLA Ops:
  0.6 1.5 %load.1 = (f32[5,8,16,256]{3,2,1,0:T(8,128)S(1)}, f32[5,8,16,256]{3,2,1,0:T(8,128)S(1)}, f32[8,16,256]{2,1,0:T(8,128)S(1)}, f32[151,128]{1,0:T(8,128)S(1)}, f32[11,8,256]{2,1,0:T(8,128)S(1)}) custom-call(f32[5,5,1,6]{3,2,1,0:T(1,128)} %bitcast.18, s32[2]{0:T(128)} %weights_hbm.1, f32[5,8,16,256]{3,2,1,0:T(8,128)} %bitcast.16, f32[5,8,16,256]{3,2,1,0:T(8,128)} %bitcast.17, ...), custom_call_target="tpu_custom_call" | custom-call | tf_op jit(solution)/shard_map/load/pallas_call | solution.py:393
  2.4 2.0 %collective-permute-start.2 = (f32[11,8,256]{2,1,0:T(8,128)S(1)}, f32[11,8,256]{2,1,0:T(8,128)S(1)}, u32[]{:S(2)}, u32[]{:S(2)}) collective-permute-start(f32[11,8,256]{2,1,0:T(8,128)S(1)} %get-tuple-element.28.sent_ya_ref), channel_id=1, source_target_pairs={{0,1},{1,0},{2,3},{3,2},{4,5},{5,4},{6,7},{7,6},{8,9},{9,8},{10,11... | collective-permute-start | bytes 270344 | tf_op jit(solution)/shard_map/ppermute | solution.py:367
  4.4 5.0 %collective-permute-start.3 = (f32[11,8,256]{2,1,0:T(8,128)S(1)}, f32[11,8,256]{2,1,0:T(8,128)S(1)}, u32[]{:S(2)}, u32[]{:S(2)}) collective-permute-start(f32[11,8,256]{2,1,0:T(8,128)S(1)} %get-tuple-element.29.sent_yb_ref), channel_id=1, source_target_pairs={{0,15},{1,2},{2,1},{3,4},{4,3},{5,6},{6,5},{7,8},{8,7},{9,10},{10,... | collective-permute-start | bytes 270344 | tf_op jit(solution)/shard_map/ppermute | solution.py:366
  9.4 0.6 collective-permute-start.1
  10.0 1.5 %inner_sweep.2.inner_ref = f32[5,8,16,256]{3,2,1,0:T(8,128)S(1)} custom-call(f32[151,128]{1,0:T(8,128)S(1)} %get-tuple-element.22.blocks_ref.table_ref, f32[5,8,16,256]{3,2,1,0:T(8,128)S(1)} %get-tuple-element.23.v_ref, f32[5,8,16,256]{3,2,1,0:T(8,128)S(1)} %get-tuple-element.24.source_ref, f32[8,16,256]{2,1,0:T(8,128)S(1)} %get-tuple-element.25.diagonal_ref), custom_call_target="tpu_custom_call" | custom-call | tf_op jit(solution)/shard_map/inner_sweep/pallas_call | solution.py:419
  11.5 1.8 %collective-permute-done.1.xb_ref = f32[5,16,256]{2,1,0:T(8,128)S(1)} collective-permute-done((f32[5,16,256]{2,1,0:T(8,128)S(1)}, f32[5,16,256]{2,1,0:T(8,128)S(1)}, u32[]{:S(2)}, u32[]{:S(2)}) %collective-permute-start.1) | collective-permute-done | bytes 81952 | tf_op jit(solution)/shard_map/ppermute | solution.py:368
  13.3 0.7 %collective-permute-done.3.yb_ref = f32[11,8,256]{2,1,0:T(8,128)S(1)} collective-permute-done((f32[11,8,256]{2,1,0:T(8,128)S(1)}, f32[11,8,256]{2,1,0:T(8,128)S(1)}, u32[]{:S(2)}, u32[]{:S(2)}) %collective-permute-start.3) | collective-permute-done | bytes 90144 | tf_op jit(solution)/shard_map/ppermute | solution.py:366
  14.4 1.2 %collective-permute-start.5 = (f32[96,256]{1,0:T(8,128)S(1)}, f32[96,256]{1,0:T(8,128)S(1)}, u32[]{:S(2)}, u32[]{:S(2)}) collective-permute-start(f32[96,256]{1,0:T(8,128)S(1)} %get-tuple-element.32), channel_id=1, source_target_pairs={{0,112},{16,32},{32,16},{48,64},{64,48},{80,96},{96,80},{112,0},{1... | collective-permute-start | bytes 294920 | tf_op jit(solution)/shard_map/ppermute | solution.py:368
  15.7 1.6 %inner_sweep.3.inner_ref = f32[5,8,16,256]{3,2,1,0:T(8,128)S(1)} custom-call(f32[151,128]{1,0:T(8,128)S(1)} %get-tuple-element.22.blocks_ref.table_ref, f32[5,8,16,256]{3,2,1,0:T(8,128)S(1)} %get-tuple-element.30.v_ref, f32[5,8,16,256]{3,2,1,0:T(8,128)S(1)} %get-tuple-element.24.source_ref, f32[8,16,256]{2,1,0:T(8,128)S(1)} %get-tuple-element.25.diagonal_ref), custom_call_target="tpu_custom_call" | custom-call | tf_op jit(solution)/shard_map/inner_sweep/pallas_call | solution.py:430
  17.3 1.1 %collective-permute-done.5.xb_ref = f32[96,256]{1,0:T(8,128)S(1)} collective-permute-done((f32[96,256]{1,0:T(8,128)S(1)}, f32[96,256]{1,0:T(8,128)S(1)}, u32[]{:S(2)}, u32[]{:S(2)}) %collective-permute-start.5) | collective-permute-done | bytes 98336 | tf_op jit(solution)/shard_map/ppermute | solution.py:368
  18.4 1.0 %last_sweep.1 = (f32[5,8,16,256]{3,2,1,0:T(8,128)S(1)}, f32[5,16,256]{2,1,0:T(8,128)S(1)}, f32[5,16,256]{2,1,0:T(8,128)S(1)}, f32[5,8,256]{2,1,0:T(8,128)S(1)}, ...) custom-call(f32[151,128]{1,0:T(8,128)S(1)} %get-tuple-element.22.blocks_ref.table_ref, ...), custom_call_target="tpu_custom_call" | custom-call | tf_op jit(solution)/shard_map/last_sweep/pallas_call | solution.py:438
  19.4 13.0 %all_to_all.9 = f32[32,1,128]{2,1,0:T(1,128)S(1)} all-to-all(f32[32,1,128]{2,1,0:T(1,128)S(1)} %bitcast.14), channel_id=1, replica_groups=mesh['cond'=2,'gx_0'=4,'gx_1'=2,'yz_0'=4,'yz_1'=4] {'gx_0','gx_1','yz_0'}, dimensions={0} | all-to-all | bytes 32768 | tf_op jit(solution)/shard_map/all_to_all | solution.py:454
  32.5 1.1 %collective-permute-start.10 = (f32[1,128]{1,0:T(1,128)S(1)}, f32[1,128]{1,0:T(1,128)S(1)}, u32[]{:S(2)}, u32[]{:S(2)}) collective-permute-start(f32[1,128]{1,0:T(1,128)S(1)} %bitcast.19), channel_id=1, source_target_pairs={{0,1},{1,0},{2,3},{3,2},{128,129},{129,128},{130,131},{131,130},{4... | collective-permute-start | bytes 1544 | tf_op jit(solution)/shard_map/ppermute | solution.py:456
  33.6 2.5 %collective-permute-done.10 = f32[1,128]{1,0:T(1,128)S(1)} collective-permute-done((f32[1,128]{1,0:T(1,128)S(1)}, f32[1,128]{1,0:T(1,128)S(1)}, u32[]{:S(2)}, u32[]{:S(2)}) %collective-permute-start.10) | collective-permute-done | bytes 544 | tf_op jit(solution)/shard_map/ppermute | solution.py:456
  36.2 5.1 %collective-permute-start.11 = (f32[1,128]{1,0:T(1,128)S(1)}, f32[1,128]{1,0:T(1,128)S(1)}, u32[]{:S(2)}, u32[]{:S(2)}) collective-permute-start(f32[1,128]{1,0:T(1,128)S(1)} %bitcast_add_fusion), channel_id=1, source_target_pairs={{0,131},{1,2},{2,1},{3,128},{128,3},{129,130},{130,129},{131,0},{4... | collective-permute-start | bytes 1544 | tf_op jit(solution)/shard_map/ppermute | solution.py:458
  41.3 1.5 %collective-permute-done.11 = f32[1,128]{1,0:T(1,128)S(1)} collective-permute-done((f32[1,128]{1,0:T(1,128)S(1)}, f32[1,128]{1,0:T(1,128)S(1)}, u32[]{:S(2)}, u32[]{:S(2)}) %collective-permute-start.11) | collective-permute-done | bytes 544 | tf_op jit(solution)/shard_map/ppermute | solution.py:458
  42.8 1.1 %collective-permute-start.12 = (f32[1,128]{1,0:T(1,128)S(1)}, f32[1,128]{1,0:T(1,128)S(1)}, u32[]{:S(2)}, u32[]{:S(2)}) collective-permute-start(f32[1,128]{1,0:T(1,128)S(1)} %add.13), channel_id=1, source_target_pairs={{0,3},{3,0},{1,130},{130,1},{2,129},{129,2},{128,131},{131,128},{4... | collective-permute-start | bytes 1544 | tf_op jit(solution)/shard_map/ppermute | solution.py:460
  43.9 1.5 %inner_residual.1 = (f32[5,8,16,256]{3,2,1,0:T(8,128)S(1)}, f32[5,8,16,256]{3,2,1,0:T(8,128)}) custom-call(f32[151,128]{1,0:T(8,128)S(1)} %get-tuple-element.22.blocks_ref.table_ref, f32[5,8,16,256]{3,2,1,0:T(8,128)S(1)} %get-tuple-element.33.v_ref, f32[5,8,16,256]{3,2,1,0:T(8,128)S(1)} %get-tuple-element.24.source_ref, ...), custom_call_target="tpu_custom_call" | custom-call | tf_op jit(solution)/shard_map/inner_residual/pallas_call | solution.py:462
  45.6 1.5 %collective-permute-start.7 = (f32[5,16,256]{2,1,0:T(8,128)S(1)}, f32[5,16,256]{2,1,0:T(8,128)S(1)}, u32[]{:S(2)}, u32[]{:S(2)}) collective-permute-start(f32[5,16,256]{2,1,0:T(8,128)S(1)} %get-tuple-element.37), channel_id=1, source_target_pairs={{0,112},{16,32},{32,16},{48,64},{64,48},{80,96},{96,80},{112,0},{1... | collective-permute-start | bytes 245768 | tf_op jit(solution)/shard_map/ppermute | solution.py:368
  47.1 1.8 %collective-permute-start.8 = (f32[5,8,256]{2,1,0:T(8,128)S(1)}, f32[5,8,256]{2,1,0:T(8,128)S(1)}, u32[]{:S(2)}, u32[]{:S(2)}) collective-permute-start(f32[5,8,256]{2,1,0:T(8,128)S(1)} %get-tuple-element.38), channel_id=1, source_target_pairs={{0,1},{1,0},{2,3},{3,2},{4,5},{5,4},{6,7},{7,6},{8,9},{9,8},{10,11... | collective-permute-start | bytes 122888 | tf_op jit(solution)/shard_map/ppermute | solution.py:367
  48.9 1.6 %collective-permute-start.9 = (f32[5,8,256]{2,1,0:T(8,128)S(1)}, f32[5,8,256]{2,1,0:T(8,128)S(1)}, u32[]{:S(2)}, u32[]{:S(2)}) collective-permute-start(f32[5,8,256]{2,1,0:T(8,128)S(1)} %get-tuple-element.39), channel_id=1, source_target_pairs={{0,15},{1,2},{2,1},{3,4},{4,3},{5,6},{6,5},{7,8},{8,7},{9,10},{10,... | collective-permute-start | bytes 122888 | tf_op jit(solution)/shard_map/ppermute | solution.py:366
  50.5 0.6 %dynamic-slice_bitcast_fusion = f32[32]{0:T(128)} fusion(f32[1,128]{1,0:T(1,128)S(1)} %add.14, s32[]{:T(128)S(6)} %select_n.3), kind=kLoop, calls=%fused_computation | loop fusion | bytes 260 | tf_op jit(solution)/shard_map/reshape | solution.py:480
  51.1 5.7 %collective-permute-done.9.yb_ref = f32[5,8,256]{2,1,0:T(8,128)S(1)} collective-permute-done((f32[5,8,256]{2,1,0:T(8,128)S(1)}, f32[5,8,256]{2,1,0:T(8,128)S(1)}, u32[]{:S(2)}, u32[]{:S(2)}) %collective-permute-start.9) | collective-permute-done | bytes 40992 | tf_op jit(solution)/shard_map/ppermute | solution.py:366
  56.8 1.0 %outer_residual.1 = f32[5,8,16,256]{3,2,1,0:T(8,128)} custom-call(f32[151,128]{1,0:T(8,128)S(1)} %get-tuple-element.22.blocks_ref.table_ref, f32[5,8,16,256]{3,2,1,0:T(8,128)S(1)} %get-tuple-element.35.inner_ref, f32[5,16,256]{2,1,0:T(8,128)S(1)} %collective-permute-done.6.xa_ref, f32[5,16,256]{2,1,0:T(8,128)S(1)} %collective-permute-done.7.xb_ref, ...), custom_call_target="tpu_custom_call" | custom-call | tf_op jit(solution)/shard_map/outer_residual/pallas_call | solution.py:470
  (25 shorter events, 0.9 us)
Async XLA Ops:
  2.4 10.9 %collective-permute-start.2 = (f32[11,8,256]{2,1,0:T(8,128)S(1)}, f32[11,8,256]{2,1,0:T(8,128)S(1)}, u32[]{:S(2)}, u32[]{:S(2)}) collective-permute-start(f32[11,8,256]{2,1,0:T(8,128)S(1)} %get-tuple-element.28.sent_ya_ref), channel_id=1, source_target_pairs={{0,1},{1,0},{2,3},{3,2},{4,5},{5,4},{6,7},{7,6},{8,9},{9,8},{10,11... | collective-permute-start | bytes 270344 | tf_op jit(solution)/shard_map/ppermute | solution.py:367
  4.4 9.6 %collective-permute-start.3 = (f32[11,8,256]{2,1,0:T(8,128)S(1)}, f32[11,8,256]{2,1,0:T(8,128)S(1)}, u32[]{:S(2)}, u32[]{:S(2)}) collective-permute-start(f32[11,8,256]{2,1,0:T(8,128)S(1)} %get-tuple-element.29.sent_yb_ref), channel_id=1, source_target_pairs={{0,15},{1,2},{2,1},{3,4},{4,3},{5,6},{6,5},{7,8},{8,7},{9,10},{10,... | collective-permute-start | bytes 270344 | tf_op jit(solution)/shard_map/ppermute | solution.py:366
  9.4 2.1 %collective-permute-start = (f32[5,16,256]{2,1,0:T(8,128)S(1)}, f32[5,16,256]{2,1,0:T(8,128)S(1)}, u32[]{:S(2)}, u32[]{:S(2)}) collective-permute-start(f32[5,16,256]{2,1,0:T(8,128)S(1)} %get-tuple-element.26), channel_id=1, source_target_pairs={{0,16},{16,0},{32,48},{48,32},{64,80},{80,64},{96,112},{112,96},{1... | collective-permute-start | bytes 245768 | tf_op jit(solution)/shard_map/ppermute | solution.py:369
  9.4 3.9 %collective-permute-start.1 = (f32[5,16,256]{2,1,0:T(8,128)S(1)}, f32[5,16,256]{2,1,0:T(8,128)S(1)}, u32[]{:S(2)}, u32[]{:S(2)}) collective-permute-start(f32[5,16,256]{2,1,0:T(8,128)S(1)} %get-tuple-element.27), channel_id=1, source_target_pairs={{0,112},{16,32},{32,16},{48,64},{64,48},{80,96},{96,80},{112,0},{1... | collective-permute-start | bytes 245768 | tf_op jit(solution)/shard_map/ppermute | solution.py:368
  14.0 1.6 %copy-start.3 = (s32[8,16]{1,0:T(8,128)S(1)}, s32[8,16]{1,0:T(8,128)}, u32[]{:S(2)}) copy-start(s32[8,16]{1,0:T(8,128)} %slot_ref.1) | copy-start | bytes 1540
  14.2 3.1 %collective-permute-start.4 = (f32[96,256]{1,0:T(8,128)S(1)}, f32[96,256]{1,0:T(8,128)S(1)}, u32[]{:S(2)}, u32[]{:S(2)}) collective-permute-start(f32[96,256]{1,0:T(8,128)S(1)} %get-tuple-element.31), channel_id=1, source_target_pairs={{0,16},{16,0},{32,48},{48,32},{64,80},{80,64},{96,112},{112,96},{1... | collective-permute-start | bytes 294920 | tf_op jit(solution)/shard_map/ppermute | solution.py:369
  14.4 4.1 %collective-permute-start.5 = (f32[96,256]{1,0:T(8,128)S(1)}, f32[96,256]{1,0:T(8,128)S(1)}, u32[]{:S(2)}, u32[]{:S(2)}) collective-permute-start(f32[96,256]{1,0:T(8,128)S(1)} %get-tuple-element.32), channel_id=1, source_target_pairs={{0,112},{16,32},{32,16},{48,64},{64,48},{80,96},{96,80},{112,0},{1... | collective-permute-start | bytes 294920 | tf_op jit(solution)/shard_map/ppermute | solution.py:368
  15.7 2.7 %copy-start = (bf16[1,5,8,16,256]{4,3,2,1,0:T(8,128)(2,1)S(1)}, bf16[1,5,8,16,256]{4,3,2,1,0:T(8,128)(2,1)}, u32[]{:S(2)}) copy-start(bf16[1,5,8,16,256]{4,3,2,1,0:T(8,128)(2,1)} %param.13) | copy-start | bytes 983044
  15.7 2.7 %copy-start.1 = (s32[8,16,256]{2,1,0:T(8,128)S(1)}, s32[8,16,256]{2,1,0:T(8,128)}, u32[]{:S(2)}) copy-start(s32[8,16,256]{2,1,0:T(8,128)} %mask_ref.1) | copy-start | bytes 393220
  15.7 2.7 %copy-start.2 = (f32[256,128]{1,0:T(8,128)S(1)}, f32[256,128]{1,0:T(8,128)}, u32[]{:S(2)}) copy-start(f32[256,128]{1,0:T(8,128)} %basis_ref.1) | copy-start | bytes 393220
  32.5 3.6 %collective-permute-start.10 = (f32[1,128]{1,0:T(1,128)S(1)}, f32[1,128]{1,0:T(1,128)S(1)}, u32[]{:S(2)}, u32[]{:S(2)}) collective-permute-start(f32[1,128]{1,0:T(1,128)S(1)} %bitcast.19), channel_id=1, source_target_pairs={{0,1},{1,0},{2,3},{3,2},{128,129},{129,128},{130,131},{131,130},{4... | collective-permute-start | bytes 1544 | tf_op jit(solution)/shard_map/ppermute | solution.py:456
  36.2 6.7 %collective-permute-start.11 = (f32[1,128]{1,0:T(1,128)S(1)}, f32[1,128]{1,0:T(1,128)S(1)}, u32[]{:S(2)}, u32[]{:S(2)}) collective-permute-start(f32[1,128]{1,0:T(1,128)S(1)} %bitcast_add_fusion), channel_id=1, source_target_pairs={{0,131},{1,2},{2,1},{3,128},{128,3},{129,130},{130,129},{131,0},{4... | collective-permute-start | bytes 1544 | tf_op jit(solution)/shard_map/ppermute | solution.py:458
  42.8 7.7 %collective-permute-start.12 = (f32[1,128]{1,0:T(1,128)S(1)}, f32[1,128]{1,0:T(1,128)S(1)}, u32[]{:S(2)}, u32[]{:S(2)}) collective-permute-start(f32[1,128]{1,0:T(1,128)S(1)} %add.13), channel_id=1, source_target_pairs={{0,3},{3,0},{1,130},{130,1},{2,129},{129,2},{128,131},{131,128},{4... | collective-permute-start | bytes 1544 | tf_op jit(solution)/shard_map/ppermute | solution.py:460
  45.5 11.4 %collective-permute-start.6 = (f32[5,16,256]{2,1,0:T(8,128)S(1)}, f32[5,16,256]{2,1,0:T(8,128)S(1)}, u32[]{:S(2)}, u32[]{:S(2)}) collective-permute-start(f32[5,16,256]{2,1,0:T(8,128)S(1)} %get-tuple-element.36), channel_id=1, source_target_pairs={{0,16},{16,0},{32,48},{48,32},{64,80},{80,64},{96,112},{112,96},{1... | collective-permute-start | bytes 245768 | tf_op jit(solution)/shard_map/ppermute | solution.py:369
  45.6 11.3 %collective-permute-start.7 = (f32[5,16,256]{2,1,0:T(8,128)S(1)}, f32[5,16,256]{2,1,0:T(8,128)S(1)}, u32[]{:S(2)}, u32[]{:S(2)}) collective-permute-start(f32[5,16,256]{2,1,0:T(8,128)S(1)} %get-tuple-element.37), channel_id=1, source_target_pairs={{0,112},{16,32},{32,16},{48,64},{64,48},{80,96},{96,80},{112,0},{1... | collective-permute-start | bytes 245768 | tf_op jit(solution)/shard_map/ppermute | solution.py:368
  47.1 4.0 %collective-permute-start.8 = (f32[5,8,256]{2,1,0:T(8,128)S(1)}, f32[5,8,256]{2,1,0:T(8,128)S(1)}, u32[]{:S(2)}, u32[]{:S(2)}) collective-permute-start(f32[5,8,256]{2,1,0:T(8,128)S(1)} %get-tuple-element.38), channel_id=1, source_target_pairs={{0,1},{1,0},{2,3},{3,2},{4,5},{5,4},{6,7},{7,6},{8,9},{9,8},{10,11... | collective-permute-start | bytes 122888 | tf_op jit(solution)/shard_map/ppermute | solution.py:367
  48.9 7.9 %collective-permute-start.9 = (f32[5,8,256]{2,1,0:T(8,128)S(1)}, f32[5,8,256]{2,1,0:T(8,128)S(1)}, u32[]{:S(2)}, u32[]{:S(2)}) collective-permute-start(f32[5,8,256]{2,1,0:T(8,128)S(1)} %get-tuple-element.39), channel_id=1, source_target_pairs={{0,15},{1,2},{2,1},{3,4},{4,3},{5,6},{6,5},{7,8},{8,7},{9,10},{10,... | collective-permute-start | bytes 122888 | tf_op jit(solution)/shard_map/ppermute | solution.py:366
